TPU v7x, 8 devices: a whole 2x2x1 slice. The times are simulated.
8 devices in a mesh: data: 1 (over z), expert: 8 (over y, x, core).
Axes of the slice: x: 2, y: 2, z: 1, core: 2. Of those that a mesh axis runs over, the one named last changes fastest.
Arguments:
- x_tokens: bfloat16 [512, 1024], P(('data', 'expert'))
- y_mid: bfloat16 [512, 1024], P(('data', 'expert'))
- dy_out: bfloat16 [512, 1024], P(('data', 'expert'))
- experts_one: int32 [512, 8], P(('data', 'expert'))
- gates_one: float32 [512, 8], P(('data', 'expert'))
- slots_one: int32 [512, 8], P(('data', 'expert'))
- experts_two: int32 [512, 8], P(('data', 'expert'))
- gates_two: float32 [512, 8], P(('data', 'expert'))
- slots_two: int32 [512, 8], P(('data', 'expert'))
- w_gate_one: bfloat16 [32, 1024, 512], P('expert')
- w_up_one: bfloat16 [32, 1024, 512], P('expert')
- w_down_one: bfloat16 [32, 512, 1024], P('expert')
- w_gate_two: bfloat16 [32, 1024, 512], P('expert')
- w_up_two: bfloat16 [32, 1024, 512], P('expert')
- w_down_two: bfloat16 [32, 512, 1024], P('expert')
Outputs:
- output 1: bfloat16 [512, 1024], P(('data', 'expert'))
- output 2: float32 [32, 1024, 512], P(('data', 'expert'))
- output 3: float32 [32, 1024, 512], P(('data', 'expert'))
- output 4: float32 [32, 512, 1024], P(('data', 'expert'))
- output 5: float32 [32, 1024, 512], P(('data', 'expert'))
- output 6: float32 [32, 1024, 512], P(('data', 'expert'))
- output 7: float32 [32, 512, 1024], P(('data', 'expert'))
All inputs are finite; a program needn't handle non-finite values.
Results may differ from a plain program's by a relative error of at most 0.0131849.
Values are sent between devices in bfloat16 or wider.
A program may use at most 1 GiB of HBM per device.

v0:
```python
import functools
import jax
import jax.numpy as jnp
from jax import lax
from jax.sharding import PartitionSpec as P


def slot_capacity(tokens_dev, top_k, n_experts):
    return 8 * ((3 * top_k * tokens_dev + 16 * n_experts - 1) // (16 * n_experts))


def route_matrix(experts, slots, gates, n_experts, capacity):
    target = jnp.where(slots >= 0, experts * capacity + slots, -1)
    slot_ids = lax.broadcasted_iota(jnp.int32, (n_experts * capacity, 1), 0)
    matches = [slot_ids == target[None, :, choice] for choice in range(experts.shape[1])]
    send_mat = functools.reduce(jnp.logical_or, matches).astype(jnp.bfloat16)
    gate_terms = [jnp.sum(jnp.where(matches[choice], gates[None, :, choice], 0.0), axis=1) for choice in range(experts.shape[1])]
    return send_mat, functools.reduce(jnp.add, gate_terms)


def expert_grads(x_rows, dz_rows, w_gate, w_up, w_down):
    gate_act = jnp.einsum("erd,edf->erf", x_rows, w_gate, preferred_element_type=jnp.float32).astype(jnp.bfloat16)
    up_act = jnp.einsum("erd,edf->erf", x_rows, w_up, preferred_element_type=jnp.float32).astype(jnp.bfloat16)
    gate_wide = gate_act.astype(jnp.float32)
    up_wide = up_act.astype(jnp.float32)
    sig_gate = jax.nn.sigmoid(gate_wide)
    silu_gate = gate_wide * sig_gate
    hidden = (silu_gate * up_wide).astype(jnp.bfloat16)
    d_hidden = jnp.einsum("erd,efd->erf", dz_rows, w_down, preferred_element_type=jnp.float32)
    dw_down = jnp.einsum("erf,erd->efd", hidden, dz_rows, preferred_element_type=jnp.float32)
    d_gate = (d_hidden * up_wide * sig_gate * (1.0 + gate_wide * (1.0 - sig_gate))).astype(jnp.bfloat16)
    d_up = (d_hidden * silu_gate).astype(jnp.bfloat16)
    dx_rows = (jnp.einsum("erf,edf->erd", d_gate, w_gate, preferred_element_type=jnp.float32) + jnp.einsum("erf,edf->erd", d_up, w_up, preferred_element_type=jnp.float32)).astype(jnp.bfloat16)
    dw_gate = jnp.einsum("erd,erf->edf", x_rows, d_gate, preferred_element_type=jnp.float32)
    dw_up = jnp.einsum("erd,erf->edf", x_rows, d_up, preferred_element_type=jnp.float32)
    return dx_rows, dw_gate, dw_up, dw_down


def layer_backward(inputs, cotangent, experts, gates, slots, w_gate, w_up, w_down, group_size):
    tokens_dev, model_dim = inputs.shape
    n_experts = w_gate.shape[0] * group_size
    capacity = slot_capacity(tokens_dev, experts.shape[1], n_experts)
    send_mat, slot_gate = route_matrix(experts, slots, gates, n_experts, capacity)
    x_send = jnp.dot(send_mat, inputs, preferred_element_type=jnp.float32).astype(jnp.bfloat16)
    dy_send = jnp.dot(send_mat, cotangent, preferred_element_type=jnp.float32)
    z_send = (slot_gate[:, None] * dy_send).astype(jnp.bfloat16)
    x_rows = lax.all_to_all(x_send.reshape(n_experts, capacity, model_dim), "expert", 0, 1, tiled=True)
    dz_rows = lax.all_to_all(z_send.reshape(n_experts, capacity, model_dim), "expert", 0, 1, tiled=True)
    dx_rows, dw_gate, dw_up, dw_down = expert_grads(x_rows, dz_rows, w_gate, w_up, w_down)
    returned = lax.all_to_all(dx_rows, "expert", 1, 0, tiled=True).reshape(n_experts * capacity, model_dim)
    summed = jnp.einsum("rt,rd->td", send_mat, returned, preferred_element_type=jnp.float32)
    return summed, dw_gate, dw_up, dw_down


def solution(mesh):
    group_size = mesh.shape["expert"]
    tok_spec = P(("data", "expert"), None)
    weight_spec = P("expert", None, None)
    grad_spec = P(("data", "expert"), None, None)

    def local_step(x_tokens, y_mid, dy_out, experts_one, gates_one, slots_one, experts_two, gates_two, slots_two, w_gate_one, w_up_one, w_down_one, w_gate_two, w_up_two, w_down_two):
        grads_two = layer_backward(y_mid, dy_out, experts_two, gates_two, slots_two, w_gate_two, w_up_two, w_down_two, group_size)
        dy_mid = (dy_out.astype(jnp.float32) + grads_two[0]).astype(jnp.bfloat16)
        grads_one = layer_backward(x_tokens, dy_mid, experts_one, gates_one, slots_one, w_gate_one, w_up_one, w_down_one, group_size)
        dx_tokens = (dy_mid.astype(jnp.float32) + grads_one[0]).astype(jnp.bfloat16)
        return (dx_tokens,) + grads_one[1:] + grads_two[1:]

    return jax.shard_map(local_step, mesh=mesh, in_specs=(tok_spec,) * 9 + (weight_spec,) * 6, out_specs=(tok_spec,) + (grad_spec,) * 6, check_vma=False)
```

profile of v0, /device:TPU:0, one launch (start us, length us, event | category | flops | bytes accessed | tf_op | source)
XLA Modules:
  0.0 173.9 jit_solution(13411060343350518831)
XLA Ops:
  2.9 2.8 %multiply_convert_fusion.1 = bf16[768,1024]{1,0:T(8,128)(2,1)} fusion(bf16[64,1024]{1,0:T(8,128)(2,1)} %param.17, f32[768]{0:T(1024)S(1)} %add_add_fusion.1, s32[64]{0:T(128)S(1)} %get-tuple-element.24, s32[64]{0:T(128)S(1)} %get-tuple-element.25, s32[64]{0:T(128)S(1)} %get-tuple-element.26, s32[64]{0:T(128)S(1)} %get-tuple-element.27, ...), kind=kOutput, calls=%fused_computation.3 | convolution fusion | flops 102973440 | bytes 1709056 | tf_op jit(solution)/shard_map/dot_general | solution.py:45
  5.7 4.3 %all-to-all-start = ((bf16[32,24,1024]{2,1,0:T(8,128)(2,1)}), bf16[32,24,1024]{2,1,0:T(8,128)(2,1)S(1)}, u32[]{:S(2)}, u32[]{:S(2)}) async-start(bf16[32,24,1024]{2,1,0:T(8,128)(2,1)} %bitcast.16), calls=%async_computation | async-start | bytes 3145728 | tf_op jit(solution)/shard_map/all_to_all | solution.py:48
  10.0 1.9 %convolution_convert_fusion.1 = bf16[768,1024]{1,0:T(8,128)(2,1)} fusion(bf16[64,1024]{1,0:T(8,128)(2,1)S(1)} %copy-done, s32[64]{0:T(128)S(1)} %get-tuple-element.24, s32[64]{0:T(128)S(1)} %get-tuple-element.25, s32[64]{0:T(128)S(1)} %get-tuple-element.26, s32[64]{0:T(128)S(1)} %get-tuple-element.27, s32[64]{0:T(128)S(1)} %get-tuple-element.28, ...), kind=kOutput, calls=%fused_computation.15 | convolution fusion | flops 102187008 | bytes 1705984 | tf_op jit(solution)/shard_map/dot_general | solution.py:44
  11.9 19.1 %all-to-all-done = bf16[32,24,1024]{2,1,0:T(8,128)(2,1)S(1)} async-done(((bf16[32,24,1024]{2,1,0:T(8,128)(2,1)}), bf16[32,24,1024]{2,1,0:T(8,128)(2,1)S(1)}, u32[]{:S(2)}, u32[]{:S(2)}) %all-to-all-start) | async-done | bytes 1572896 | tf_op jit(solution)/shard_map/all_to_all | solution.py:48
  32.1 2.3 %all-to-all-start.1 = ((bf16[32,24,1024]{2,1,0:T(8,128)(2,1)}), bf16[32,24,1024]{2,1,0:T(8,128)(2,1)S(1)}, u32[]{:S(2)}, u32[]{:S(2)}) async-start(bf16[32,24,1024]{2,1,0:T(8,128)(2,1)} %bitcast.138), calls=%async_computation.1 | async-start | bytes 3145728 | tf_op jit(solution)/shard_map/all_to_all | solution.py:47
  34.8 1.9 %convolution_convert_fusion = bf16[768,1024]{1,0:T(8,128)(2,1)} fusion(bf16[64,1024]{1,0:T(8,128)(2,1)S(1)} %copy-done.26, s32[64]{0:T(128)S(1)} %get-tuple-element.8, s32[64]{0:T(128)S(1)} %get-tuple-element.9, s32[64]{0:T(128)S(1)} %get-tuple-element.10, s32[64]{0:T(128)S(1)} %get-tuple-element.11, s32[64]{0:T(128)S(1)} %get-tuple-element.12, ...), kind=kOutput, calls=%fused_computation.14 | convolution fusion | flops 102187008 | bytes 1705984 | tf_op jit(solution)/shard_map/dot_general | solution.py:44
  36.9 18.5 %all-to-all-done.1 = bf16[32,24,1024]{2,1,0:T(8,128)(2,1)S(1)} async-done(((bf16[32,24,1024]{2,1,0:T(8,128)(2,1)}), bf16[32,24,1024]{2,1,0:T(8,128)(2,1)S(1)}, u32[]{:S(2)}, u32[]{:S(2)}) %all-to-all-start.1) | async-done | bytes 1572896 | tf_op jit(solution)/shard_map/all_to_all | solution.py:47
  56.5 3.0 %all-to-all-start.4 = ((bf16[32,24,1024]{2,1,0:T(8,128)(2,1)}), bf16[32,24,1024]{2,1,0:T(8,128)(2,1)}, u32[]{:S(2)}, u32[]{:S(2)}) async-start(bf16[32,24,1024]{2,1,0:T(8,128)(2,1)} %bitcast.139), calls=%async_computation.4 | async-start | bytes 3145728 | tf_op jit(solution)/shard_map/all_to_all | solution.py:47
  61.1 3.3 %convolution_convert_fusion.4 = bf16[4,192,512]{2,1,0:T(8,128)(2,1)S(1)} fusion(bf16[4,192,1024]{2,1,0:T(8,128)(2,1)S(1)} %bitcast.124, bf16[4,1024,512]{2,1,0:T(8,128)(2,1)} %param.27), kind=kOutput, calls=%fused_computation.36 | convolution fusion | flops 805699584 | bytes 6553600 | tf_op jit(solution)/shard_map/erd,edf->erf/dot_general | solution.py:22
  65.6 1.7 copy-done.30
  67.3 1.8 %fusion.2 = (bf16[4,192,512]{2,1,0:T(8,128)(2,1)S(1)}, f32[4,192,512]{2,1,0:T(8,128)S(1)}) fusion(bf16[4,192,512]{2,1,0:T(8,128)(2,1)S(1)} %convolution_convert_fusion.5, bf16[4,192,512]{2,1,0:T(8,128)(2,1)S(1)} %convolution_convert_fusion.4, bf16[4,192,1024]{2,1,0:T(8,128)(2,1)S(1)} %bitcast.132, bf16[4,512,1024]{2,1,0:T(8,128)(2,1)S(1)} %copy-done.30), kind=kOutput, calls=%fused_computation.18 | convolution fusion | flops 810024960 | bytes 9699328 | tf_op jit(solution)/shard_map/erd,efd->erf/dot_general | solution.py:29
  72.6 2.4 %copy.50 = bf16[4,192,1024]{2,0,1:T(4,128)(2,1)} copy(bf16[4,192,1024]{2,1,0:T(8,128)(2,1)S(1)} %add_convert_fusion.1) | data formatting | bytes 3145728 | tf_op jit(solution)/shard_map/convert_element_type | solution.py:33
  75.0 5.5 %all-to-all-done.4 = bf16[32,24,1024]{2,1,0:T(8,128)(2,1)} async-done(((bf16[32,24,1024]{2,1,0:T(8,128)(2,1)}), bf16[32,24,1024]{2,1,0:T(8,128)(2,1)}, u32[]{:S(2)}, u32[]{:S(2)}) %all-to-all-start.4) | async-done | bytes 1572896 | tf_op jit(solution)/shard_map/all_to_all | solution.py:47
  80.4 3.2 %all-to-all-start.2 = ((bf16[4,192,1024]{2,0,1:T(4,128)(2,1)}), bf16[4,192,1024]{2,0,1:T(4,128)(2,1)}, u32[]{:S(2)}, u32[]{:S(2)}) async-start(bf16[4,192,1024]{2,0,1:T(4,128)(2,1)} %copy.50), calls=%async_computation.2 | async-start | bytes 3145728 | tf_op jit(solution)/shard_map/all_to_all | solution.py:50
  85.5 4.1 %convolution_convert_fusion.2 = bf16[4,192,512]{2,1,0:T(8,128)(2,1)} fusion(bf16[4,192,1024]{2,1,0:T(8,128)(2,1)S(1)} %bitcast.128, bf16[4,1024,512]{2,1,0:T(8,128)(2,1)} %param.24), kind=kOutput, calls=%fused_computation.34 | convolution fusion | flops 805699584 | bytes 6553600 | tf_op jit(solution)/shard_map/erd,edf->erf/dot_general | solution.py:22
  89.6 4.8 %fusion.49 = f32[4,1024,512]{2,1,0:T(8,128)} fusion(bf16[4,192,1024]{2,1,0:T(8,128)(2,1)S(1)} %bitcast.126, bf16[4,192,512]{2,1,0:T(8,128)(2,1)S(1)} %copy-done.20), kind=kOutput, calls=%fused_computation.133 | convolution fusion | flops 805306368 | bytes 10747904 | tf_op jit(solution)/shard_map/erd,erf->edf/dot_general | solution.py:34
  94.4 9.9 %all-to-all-done.2 = bf16[4,192,1024]{2,0,1:T(4,128)(2,1)} async-done(((bf16[4,192,1024]{2,0,1:T(4,128)(2,1)}), bf16[4,192,1024]{2,0,1:T(4,128)(2,1)}, u32[]{:S(2)}, u32[]{:S(2)}) %all-to-all-start.2) | async-done | bytes 1572896 | tf_op jit(solution)/shard_map/all_to_all | solution.py:50
  104.3 1.9 %copy.51 = bf16[4,192,1024]{2,1,0:T(8,128)(2,1)S(1)} copy(bf16[4,192,1024]{2,0,1:T(4,128)(2,1)} %all-to-all-done.2) | data formatting | bytes 3145728 | tf_op jit(solution)/shard_map/all_to_all | solution.py:50
  107.6 1.9 %multiply_convert_fusion = bf16[768,1024]{1,0:T(8,128)(2,1)} fusion(bf16[64,1024]{1,0:T(8,128)(2,1)S(1)} %fusion.16, f32[768]{0:T(1024)S(1)} %add_add_fusion, s32[64]{0:T(128)S(1)} %get-tuple-element.8, s32[64]{0:T(128)S(1)} %get-tuple-element.9, s32[64]{0:T(128)S(1)} %get-tuple-element.10, s32[64]{0:T(128)S(1)} %get-tuple-element.11, ...), kind=kOutput, calls=%fused_computation.1 | convolution fusion | flops 102973440 | bytes 1709056 | tf_op jit(solution)/shard_map/dot_general | solution.py:45
  109.5 3.0 %all-to-all-start.3 = ((bf16[32,24,1024]{2,1,0:T(8,128)(2,1)}), bf16[32,24,1024]{2,1,0:T(8,128)(2,1)}, u32[]{:S(2)}, u32[]{:S(2)}) async-start(bf16[32,24,1024]{2,1,0:T(8,128)(2,1)} %bitcast.142), calls=%async_computation.3 | async-start | bytes 3145728 | tf_op jit(solution)/shard_map/all_to_all | solution.py:48
  112.6 4.2 %convolution_convert_fusion.3 = bf16[4,192,512]{2,1,0:T(8,128)(2,1)} fusion(bf16[4,192,1024]{2,1,0:T(8,128)(2,1)S(1)} %bitcast.129, bf16[4,1024,512]{2,1,0:T(8,128)(2,1)} %param.25), kind=kOutput, calls=%fused_computation.35 | convolution fusion | flops 805699584 | bytes 6553600 | tf_op jit(solution)/shard_map/erd,edf->erf/dot_general | solution.py:23
  116.9 4.8 %fusion.20 = f32[4,512,1024]{2,1,0:T(8,128)} fusion(bf16[4,192,1024]{2,1,0:T(8,128)(2,1)S(1)} %bitcast.133, bf16[4,192,512]{2,1,0:T(8,128)(2,1)S(1)} %copy-done.14, bf16[4,192,512]{2,1,0:T(8,128)(2,1)S(1)} %copy-done.5), kind=kOutput, calls=%fused_computation.43 | convolution fusion | flops 808452096 | bytes 11534336 | tf_op jit(solution)/shard_map/erf,erd->efd/dot_general | solution.py:30
  121.6 4.8 %fusion.44 = f32[4,1024,512]{2,1,0:T(8,128)} fusion(bf16[4,192,1024]{2,1,0:T(8,128)(2,1)S(1)} %bitcast.127, f32[4,192,512]{2,1,0:T(8,128)S(1)} %copy-done.23, bf16[4,192,512]{2,1,0:T(8,128)(2,1)S(1)} %copy-done.5), kind=kOutput, calls=%fused_computation.128 | convolution fusion | flops 808058880 | bytes 12320768 | tf_op jit(solution)/shard_map/erd,erf->edf/dot_general | solution.py:35
  126.4 7.1 %all-to-all-done.3 = bf16[32,24,1024]{2,1,0:T(8,128)(2,1)} async-done(((bf16[32,24,1024]{2,1,0:T(8,128)(2,1)}), bf16[32,24,1024]{2,1,0:T(8,128)(2,1)}, u32[]{:S(2)}, u32[]{:S(2)}) %all-to-all-start.3) | async-done | bytes 1572896 | tf_op jit(solution)/shard_map/all_to_all | solution.py:48
  135.3 4.4 %fusion.6 = (bf16[4,192,512]{2,1,0:T(8,128)(2,1)S(1)}, f32[4,192,512]{2,1,0:T(8,128)S(1)}) fusion(bf16[4,192,512]{2,1,0:T(8,128)(2,1)S(1)} %copy-done.15, bf16[4,192,512]{2,1,0:T(8,128)(2,1)S(1)} %copy-done.6, bf16[4,192,1024]{2,1,0:T(8,128)(2,1)S(1)} %bitcast.134, bf16[4,512,1024]{2,1,0:T(8,128)(2,1)} %param.26), kind=kOutput, calls=%fused_computation.22 | convolution fusion | flops 810024960 | bytes 9699328 | tf_op jit(solution)/shard_map/erd,efd->erf/dot_general | solution.py:29
  144.4 2.4 %copy.55 = bf16[4,192,1024]{2,0,1:T(4,128)(2,1)} copy(bf16[4,192,1024]{2,1,0:T(8,128)(2,1)S(1)} %add_convert_fusion) | data formatting | bytes 3145728 | tf_op jit(solution)/shard_map/convert_element_type | solution.py:33
  146.8 3.2 %all-to-all-start.5 = ((bf16[4,192,1024]{2,0,1:T(4,128)(2,1)}), bf16[4,192,1024]{2,0,1:T(4,128)(2,1)}, u32[]{:S(2)}, u32[]{:S(2)}) async-start(bf16[4,192,1024]{2,0,1:T(4,128)(2,1)} %copy.55), calls=%async_computation.5 | async-start | bytes 3145728 | tf_op jit(solution)/shard_map/all_to_all | solution.py:50
  150.0 6.0 %fusion.48 = f32[4,1024,512]{2,1,0:T(8,128)} fusion(bf16[4,192,1024]{2,1,0:T(8,128)(2,1)S(1)} %bitcast.130, bf16[4,192,512]{2,1,0:T(8,128)(2,1)} %copy-done.21), kind=kOutput, calls=%fused_computation.132 | convolution fusion | flops 805306368 | bytes 10747904 | tf_op jit(solution)/shard_map/erd,erf->edf/dot_general | solution.py:34
  156.1 4.7 %fusion.18 = f32[4,512,1024]{2,1,0:T(8,128)} fusion(bf16[4,192,1024]{2,1,0:T(8,128)(2,1)S(1)} %bitcast.135, bf16[4,192,512]{2,1,0:T(8,128)(2,1)S(1)} %copy-done.15, bf16[4,192,512]{2,1,0:T(8,128)(2,1)S(1)} %copy-done.6), kind=kOutput, calls=%fused_computation.42 | convolution fusion | flops 808452096 | bytes 11534336 | tf_op jit(solution)/shard_map/erf,erd->efd/dot_general | solution.py:30
  160.8 4.8 %fusion.45 = f32[4,1024,512]{2,1,0:T(8,128)} fusion(bf16[4,192,1024]{2,1,0:T(8,128)(2,1)S(1)} %bitcast.131, f32[4,192,512]{2,1,0:T(8,128)S(1)} %copy-done.25, bf16[4,192,512]{2,1,0:T(8,128)(2,1)S(1)} %copy-done.6), kind=kOutput, calls=%fused_computation.129 | convolution fusion | flops 808058880 | bytes 12320768 | tf_op jit(solution)/shard_map/erd,erf->edf/dot_general | solution.py:35
  165.6 5.1 %all-to-all-done.5 = bf16[4,192,1024]{2,0,1:T(4,128)(2,1)} async-done(((bf16[4,192,1024]{2,0,1:T(4,128)(2,1)}), bf16[4,192,1024]{2,0,1:T(4,128)(2,1)}, u32[]{:S(2)}, u32[]{:S(2)}) %all-to-all-start.5) | async-done | bytes 1572896 | tf_op jit(solution)/shard_map/all_to_all | solution.py:50
  170.7 1.9 %copy.56 = bf16[4,192,1024]{2,1,0:T(8,128)(2,1)S(1)} copy(bf16[4,192,1024]{2,0,1:T(4,128)(2,1)} %all-to-all-done.5) | data formatting | bytes 3145728 | tf_op jit(solution)/shard_map/all_to_all | solution.py:50
  (92 shorter events, 22.0 us)
Async XLA Ops:
  0.6 9.4 %copy-start = (bf16[64,1024]{1,0:T(8,128)(2,1)S(1)}, bf16[64,1024]{1,0:T(8,128)(2,1)}, u32[]{:S(2)}) copy-start(bf16[64,1024]{1,0:T(8,128)(2,1)} %param.16) | copy-start | bytes 393220
  5.7 25.3 %all-to-all-start = ((bf16[32,24,1024]{2,1,0:T(8,128)(2,1)}), bf16[32,24,1024]{2,1,0:T(8,128)(2,1)S(1)}, u32[]{:S(2)}, u32[]{:S(2)}) async-start(bf16[32,24,1024]{2,1,0:T(8,128)(2,1)} %bitcast.16), calls=%async_computation | async-start | bytes 3145728 | tf_op jit(solution)/shard_map/all_to_all | solution.py:48
  31.0 3.5 %copy-start.27 = (s32[64,8]{0,1:T(8,128)S(1)}, s32[64,8]{0,1:T(8,128)}, u32[]{:S(2)}) copy-start(s32[64,8]{0,1:T(8,128)} %param.20) | copy-start | bytes 6148
  31.0 3.5 %copy-start.28 = (s32[64,8]{0,1:T(8,128)S(1)}, s32[64,8]{0,1:T(8,128)}, u32[]{:S(2)}) copy-start(s32[64,8]{0,1:T(8,128)} %param.18) | copy-start | bytes 6148
  31.0 3.5 %copy-start.29 = (f32[64,8]{0,1:T(8,128)S(1)}, f32[64,8]{0,1:T(8,128)}, u32[]{:S(2)}) copy-start(f32[64,8]{0,1:T(8,128)} %param.19) | copy-start | bytes 6148
  31.0 3.8 %copy-start.26 = (bf16[64,1024]{1,0:T(8,128)(2,1)S(1)}, bf16[64,1024]{1,0:T(8,128)(2,1)}, u32[]{:S(2)}) copy-start(bf16[64,1024]{1,0:T(8,128)(2,1)} %param.15) | copy-start | bytes 393220
  32.1 23.2 %all-to-all-start.1 = ((bf16[32,24,1024]{2,1,0:T(8,128)(2,1)}), bf16[32,24,1024]{2,1,0:T(8,128)(2,1)S(1)}, u32[]{:S(2)}, u32[]{:S(2)}) async-start(bf16[32,24,1024]{2,1,0:T(8,128)(2,1)} %bitcast.138), calls=%async_computation.1 | async-start | bytes 3145728 | tf_op jit(solution)/shard_map/all_to_all | solution.py:47
  34.5 2.2 %copy-start.18 = (bf16[32,24,1024]{2,1,0:T(8,128)(2,1)S(1)}, bf16[32,24,1024]{2,1,0:T(8,128)(2,1)}, u32[]{:S(2)}) copy-start(bf16[32,24,1024]{2,1,0:T(8,128)(2,1)} %copy-done.17) | copy-start | bytes 4718596
  36.9 28.8 %copy-start.7 = (bf16[8,4,24,1024]{3,2,0,1:T(8,128)(2,1)}, bf16[8,4,24,1024]{3,2,0,1:T(8,128)(2,1)S(1)}, u32[]{:S(2)}) copy-start(bf16[8,4,24,1024]{3,2,0,1:T(8,128)(2,1)S(1)} %copy.48) | copy-start | bytes 4718596
  56.5 23.9 %all-to-all-start.4 = ((bf16[32,24,1024]{2,1,0:T(8,128)(2,1)}), bf16[32,24,1024]{2,1,0:T(8,128)(2,1)}, u32[]{:S(2)}, u32[]{:S(2)}) async-start(bf16[32,24,1024]{2,1,0:T(8,128)(2,1)} %bitcast.139), calls=%async_computation.4 | async-start | bytes 3145728 | tf_op jit(solution)/shard_map/all_to_all | solution.py:47
  61.1 3.5 %copy-start.11 = (bf16[4,1024,512]{2,1,0:T(8,128)(2,1)S(1)}, bf16[4,1024,512]{2,1,0:T(8,128)(2,1)}, u32[]{:S(2)}) copy-start(bf16[4,1024,512]{2,1,0:T(8,128)(2,1)} %param.28) | copy-start | bytes 12582916
  64.6 6.5 %copy-start.4 = (bf16[4,192,512]{2,1,0:T(8,128)(2,1)}, bf16[4,192,512]{2,1,0:T(8,128)(2,1)S(1)}, u32[]{:S(2)}) copy-start(bf16[4,192,512]{2,1,0:T(8,128)(2,1)S(1)} %convolution_convert_fusion.4) | copy-start | bytes 2359300
  64.6 2.8 %copy-start.30 = (bf16[4,512,1024]{2,1,0:T(8,128)(2,1)S(1)}, bf16[4,512,1024]{2,1,0:T(8,128)(2,1)}, u32[]{:S(2)}) copy-start(bf16[4,512,1024]{2,1,0:T(8,128)(2,1)} %param.29) | copy-start | bytes 12582916
  65.6 3.5 %copy-start.13 = (bf16[4,192,512]{2,1,0:T(8,128)(2,1)}, bf16[4,192,512]{2,1,0:T(8,128)(2,1)S(1)}, u32[]{:S(2)}) copy-start(bf16[4,192,512]{2,1,0:T(8,128)(2,1)S(1)} %convolution_convert_fusion.5) | copy-start | bytes 2359300
  67.3 2.2 %copy-start.2 = (bf16[4,1024,512]{2,1,0:T(8,128)(2,1)S(1)}, bf16[4,1024,512]{2,1,0:T(8,128)(2,1)}, u32[]{:S(2)}) copy-start(bf16[4,1024,512]{2,1,0:T(8,128)(2,1)} %param.27) | copy-start | bytes 12582916
  69.1 1.9 %copy-start.19 = (bf16[4,192,512]{2,1,0:T(8,128)(2,1)}, bf16[4,192,512]{2,1,0:T(8,128)(2,1)S(1)}, u32[]{:S(2)}) copy-start(bf16[4,192,512]{2,1,0:T(8,128)(2,1)S(1)} %get-tuple-element.39) | copy-start | bytes 2359300
  69.2 1.9 %copy-start.22 = (f32[4,192,512]{2,1,0:T(8,128)}, f32[4,192,512]{2,1,0:T(8,128)S(1)}, u32[]{:S(2)}) copy-start(f32[4,192,512]{2,1,0:T(8,128)S(1)} %get-tuple-element.40) | copy-start | bytes 4718596
  80.4 23.9 %all-to-all-start.2 = ((bf16[4,192,1024]{2,0,1:T(4,128)(2,1)}), bf16[4,192,1024]{2,0,1:T(4,128)(2,1)}, u32[]{:S(2)}, u32[]{:S(2)}) async-start(bf16[4,192,1024]{2,0,1:T(4,128)(2,1)} %copy.50), calls=%async_computation.2 | async-start | bytes 3145728 | tf_op jit(solution)/shard_map/all_to_all | solution.py:50
  85.5 4.1 %copy-start.20 = (bf16[4,192,512]{2,1,0:T(8,128)(2,1)S(1)}, bf16[4,192,512]{2,1,0:T(8,128)(2,1)}, u32[]{:S(2)}) copy-start(bf16[4,192,512]{2,1,0:T(8,128)(2,1)} %copy-done.19) | copy-start | bytes 2359300
  109.5 23.9 %all-to-all-start.3 = ((bf16[32,24,1024]{2,1,0:T(8,128)(2,1)}), bf16[32,24,1024]{2,1,0:T(8,128)(2,1)}, u32[]{:S(2)}, u32[]{:S(2)}) async-start(bf16[32,24,1024]{2,1,0:T(8,128)(2,1)} %bitcast.142), calls=%async_computation.3 | async-start | bytes 3145728 | tf_op jit(solution)/shard_map/all_to_all | solution.py:48
  112.6 4.3 %copy-start.5 = (bf16[4,192,512]{2,1,0:T(8,128)(2,1)S(1)}, bf16[4,192,512]{2,1,0:T(8,128)(2,1)}, u32[]{:S(2)}) copy-start(bf16[4,192,512]{2,1,0:T(8,128)(2,1)} %copy-done.4) | copy-start | bytes 2359300
  112.6 4.2 %copy-start.8 = (bf16[8,4,24,1024]{3,2,0,1:T(8,128)(2,1)S(1)}, bf16[8,4,24,1024]{3,2,0,1:T(8,128)(2,1)}, u32[]{:S(2)}) copy-start(bf16[8,4,24,1024]{3,2,0,1:T(8,128)(2,1)} %copy-done.7) | copy-start | bytes 4718596
  112.6 4.2 %copy-start.14 = (bf16[4,192,512]{2,1,0:T(8,128)(2,1)S(1)}, bf16[4,192,512]{2,1,0:T(8,128)(2,1)}, u32[]{:S(2)}) copy-start(bf16[4,192,512]{2,1,0:T(8,128)(2,1)} %copy-done.13) | copy-start | bytes 2359300
  116.8 4.8 %copy-start.23 = (f32[4,192,512]{2,1,0:T(8,128)S(1)}, f32[4,192,512]{2,1,0:T(8,128)}, u32[]{:S(2)}) copy-start(f32[4,192,512]{2,1,0:T(8,128)} %copy-done.22) | copy-start | bytes 4718596
  133.5 1.7 copy-start.6
  133.5 1.8 %copy-start.15 = (bf16[4,192,512]{2,1,0:T(8,128)(2,1)S(1)}, bf16[4,192,512]{2,1,0:T(8,128)(2,1)}, u32[]{:S(2)}) copy-start(bf16[4,192,512]{2,1,0:T(8,128)(2,1)} %convolution_convert_fusion.3) | copy-start | bytes 2359300
  135.1 4.6 %copy-start.9 = (bf16[8,4,24,1024]{3,2,0,1:T(8,128)(2,1)}, bf16[8,4,24,1024]{3,2,0,1:T(8,128)(2,1)S(1)}, u32[]{:S(2)}) copy-start(bf16[8,4,24,1024]{3,2,0,1:T(8,128)(2,1)S(1)} %copy.53) | copy-start | bytes 4718596
  135.3 4.5 %copy-start.3 = (bf16[4,1024,512]{2,1,0:T(8,128)(2,1)S(1)}, bf16[4,1024,512]{2,1,0:T(8,128)(2,1)}, u32[]{:S(2)}) copy-start(bf16[4,1024,512]{2,1,0:T(8,128)(2,1)} %param.24) | copy-start | bytes 12582916
  139.8 3.0 %copy-start.12 = (bf16[4,1024,512]{2,1,0:T(8,128)(2,1)S(1)}, bf16[4,1024,512]{2,1,0:T(8,128)(2,1)}, u32[]{:S(2)}) copy-start(bf16[4,1024,512]{2,1,0:T(8,128)(2,1)} %param.25) | copy-start | bytes 12582916
  146.8 23.9 %all-to-all-start.5 = ((bf16[4,192,1024]{2,0,1:T(4,128)(2,1)}), bf16[4,192,1024]{2,0,1:T(4,128)(2,1)}, u32[]{:S(2)}, u32[]{:S(2)}) async-start(bf16[4,192,1024]{2,0,1:T(4,128)(2,1)} %copy.55), calls=%async_computation.5 | async-start | bytes 3145728 | tf_op jit(solution)/shard_map/all_to_all | solution.py:50
  150.0 6.0 %copy-start.10 = (bf16[8,4,24,1024]{3,2,0,1:T(8,128)(2,1)S(1)}, bf16[8,4,24,1024]{3,2,0,1:T(8,128)(2,1)}, u32[]{:S(2)}) copy-start(bf16[8,4,24,1024]{3,2,0,1:T(8,128)(2,1)} %copy-done.9) | copy-start | bytes 4718596
  156.1 4.7 %copy-start.25 = (f32[4,192,512]{2,1,0:T(8,128)S(1)}, f32[4,192,512]{2,1,0:T(8,128)}, u32[]{:S(2)}) copy-start(f32[4,192,512]{2,1,0:T(8,128)} %copy-done.24) | copy-start | bytes 4718596
  (6 other events, 7.6 us)
where the time goes:
time: 175 us; the launch traced here: 174 us
  waiting for transfers between devices  65.2 us (37%)
  matrix products  65.1 us (37%)
  local copies, waits for them, and re-layouts  21.6 us (12%)
  starting transfers between devices  19.1 us (11%)
    all_to_all x2, waiting for transfers between devices, layer_backward(): lax.all_to_all(z_send.reshape(n_experts, capacity, model_dim), 'expert',...  26.2 us
    all_to_all x2, waiting for transfers between devices, layer_backward(): lax.all_to_all(x_send.reshape(n_experts, capacity, model_dim), 'expert',...  24 us
    all_to_all x2, waiting for transfers between devices, layer_backward(): lax.all_to_all(dx_rows, 'expert', 1, 0, tiled=True)  15.1 us
    dot_general x2, matrix products, expert_grads(): jnp.einsum('erd,erf->edf', x_rows, d_gate, preferred_element_type=jnp.flo...  10.8 us
    dot_general x2, matrix products, expert_grads(): jnp.einsum('erd,erf->edf', x_rows, d_up, preferred_element_type=jnp.float32)  9.54 us
    dot_general x2, matrix products, expert_grads(): jnp.einsum('erf,erd->efd', hidden, dz_rows, preferred_element_type=jnp.fl...  9.49 us
    dot_general x2, matrix products, expert_grads(): jnp.einsum('erd,edf->erf', x_rows, w_gate, preferred_element_type=jnp.flo...  7.46 us
    all_to_all x2, starting transfers between devices, layer_backward(): lax.all_to_all(z_send.reshape(n_experts, capacity, model_dim), 'expert',...  7.34 us
  transfers between devices with their start and end apart: 6, of which 6 were waited for; matrix products, arithmetic and copies ran while one was open for 33% of the time, Pallas kernels for 0%

commit v1 on v0

v1 whole, which is shorter than its diff:
```python
import functools
import jax
import jax.numpy as jnp
from jax import lax
from jax.experimental import pallas as pl
from jax.experimental.pallas import tpu as pltpu
from jax.sharding import PartitionSpec as P

MESH = pl.DeviceIdType.MESH
F32 = jnp.float32
BF16 = jnp.bfloat16

TOK = 64
CHIPS = 4
DEVS = 8
D = 1024
F = 512
E = 4
CAP = 24
PAIR = 2 * CAP
ROWS = CHIPS * PAIR
PROWS = E * PAIR
CH = 4
CW = D // CH
VMEM_LIMIT = 66_000_000

S_ROUTE, S_Y, S_DY, S_X, S_D1 = 0, 1, 2, 3, 4
N_STREAMS = S_D1 + CH


def nt_dot(a, b):
    return lax.dot_general(a, b, (((1,), (1,)), ((), ())), preferred_element_type=F32)


def tn_dot(a, b):
    return lax.dot_general(a, b, (((0,), (0,)), ((), ())), preferred_element_type=F32)


def nn_dot(a, b):
    return jnp.dot(a, b, preferred_element_type=F32)


def main_kernel(
    route_ref, x_ref, y_ref, dy_ref, w1b_hbm, w3b_hbm, w2b_hbm, w1a_hbm, w3a_hbm, w2a_hbm,
    dx_ref, xrb_hbm, zrb_hbm, hb_hbm, dab_hbm, dbb_hbm, xra_hbm, zra_hbm, ha_hbm, daa_hbm, dba_hbm,
    w_vm, route_g, y_g, dy_g, x_g, d1_g, d1_own,
    xr, zr, act_s, act_f, hid, da, db, dxp, perm, perm_t, gate,
    part, mate_recv, far_recv,
    w_sem, ag_send, ag_recv, rs_send, rs_recv, out_sem,
):
    me = lax.axis_index("expert")
    core = lax.rem(me, 2)
    xpos = lax.rem(me // 2, 2)
    ypos = me // 4
    chip = me // 2
    mate = me + 1 - 2 * core
    nx = me + 2 - 4 * xpos
    ny = me + 4 - 8 * ypos
    nd = ny + 2 - 4 * xpos
    far = (nx, ny, nd)

    def remote(src, dst, send, recv, dev):
        return pltpu.make_async_remote_copy(src_ref=src, dst_ref=dst, send_sem=send, recv_sem=recv, device_id={"expert": dev}, device_id_type=MESH)

    w_hbm = (w1b_hbm, w3b_hbm, w2b_hbm, w1a_hbm, w3a_hbm, w2a_hbm)

    def w_copy(i):
        return pltpu.make_async_copy(w_hbm[i], w_vm[i], w_sem.at[i])

    for i in range(3):
        w_copy(i).start()

    barrier = pltpu.get_barrier_semaphore()
    for dev in (mate,) + far:
        pl.semaphore_signal(barrier, inc=1, device_id={"expert": dev}, device_id_type=MESH)
    pl.semaphore_wait(barrier, 4)

    sends = []

    def ag_start(stream, src, buf):
        for k, dev in enumerate(far + (mate,)):
            c = remote(src, buf.at[me], ag_send.at[stream, k], ag_recv.at[stream, k], dev)
            c.start()
            sends.append(c)

    def ag_pass_on(stream, buf):
        for k, dev in enumerate(far):
            remote(buf.at[dev], buf.at[dev], ag_send.at[stream, k], ag_recv.at[stream, k], dev).wait_recv()
            c = remote(buf.at[dev], buf.at[dev], ag_send.at[stream, 4 + k], ag_recv.at[stream, 4 + k], mate)
            c.start()
            sends.append(c)

    def ag_finish(stream, buf):
        remote(buf.at[mate], buf.at[mate], ag_send.at[stream, 3], ag_recv.at[stream, 3], mate).wait_recv()
        for k, dev in enumerate(far):
            dev_mate = dev + 1 - 2 * core
            remote(buf.at[dev_mate], buf.at[dev_mate], ag_send.at[stream, 4 + k], ag_recv.at[stream, 4 + k], mate).wait_recv()

    ag_start(S_ROUTE, route_ref, route_g)
    ag_start(S_Y, y_ref, y_g)
    ag_start(S_DY, dy_ref, dy_g)
    ag_start(S_X, x_ref, x_g)
    for i in range(3, 6):
        w_copy(i).start()
    route_g[me] = route_ref[...]
    y_g[me] = y_ref[...]
    dy_g[me] = dy_ref[...]
    x_g[me] = x_ref[...]

    outs = []

    def out_start(src, dst):
        c = pltpu.make_async_copy(src, dst, out_sem.at[len(outs)])
        c.start()
        outs.append(c)

    def build_routes(layer):
        base = (me * PROWS).astype(F32)
        row_id = lax.broadcasted_iota(jnp.int32, (PROWS, 2 * TOK), 0).astype(F32)
        for p in range(CHIPS):
            target = jnp.maximum(route_g[2 * p, layer, 0:8, :], route_g[2 * p + 1, layer, 0:8, :]) - base
            gates = route_g[2 * p, layer, 8:16, :] + route_g[2 * p + 1, layer, 8:16, :]
            hit = jnp.zeros((PROWS, 2 * TOK), F32)
            gsum = jnp.zeros((PROWS, 2 * TOK), F32)
            for j in range(8):
                m = row_id == target[j : j + 1, :]
                hit = jnp.where(m, 1.0, hit)
                gsum = jnp.where(m, gates[j : j + 1, :], gsum)
            perm[p] = hit.astype(BF16)
            perm_t[p] = hit.T.astype(BF16)
            gate[p] = jnp.sum(gsum, axis=1, keepdims=True)

    def gather_rows(tokens, dst, layer, cols, gated):
        for p in range(CHIPS):
            got = nn_dot(perm[p], tokens(p))
            if gated:
                got = got * gate[p]
            got = got.astype(BF16)
            for e in range(E):
                dst[layer, e, p * PAIR : (p + 1) * PAIR, cols] = got[e * PAIR : (e + 1) * PAIR]

    def forward_expert(layer, e):
        w1, w3 = w_vm[3 * layer], w_vm[3 * layer + 1]
        rows = xr[layer, e]
        a = nn_dot(rows, w1[e]).astype(BF16).astype(F32)
        b = nn_dot(rows, w3[e]).astype(BF16).astype(F32)
        sig = jax.nn.sigmoid(a)
        s = a * sig
        act_s[e] = s
        act_f[e] = b * (sig * (1.0 + a * (1.0 - sig)))
        hid[layer, e] = (s * b).astype(BF16)

    def hidden_grads(layer):
        w2 = w_vm[3 * layer + 2]

        @pl.loop(0, E)
        def _(e):
            dh = nt_dot(zr[layer, e], w2[e])
            da[layer, e] = (dh * act_f[e]).astype(BF16)
            db[layer, e] = (dh * act_s[e]).astype(BF16)

    def row_chunk(layer, k):
        w1, w3 = w_vm[3 * layer], w_vm[3 * layer + 1]
        cols = slice(k * CW, (k + 1) * CW)

        @pl.loop(0, E)
        def _(e):
            g = nt_dot(da[layer, e], w1[e, cols, :]) + nt_dot(db[layer, e], w3[e, cols, :])
            g = g.astype(BF16)
            for p in range(CHIPS):
                dxp[k % 2, p, e] = g[p * PAIR : (p + 1) * PAIR]

        for p in range(CHIPS):
            r = nn_dot(perm_t[p], dxp[k % 2, p].reshape(PROWS, CW))
            part[layer, k, 0, p] = r[:TOK]
            part[layer, k, 1, p] = r[TOK:]
        c = mate_copy(layer, k)
        c.start()
        sends.append(c)

    def mate_copy(layer, k):
        return remote(part.at[layer, k, 1 - core], mate_recv.at[layer, k], rs_send.at[layer, k, 3], rs_recv.at[layer, k, 3], mate)

    def far_copy(layer, k, i):
        dev = far[i]
        return remote(part.at[layer, k, core, dev // 2], far_recv.at[layer, k, i], rs_send.at[layer, k, i], rs_recv.at[layer, k, i], dev)

    def mate_sum(layer, k):
        mate_copy(layer, k).wait_recv()
        for p in range(CHIPS):
            part[layer, k, core, p] = part[layer, k, core, p] + mate_recv[layer, k, p]
        for i in range(3):
            c = far_copy(layer, k, i)
            c.start()
            sends.append(c)

    def far_sum(layer, k):
        for i in range(3):
            far_copy(layer, k, i).wait_recv()
        return part[layer, k, core, chip] + (far_recv[layer, k, 0] + far_recv[layer, k, 1] + far_recv[layer, k, 2])

    def pair_of(buf, p):
        return buf[2 * p : 2 * p + 2].reshape(2 * TOK, buf.shape[-1])

    ag_pass_on(S_ROUTE, route_g)
    ag_finish(S_ROUTE, route_g)
    build_routes(0)
    ag_pass_on(S_Y, y_g)
    ag_finish(S_Y, y_g)
    gather_rows(lambda p: pair_of(y_g, p), xr, 0, slice(None), False)
    out_start(xr.at[0], xrb_hbm)
    w_copy(0).wait()
    w_copy(1).wait()

    @pl.loop(0, E)
    def _(e):
        forward_expert(0, e)

    out_start(hid.at[0], hb_hbm)
    ag_pass_on(S_DY, dy_g)
    ag_finish(S_DY, dy_g)
    gather_rows(lambda p: pair_of(dy_g, p), zr, 0, slice(None), True)
    out_start(zr.at[0], zrb_hbm)
    w_copy(2).wait()
    hidden_grads(0)
    out_start(da.at[0], dab_hbm)
    out_start(db.at[0], dbb_hbm)
    for k in range(CH):
        row_chunk(0, k)
        if k >= 1:
            mate_sum(0, k - 1)
    mate_sum(0, CH - 1)

    ag_pass_on(S_X, x_g)
    build_routes(1)
    ag_finish(S_X, x_g)
    gather_rows(lambda p: pair_of(x_g, p), xr, 1, slice(None), False)
    out_start(xr.at[1], xra_hbm)
    for i in range(3, 6):
        w_copy(i).wait()

    def mid_grad(k):
        cols = slice(k * CW, (k + 1) * CW)
        mine = (dy_ref[:, cols].astype(F32) + far_sum(0, k)).astype(BF16)
        d1_own[k] = mine
        d1_g[k, me] = mine
        ag_start(S_D1 + k, d1_own.at[k], d1_g.at[k])

    for k in range(CH):
        forward_expert(1, k)
        mid_grad(k)
    out_start(hid.at[1], ha_hbm)
    for k in range(CH):
        ag_pass_on(S_D1 + k, d1_g.at[k])
    for k in range(CH):
        ag_finish(S_D1 + k, d1_g.at[k])
        gather_rows(lambda p: d1_g[k, 2 * p : 2 * p + 2].reshape(2 * TOK, CW), zr, 1, slice(k * CW, (k + 1) * CW), True)
    out_start(zr.at[1], zra_hbm)
    hidden_grads(1)
    out_start(da.at[1], daa_hbm)
    out_start(db.at[1], dba_hbm)
    for k in range(CH):
        row_chunk(1, k)
        if k >= 1:
            mate_sum(1, k - 1)
    mate_sum(1, CH - 1)
    for k in range(CH):
        dx_ref[:, k * CW : (k + 1) * CW] = (d1_own[k].astype(F32) + far_sum(1, k)).astype(BF16)
    for c in sends:
        c.wait_send()
    for c in outs:
        c.wait()


def main_call(route, x, y, dy, weights_two, weights_one):
    vm = pl.BlockSpec(memory_space=pltpu.VMEM)
    hbm = pl.BlockSpec(memory_space=pl.ANY)
    rows_d = jax.ShapeDtypeStruct((E, ROWS, D), BF16)
    rows_f = jax.ShapeDtypeStruct((E, ROWS, F), BF16)
    saved = (rows_d, rows_d, rows_f, rows_f, rows_f)
    w_up = pltpu.VMEM((E, D, F), BF16)
    w_dn = pltpu.VMEM((E, F, D), BF16)
    dma = pltpu.SemaphoreType.DMA
    return pl.pallas_call(
        main_kernel,
        out_shape=(jax.ShapeDtypeStruct((TOK, D), BF16),) + saved + saved,
        in_specs=[vm] * 4 + [hbm] * 6,
        out_specs=(vm,) + (hbm,) * 10,
        scratch_shapes=[
            (w_up, w_up, w_dn, w_up, w_up, w_dn),
            pltpu.VMEM((DEVS, 2, 16, 2 * TOK), F32),
            pltpu.VMEM((DEVS, TOK, D), BF16),
            pltpu.VMEM((DEVS, TOK, D), BF16),
            pltpu.VMEM((DEVS, TOK, D), BF16),
            pltpu.VMEM((CH, DEVS, TOK, CW), BF16),
            pltpu.VMEM((CH, TOK, CW), BF16),
            pltpu.VMEM((2, E, ROWS, D), BF16),
            pltpu.VMEM((2, E, ROWS, D), BF16),
            pltpu.VMEM((E, ROWS, F), F32),
            pltpu.VMEM((E, ROWS, F), F32),
            pltpu.VMEM((2, E, ROWS, F), BF16),
            pltpu.VMEM((2, E, ROWS, F), BF16),
            pltpu.VMEM((2, E, ROWS, F), BF16),
            pltpu.VMEM((2, CHIPS, E, PAIR, CW), BF16),
            pltpu.VMEM((CHIPS, PROWS, 2 * TOK), BF16),
            pltpu.VMEM((CHIPS, 2 * TOK, PROWS), BF16),
            pltpu.VMEM((CHIPS, PROWS, 1), F32),
            pltpu.VMEM((2, CH, 2, CHIPS, TOK, CW), F32),
            pltpu.VMEM((2, CH, CHIPS, TOK, CW), F32),
            pltpu.VMEM((2, CH, 3, TOK, CW), F32),
            dma((6,)),
            dma((N_STREAMS, 7)),
            dma((N_STREAMS, 7)),
            dma((2, CH, 4)),
            dma((2, CH, 4)),
            dma((10,)),
        ],
        compiler_params=pltpu.CompilerParams(collective_id=0, has_side_effects=True, vmem_limit_bytes=VMEM_LIMIT),
        name="moe_backward",
    )(route, x, y, dy, *weights_two, *weights_one)


def wgrad_kernel(x_ref, z_ref, h_ref, da_ref, db_ref, dw1_ref, dw3_ref, dw2_ref):
    x = x_ref[0]
    dw1_ref[0] = tn_dot(x, da_ref[0])
    dw3_ref[0] = tn_dot(x, db_ref[0])
    dw2_ref[0] = tn_dot(h_ref[0], z_ref[0])


def wgrad_call(xr, zr, hid, da, db, name):
    split = 2
    whole_d = pl.BlockSpec((1, ROWS, D), lambda e, j: (e, 0, 0))
    whole_f = pl.BlockSpec((1, ROWS, F), lambda e, j: (e, 0, 0))
    part_d = pl.BlockSpec((1, ROWS, D // split), lambda e, j: (e, 0, j))
    part_f = pl.BlockSpec((1, ROWS, F // split), lambda e, j: (e, 0, j))
    up = pl.BlockSpec((1, D // split, F), lambda e, j: (e, j, 0))
    dn = pl.BlockSpec((1, F // split, D), lambda e, j: (e, j, 0))
    return pl.pallas_call(
        wgrad_kernel,
        grid=(E, split),
        out_shape=(jax.ShapeDtypeStruct((E, D, F), F32), jax.ShapeDtypeStruct((E, D, F), F32), jax.ShapeDtypeStruct((E, F, D), F32)),
        in_specs=[part_d, whole_d, part_f, whole_f, whole_f],
        out_specs=(up, up, dn),
        compiler_params=pltpu.CompilerParams(vmem_limit_bytes=40_000_000),
        cost_estimate=pl.CostEstimate(flops=6 * E * ROWS * D * F, bytes_accessed=12 * E * D * F, transcendentals=0),
        name=name,
    )(xr, zr, hid, da, db)


def route_of(experts, gates, slots, core):
    code = jnp.where(slots >= 0, experts * PAIR + core * CAP + slots, -1).astype(F32).T
    gate = gates.T
    lane_core = lax.broadcasted_iota(jnp.int32, (8, 2 * TOK), 1) // TOK
    mine = lane_core == core
    code = jnp.where(mine, jnp.concatenate([code, code], axis=1), -1.0)
    gate = jnp.where(mine, jnp.concatenate([gate, gate], axis=1), 0.0)
    return jnp.concatenate([code, gate], axis=0)


def solution(mesh):
    tok_spec = P(("data", "expert"), None)
    weight_spec = P("expert", None, None)
    grad_spec = P(("data", "expert"), None, None)

    def local_step(x_tokens, y_mid, dy_out, experts_one, gates_one, slots_one, experts_two, gates_two, slots_two, w_gate_one, w_up_one, w_down_one, w_gate_two, w_up_two, w_down_two):
        core = lax.rem(lax.axis_index("expert"), 2)
        route = jnp.stack([route_of(experts_two, gates_two, slots_two, core), route_of(experts_one, gates_one, slots_one, core)])
        got = main_call(route, x_tokens, y_mid, dy_out, (w_gate_two, w_up_two, w_down_two), (w_gate_one, w_up_one, w_down_one))
        grads_two = wgrad_call(*got[1:6], "wgrad_two")
        grads_one = wgrad_call(*got[6:11], "wgrad_one")
        return (got[0],) + tuple(grads_one) + tuple(grads_two)

    return jax.shard_map(local_step, mesh=mesh, in_specs=(tok_spec,) * 9 + (weight_spec,) * 6, out_specs=(tok_spec,) + (grad_spec,) * 6, check_vma=False)
```

time: 175 us -> 98.2 us (0.56)
  Pallas kernels: 0 us -> 88 us
  waiting for transfers between devices: 65.2 us -> 0 us
  matrix products: 65.1 us -> 0 us
  starting transfers between devices: 19.1 us -> 0 us
  local copies, waits for them, and re-layouts: 21.6 us -> 6.88 us
    pallas_call x0 -> x3, Pallas kernels: none -> 88 us  [the longest x1 68.6 us: main_call(): pl.pallas_call(main_kernel, out_shape=(jax.ShapeDtypeStruct((TOK, D), BF1...]
    all_to_all x6 -> x0, waiting for transfers between devices: 65.2 us -> none  [the longest x2 26.2 us: layer_backward(): lax.all_to_all(z_send.reshape(n_experts, capacity, model_dim), 'expert',...]
    dot_general x22 -> x0, matrix products: 65.1 us -> none  [the longest x2 10.8 us: expert_grads(): jnp.einsum('erd,erf->edf', x_rows, d_gate, preferred_element_type=jnp.flo...]
    all_to_all x6 -> x0, starting transfers between devices: 19.1 us -> none  [the longest x2 7.34 us: layer_backward(): lax.all_to_all(z_send.reshape(n_experts, capacity, model_dim), 'expert',...]
    all_to_all x8 -> x0, local copies, waits for them, and re-layouts: 8.98 us -> none  [the longest x4 4.05 us: layer_backward(): lax.all_to_all(dx_rows, 'expert', 1, 0, tiled=True)]
    convert_element_type x2 -> x0, local copies, waits for them, and re-layouts: 4.73 us -> none  [expert_grads(): (jnp.einsum('erf,edf->erd', d_gate, w_gate, preferred_element_type=jnp.fl...]
    unnamed x64 -> x23, local copies, waits for them, and re-layouts: 6.92 us -> 6.88 us
  transfers between devices with their start and end apart: 6 -> 0, of which waited for: 6 -> 0; matrix products, arithmetic and copies ran while one was open for 33% -> 0% of each run, Pallas kernels for 0% -> 0%
where the time goes in v1:
time: 98.2 us; the launch traced here: 97.9 us
  Pallas kernels  88 us (90%)
  local copies, waits for them, and re-layouts  6.88 us (7%)
  other arithmetic  2.22 us (2%)
    pallas_call x1, Pallas kernels, main_call(): pl.pallas_call(main_kernel, out_shape=(jax.ShapeDtypeStruct((TOK, D), BF1...  68.6 us
    pallas_call x2, Pallas kernels, wgrad_call(): pl.pallas_call(wgrad_kernel, grid=(E, split), out_shape=(jax.ShapeDtypeSt...  19.5 us
    unnamed x23, local copies, waits for them, and re-layouts  6.88 us

profile of v1, /device:TPU:0, one launch (start us, length us, event | category | flops | bytes accessed | tf_op | source)
XLA Modules:
  0.0 97.9 jit_solution(5347011003804878538)
XLA Ops:
  0.7 0.7 convert_bitcast_fusion
  1.4 0.8 maximum_select_fusion
  2.3 0.6 pad_maximum_fusion.route_ref
  2.9 68.6 %moe_backward.1 = (bf16[64,1024]{1,0:T(8,128)(2,1)}, bf16[4,192,1024]{2,1,0:T(8,128)(2,1)}, bf16[4,192,1024]{2,1,0:T(8,128)(2,1)}, bf16[4,192,512]{2,1,0:T(8,128...) custom-call(f32[2,16,128]{2,1,0:T(8,128)} %pad_maximum_fusion.route_, ...), custom_call_target="tpu_custom_call" | custom-call | tf_op jit(solution)/shard_map/moe_backward/pallas_call | solution.py:284
  71.4 0.0 copy-start.2
  71.5 1.4 %copy-done.2 = bf16[4,192,1024]{2,1,0:T(8,128)(2,1)S(1)} copy-done((bf16[4,192,1024]{2,1,0:T(8,128)(2,1)S(1)}, bf16[4,192,1024]{2,1,0:T(8,128)(2,1)}, u32[]{:S(2)}) %copy-start.2) | copy-done | bytes 1572888
  72.9 0.0 copy-start.3
  72.9 1.4 %copy-done.3 = bf16[4,192,1024]{2,1,0:T(8,128)(2,1)S(1)} copy-done((bf16[4,192,1024]{2,1,0:T(8,128)(2,1)S(1)}, bf16[4,192,1024]{2,1,0:T(8,128)(2,1)}, u32[]{:S(2)}) %copy-start.3) | copy-done | bytes 1572888
  74.3 0.0 copy-start.7
  74.3 1.1 %copy-done.7 = bf16[4,192,512]{2,1,0:T(8,128)(2,1)S(1)} copy-done((bf16[4,192,512]{2,1,0:T(8,128)(2,1)S(1)}, bf16[4,192,512]{2,1,0:T(8,128)(2,1)}, u32[]{:S(2)}) %copy-start.7) | copy-done | bytes 786456
  75.4 0.0 copy-start.8
  75.4 1.1 %copy-done.8 = bf16[4,192,512]{2,1,0:T(8,128)(2,1)S(1)} copy-done((bf16[4,192,512]{2,1,0:T(8,128)(2,1)S(1)}, bf16[4,192,512]{2,1,0:T(8,128)(2,1)}, u32[]{:S(2)}) %copy-start.8) | copy-done | bytes 786456
  76.5 0.0 copy-start.9
  76.5 1.1 %copy-done.9 = bf16[4,192,512]{2,1,0:T(8,128)(2,1)S(1)} copy-done((bf16[4,192,512]{2,1,0:T(8,128)(2,1)S(1)}, bf16[4,192,512]{2,1,0:T(8,128)(2,1)}, u32[]{:S(2)}) %copy-start.9) | copy-done | bytes 786456
  77.7 0.0 copy-start
  77.7 0.0 copy-start.1
  77.7 0.0 copy-start.4
  77.7 0.0 copy-start.5
  77.7 0.0 copy-start.6
  77.7 10.0 %wgrad_one.1 = (f32[4,1024,512]{2,1,0:T(8,128)}, f32[4,1024,512]{2,1,0:T(8,128)}, f32[4,512,1024]{2,1,0:T(8,128)}) custom-call(bf16[4,192,1024]{2,1,0:T(8,128)(2,1)S(1)} %copy-done.2, bf16[4,192,1024]{2,1,0:T(8,128)(2,1)S(1)} %copy-done.3, bf16[4,192,512]{2,1,0:T(8,128)(2,1)S(1)} %copy-done.7, bf16[4,192,512]{2,1,0:T(8,128)(2,1)S(1)} %copy-done.8, ...), custom_call_target="tpu_custom_call" | custom-call | flops 2415919104 | bytes 25165824 | tf_op jit(solution)/shard_map/wgrad_one/pallas_call | solution.py:338
  87.7 0.0 copy-done
  87.7 0.0 copy-done.1
  87.7 0.0 copy-done.4
  87.7 0.0 copy-done.5
  87.7 0.0 copy-done.6
  87.7 0.0 copy-start.10
  87.7 9.5 %wgrad_two.1 = (f32[4,1024,512]{2,1,0:T(8,128)}, f32[4,1024,512]{2,1,0:T(8,128)}, f32[4,512,1024]{2,1,0:T(8,128)}) custom-call(bf16[4,192,1024]{2,1,0:T(8,128)(2,1)S(1)} %copy-done, bf16[4,192,1024]{2,1,0:T(8,128)(2,1)S(1)} %copy-done.1, bf16[4,192,512]{2,1,0:T(8,128)(2,1)S(1)} %copy-done.4, bf16[4,192,512]{2,1,0:T(8,128)(2,1)S(1)} %copy-done.5, ...), custom_call_target="tpu_custom_call" | custom-call | flops 2415919104 | bytes 25165824 | tf_op jit(solution)/shard_map/wgrad_two/pallas_call | solution.py:338
  97.2 0.0 copy-done.10
  97.2 0.7 copy.23
  (4 shorter events, 0.0 us)
Async XLA Ops:
  71.4 1.4 %copy-start.2 = (bf16[4,192,1024]{2,1,0:T(8,128)(2,1)S(1)}, bf16[4,192,1024]{2,1,0:T(8,128)(2,1)}, u32[]{:S(2)}) copy-start(bf16[4,192,1024]{2,1,0:T(8,128)(2,1)} %get-tuple-element.25.x_ref) | copy-start | bytes 4718596
  72.9 1.4 %copy-start.3 = (bf16[4,192,1024]{2,1,0:T(8,128)(2,1)S(1)}, bf16[4,192,1024]{2,1,0:T(8,128)(2,1)}, u32[]{:S(2)}) copy-start(bf16[4,192,1024]{2,1,0:T(8,128)(2,1)} %get-tuple-element.26.z_ref) | copy-start | bytes 4718596
  74.3 1.1 %copy-start.7 = (bf16[4,192,512]{2,1,0:T(8,128)(2,1)S(1)}, bf16[4,192,512]{2,1,0:T(8,128)(2,1)}, u32[]{:S(2)}) copy-start(bf16[4,192,512]{2,1,0:T(8,128)(2,1)} %get-tuple-element.27.h_ref) | copy-start | bytes 2359300
  75.4 1.1 %copy-start.8 = (bf16[4,192,512]{2,1,0:T(8,128)(2,1)S(1)}, bf16[4,192,512]{2,1,0:T(8,128)(2,1)}, u32[]{:S(2)}) copy-start(bf16[4,192,512]{2,1,0:T(8,128)(2,1)} %get-tuple-element.28.da_ref) | copy-start | bytes 2359300
  76.5 1.1 %copy-start.9 = (bf16[4,192,512]{2,1,0:T(8,128)(2,1)S(1)}, bf16[4,192,512]{2,1,0:T(8,128)(2,1)}, u32[]{:S(2)}) copy-start(bf16[4,192,512]{2,1,0:T(8,128)(2,1)} %get-tuple-element.29.db_ref) | copy-start | bytes 2359300
  77.7 10.0 %copy-start = (bf16[4,192,1024]{2,1,0:T(8,128)(2,1)S(1)}, bf16[4,192,1024]{2,1,0:T(8,128)(2,1)}, u32[]{:S(2)}) copy-start(bf16[4,192,1024]{2,1,0:T(8,128)(2,1)} %get-tuple-element.33.x_ref) | copy-start | bytes 4718596
  77.7 10.0 %copy-start.1 = (bf16[4,192,1024]{2,1,0:T(8,128)(2,1)S(1)}, bf16[4,192,1024]{2,1,0:T(8,128)(2,1)}, u32[]{:S(2)}) copy-start(bf16[4,192,1024]{2,1,0:T(8,128)(2,1)} %get-tuple-element.34.z_ref) | copy-start | bytes 4718596
  77.7 10.0 %copy-start.4 = (bf16[4,192,512]{2,1,0:T(8,128)(2,1)S(1)}, bf16[4,192,512]{2,1,0:T(8,128)(2,1)}, u32[]{:S(2)}) copy-start(bf16[4,192,512]{2,1,0:T(8,128)(2,1)} %get-tuple-element.35.h_ref) | copy-start | bytes 2359300
  77.7 10.0 %copy-start.5 = (bf16[4,192,512]{2,1,0:T(8,128)(2,1)S(1)}, bf16[4,192,512]{2,1,0:T(8,128)(2,1)}, u32[]{:S(2)}) copy-start(bf16[4,192,512]{2,1,0:T(8,128)(2,1)} %get-tuple-element.36.da_ref) | copy-start | bytes 2359300
  77.7 10.0 %copy-start.6 = (bf16[4,192,512]{2,1,0:T(8,128)(2,1)S(1)}, bf16[4,192,512]{2,1,0:T(8,128)(2,1)}, u32[]{:S(2)}) copy-start(bf16[4,192,512]{2,1,0:T(8,128)(2,1)} %get-tuple-element.37.db_ref) | copy-start | bytes 2359300
  87.7 9.5 %copy-start.10 = (bf16[64,1024]{1,0:T(8,128)(2,1)S(1)}, bf16[64,1024]{1,0:T(8,128)(2,1)}, u32[]{:S(2)}) copy-start(bf16[64,1024]{1,0:T(8,128)(2,1)} %get-tuple-element.56) | copy-start | bytes 393220

commit v2 on v1

--- a/solution.py
+++ b/solution.py
@@ -7,6 +7,7 @@
 from jax.sharding import PartitionSpec as P
 
 MESH = pl.DeviceIdType.MESH
+scope = jax.named_scope
 F32 = jnp.float32
 BF16 = jnp.bfloat16
 
@@ -42,7 +43,7 @@
 
 def main_kernel(
     route_ref, x_ref, y_ref, dy_ref, w1b_hbm, w3b_hbm, w2b_hbm, w1a_hbm, w3a_hbm, w2a_hbm,
-    dx_ref, xrb_hbm, zrb_hbm, hb_hbm, dab_hbm, dbb_hbm, xra_hbm, zra_hbm, ha_hbm, daa_hbm, dba_hbm,
+    own_hbm, d1_hbm, far0_hbm, far1_hbm, far2_hbm, xrb_hbm, zrb_hbm, hb_hbm, dab_hbm, dbb_hbm, xra_hbm, zra_hbm, ha_hbm, daa_hbm, dba_hbm,
     w_vm, route_g, y_g, dy_g, x_g, d1_g, d1_own,
     xr, zr, act_s, act_f, hid, da, db, dxp, perm, perm_t, gate,
     part, mate_recv, far_recv,
@@ -189,6 +190,12 @@
         mate_copy(layer, k).wait_recv()
         for p in range(CHIPS):
             part[layer, k, core, p] = part[layer, k, core, p] + mate_recv[layer, k, p]
+        if layer == 1:
+            cols = pl.ds(k * CW, CW)
+            out_start(part.at[layer, k, core, chip], own_hbm.at[:, cols])
+            for i, out in enumerate((far0_hbm, far1_hbm, far2_hbm)):
+                out_start(part.at[layer, k, core, far[i] // 2], out.at[:, cols])
+            return
         for i in range(3):
             c = far_copy(layer, k, i)
             c.start()
@@ -202,74 +209,95 @@
     def pair_of(buf, p):
         return buf[2 * p : 2 * p + 2].reshape(2 * TOK, buf.shape[-1])
 
-    ag_pass_on(S_ROUTE, route_g)
-    ag_finish(S_ROUTE, route_g)
-    build_routes(0)
-    ag_pass_on(S_Y, y_g)
-    ag_finish(S_Y, y_g)
-    gather_rows(lambda p: pair_of(y_g, p), xr, 0, slice(None), False)
-    out_start(xr.at[0], xrb_hbm)
-    w_copy(0).wait()
-    w_copy(1).wait()
-
-    @pl.loop(0, E)
-    def _(e):
-        forward_expert(0, e)
-
-    out_start(hid.at[0], hb_hbm)
-    ag_pass_on(S_DY, dy_g)
-    ag_finish(S_DY, dy_g)
-    gather_rows(lambda p: pair_of(dy_g, p), zr, 0, slice(None), True)
-    out_start(zr.at[0], zrb_hbm)
-    w_copy(2).wait()
-    hidden_grads(0)
-    out_start(da.at[0], dab_hbm)
-    out_start(db.at[0], dbb_hbm)
+    with scope("route_two"):
+        ag_pass_on(S_ROUTE, route_g)
+        ag_finish(S_ROUTE, route_g)
+        build_routes(0)
+    with scope("wait_y"):
+        ag_pass_on(S_Y, y_g)
+        ag_finish(S_Y, y_g)
+    with scope("rows_y"):
+        gather_rows(lambda p: pair_of(y_g, p), xr, 0, slice(None), False)
+        out_start(xr.at[0], xrb_hbm)
+        w_copy(0).wait()
+        w_copy(1).wait()
+
+    with scope("forward_two"):
+        @pl.loop(0, E)
+        def _(e):
+            forward_expert(0, e)
+
+        out_start(hid.at[0], hb_hbm)
+    with scope("wait_dy"):
+        ag_pass_on(S_DY, dy_g)
+        ag_finish(S_DY, dy_g)
+    with scope("rows_dy"):
+        gather_rows(lambda p: pair_of(dy_g, p), zr, 0, slice(None), True)
+        out_start(zr.at[0], zrb_hbm)
+        w_copy(2).wait()
+    with scope("hidden_two"):
+        hidden_grads(0)
+        out_start(da.at[0], dab_hbm)
+        out_start(db.at[0], dbb_hbm)
     for k in range(CH):
-        row_chunk(0, k)
+        with scope(f"chunk_two_{k}"):
+            row_chunk(0, k)
         if k >= 1:
-            mate_sum(0, k - 1)
-    mate_sum(0, CH - 1)
-
-    ag_pass_on(S_X, x_g)
-    build_routes(1)
-    ag_finish(S_X, x_g)
-    gather_rows(lambda p: pair_of(x_g, p), xr, 1, slice(None), False)
-    out_start(xr.at[1], xra_hbm)
-    for i in range(3, 6):
-        w_copy(i).wait()
+            with scope(f"mate_two_{k - 1}"):
+                mate_sum(0, k - 1)
+    with scope("mate_two_last"):
+        mate_sum(0, CH - 1)
+
+    with scope("wait_x"):
+        ag_pass_on(S_X, x_g)
+        build_routes(1)
+        ag_finish(S_X, x_g)
+    with scope("rows_x"):
+        gather_rows(lambda p: pair_of(x_g, p), xr, 1, slice(None), False)
+        out_start(xr.at[1], xra_hbm)
+        for i in range(3, 6):
+            w_copy(i).wait()
 
     def mid_grad(k):
         cols = slice(k * CW, (k + 1) * CW)
         mine = (dy_ref[:, cols].astype(F32) + far_sum(0, k)).astype(BF16)
         d1_own[k] = mine
         d1_g[k, me] = mine
+        out_start(d1_own.at[k], d1_hbm.at[:, pl.ds(k * CW, CW)])
         ag_start(S_D1 + k, d1_own.at[k], d1_g.at[k])
 
     for k in range(CH):
-        forward_expert(1, k)
-        mid_grad(k)
+        with scope(f"forward_one_{k}"):
+            forward_expert(1, k)
+        with scope(f"mid_{k}"):
+            mid_grad(k)
     out_start(hid.at[1], ha_hbm)
     for k in range(CH):
-        ag_pass_on(S_D1 + k, d1_g.at[k])
+        with scope(f"pass_on_{k}"):
+            ag_pass_on(S_D1 + k, d1_g.at[k])
     for k in range(CH):
-        ag_finish(S_D1 + k, d1_g.at[k])
-        gather_rows(lambda p: d1_g[k, 2 * p : 2 * p + 2].reshape(2 * TOK, CW), zr, 1, slice(k * CW, (k + 1) * CW), True)
+        with scope(f"finish_{k}"):
+            ag_finish(S_D1 + k, d1_g.at[k])
+        with scope(f"rows_d1_{k}"):
+            gather_rows(lambda p: d1_g[k, 2 * p : 2 * p + 2].reshape(2 * TOK, CW), zr, 1, slice(k * CW, (k + 1) * CW), True)
     out_start(zr.at[1], zra_hbm)
-    hidden_grads(1)
-    out_start(da.at[1], daa_hbm)
-    out_start(db.at[1], dba_hbm)
+    with scope("hidden_one"):
+        hidden_grads(1)
+        out_start(da.at[1], daa_hbm)
+        out_start(db.at[1], dba_hbm)
     for k in range(CH):
-        row_chunk(1, k)
+        with scope(f"chunk_one_{k}"):
+            row_chunk(1, k)
         if k >= 1:
-            mate_sum(1, k - 1)
-    mate_sum(1, CH - 1)
-    for k in range(CH):
-        dx_ref[:, k * CW : (k + 1) * CW] = (d1_own[k].astype(F32) + far_sum(1, k)).astype(BF16)
-    for c in sends:
-        c.wait_send()
-    for c in outs:
-        c.wait()
+            with scope(f"mate_one_{k - 1}"):
+                mate_sum(1, k - 1)
+    with scope("mate_one_last"):
+        mate_sum(1, CH - 1)
+    with scope("drain"):
+        for c in sends:
+            c.wait_send()
+        for c in outs:
+            c.wait()
 
 
 def main_call(route, x, y, dy, weights_two, weights_one):
@@ -277,15 +305,16 @@
     hbm = pl.BlockSpec(memory_space=pl.ANY)
     rows_d = jax.ShapeDtypeStruct((E, ROWS, D), BF16)
     rows_f = jax.ShapeDtypeStruct((E, ROWS, F), BF16)
+    sums = jax.ShapeDtypeStruct((TOK, D), F32)
     saved = (rows_d, rows_d, rows_f, rows_f, rows_f)
     w_up = pltpu.VMEM((E, D, F), BF16)
     w_dn = pltpu.VMEM((E, F, D), BF16)
     dma = pltpu.SemaphoreType.DMA
     return pl.pallas_call(
         main_kernel,
-        out_shape=(jax.ShapeDtypeStruct((TOK, D), BF16),) + saved + saved,
+        out_shape=(sums, jax.ShapeDtypeStruct((TOK, D), BF16), sums, sums, sums) + saved + saved,
         in_specs=[vm] * 4 + [hbm] * 6,
-        out_specs=(vm,) + (hbm,) * 10,
+        out_specs=(hbm,) * 15,
         scratch_shapes=[
             (w_up, w_up, w_dn, w_up, w_up, w_dn),
             pltpu.VMEM((DEVS, 2, 16, 2 * TOK), F32),
@@ -313,7 +342,7 @@
             dma((N_STREAMS, 7)),
             dma((2, CH, 4)),
             dma((2, CH, 4)),
-            dma((10,)),
+            dma((10 + 5 * CH,)),
         ],
         compiler_params=pltpu.CompilerParams(collective_id=0, has_side_effects=True, vmem_limit_bytes=VMEM_LIMIT),
         name="moe_backward",
@@ -341,7 +370,7 @@
         out_shape=(jax.ShapeDtypeStruct((E, D, F), F32), jax.ShapeDtypeStruct((E, D, F), F32), jax.ShapeDtypeStruct((E, F, D), F32)),
         in_specs=[part_d, whole_d, part_f, whole_f, whole_f],
         out_specs=(up, up, dn),
-        compiler_params=pltpu.CompilerParams(vmem_limit_bytes=40_000_000),
+        compiler_params=pltpu.CompilerParams(vmem_limit_bytes=VMEM_LIMIT),
         cost_estimate=pl.CostEstimate(flops=6 * E * ROWS * D * F, bytes_accessed=12 * E * D * F, transcendentals=0),
         name=name,
     )(xr, zr, hid, da, db)
@@ -366,8 +395,11 @@
         core = lax.rem(lax.axis_index("expert"), 2)
         route = jnp.stack([route_of(experts_two, gates_two, slots_two, core), route_of(experts_one, gates_one, slots_one, core)])
         got = main_call(route, x_tokens, y_mid, dy_out, (w_gate_two, w_up_two, w_down_two), (w_gate_one, w_up_one, w_down_one))
-        grads_two = wgrad_call(*got[1:6], "wgrad_two")
-        grads_one = wgrad_call(*got[6:11], "wgrad_one")
-        return (got[0],) + tuple(grads_one) + tuple(grads_two)
+        own, d1 = got[0:2]
+        far = [lax.ppermute(got[2 + i], "expert", [(d, d ^ flip) for d in range(DEVS)]) for i, flip in enumerate((2, 4, 6))]
+        grads_two = wgrad_call(*got[5:10], "wgrad_two")
+        grads_one = wgrad_call(*got[10:15], "wgrad_one")
+        dx = (d1.astype(F32) + (own + (far[0] + far[1] + far[2]))).astype(BF16)
+        return (dx,) + tuple(grads_one) + tuple(grads_two)
 
     return jax.shard_map(local_step, mesh=mesh, in_specs=(tok_spec,) * 9 + (weight_spec,) * 6, out_specs=(tok_spec,) + (grad_spec,) * 6, check_vma=False)

time: 98.2 us -> 93.9 us (0.956)
  local copies, waits for them, and re-layouts: 6.88 us -> 0.01 us
  starting transfers between devices: 0 us -> 3.51 us
  Pallas kernels: 88 us -> 85.1 us
  other arithmetic: 2.22 us -> 3.9 us
    pallas_call x1, Pallas kernels: 68.6 us -> 60 us  [main_call(): pl.pallas_call(main_kernel, out_shape=(sums, jax.ShapeDtypeStruct((TOK, D...]
    unnamed x23 -> x4, local copies, waits for them, and re-layouts: 6.88 us -> 0.01 us
    pallas_call x2, Pallas kernels: 19.5 us -> 25.1 us  [wgrad_call(): pl.pallas_call(wgrad_kernel, grid=(E, split), out_shape=(jax.ShapeDtypeSt...]
    ppermute x0 -> x3, starting transfers between devices: none -> 3.51 us  [local_step(): lax.ppermute(got[2 + i], 'expert', [(d, d ^ flip) for d in range(DEVS)])]
    convert_element_type x0 -> x1, other arithmetic: none -> 1.69 us  [local_step(): dx = (d1.astype(F32) + (own + (far[0] + far[1] + far[2]))).astype(BF16)]
  transfers between devices with their start and end apart: 0 -> 3, of which waited for: 0 -> 0; matrix products, arithmetic and copies ran while one was open for 0% -> 0% of each run, Pallas kernels for 0% -> 27%
where the time goes in v2:
time: 93.9 us; the launch traced here: 93.2 us
  Pallas kernels  85.1 us (91%)
  other arithmetic  3.9 us (4%)
  starting transfers between devices  3.51 us (4%)
    pallas_call x1, Pallas kernels, main_call(): pl.pallas_call(main_kernel, out_shape=(sums, jax.ShapeDtypeStruct((TOK, D...  60 us
    pallas_call x2, Pallas kernels, wgrad_call(): pl.pallas_call(wgrad_kernel, grid=(E, split), out_shape=(jax.ShapeDtypeSt...  25.1 us
    ppermute x3, starting transfers between devices, local_step(): lax.ppermute(got[2 + i], 'expert', [(d, d ^ flip) for d in range(DEVS)])  3.51 us
  transfers between devices with their start and end apart: 3, of which 0 were waited for; matrix products, arithmetic and copies ran while one was open for 0% of the time, Pallas kernels for 27%

profile of v2, /device:TPU:0, one launch (start us, length us, event | category | flops | bytes accessed | tf_op | source)
XLA Modules:
  0.0 93.2 jit_solution(7257634628086553997)
XLA Ops:
  0.7 0.7 convert_bitcast_fusion
  1.4 0.8 maximum_select_fusion
  2.3 0.6 pad_maximum_fusion.route_ref
  2.9 60.0 %moe_backward.1 = (f32[64,1024]{1,0:T(8,128)}, bf16[64,1024]{1,0:T(8,128)(2,1)}, f32[64,1024]{1,0:T(8,128)}, f32[64,1024]{1,0:T(8,128)}, f32[64,1024]{1,0:T(8,12...) custom-call(f32[2,16,128]{2,1,0:T(8,128)} %pad_maximum_fusion.route_, ...), custom_call_target="tpu_custom_call" | custom-call | tf_op jit(solution)/shard_map/moe_backward/pallas_call | solution.py:313
  62.9 0.6 collective-permute-start
  63.4 0.5 collective-permute-start.1
  64.0 2.4 %collective-permute-start.2 = (f32[64,1024]{1,0:T(8,128)}, f32[64,1024]{1,0:T(8,128)}, u32[]{:S(2)}, u32[]{:S(2)}) collective-permute-start(f32[64,1024]{1,0:T(8,128)} %get-tuple-element.32), channel_id=1, source_target_pairs={{0,6},{1,7},{2,4},{3,5},{4,2},{5,3},{6,0},{7,1}} | collective-permute-start | bytes 786440 | tf_op jit(solution)/shard_map/ppermute | solution.py:399
  66.4 12.5 %wgrad_one.1 = (f32[4,1024,512]{2,1,0:T(8,128)}, f32[4,1024,512]{2,1,0:T(8,128)}, f32[4,512,1024]{2,1,0:T(8,128)}) custom-call(bf16[4,192,1024]{2,1,0:T(8,128)(2,1)} %get-tuple-element.33.x_ref, bf16[4,192,1024]{2,1,0:T(8,128)(2,1)} %get-tuple-element.34.z_ref, bf16[4,192,512]{2,1,0:T(8,128)(2,1)} %get-tuple-element.35.h_ref, ...), custom_call_target="tpu_custom_call" | custom-call | flops 2415919104 | bytes 25165824 | tf_op jit(solution)/shard_map/wgrad_one/pallas_call | solution.py:367
  78.9 0.0 copy-start
  78.9 0.0 copy-start.1
  78.9 12.6 %wgrad_two.1 = (f32[4,1024,512]{2,1,0:T(8,128)}, f32[4,1024,512]{2,1,0:T(8,128)}, f32[4,512,1024]{2,1,0:T(8,128)}) custom-call(bf16[4,192,1024]{2,1,0:T(8,128)(2,1)} %get-tuple-element.41.x_ref, bf16[4,192,1024]{2,1,0:T(8,128)(2,1)} %get-tuple-element.42.z_ref, bf16[4,192,512]{2,1,0:T(8,128)(2,1)} %get-tuple-element.43.h_ref, ...), custom_call_target="tpu_custom_call" | custom-call | flops 2415919104 | bytes 25165824 | tf_op jit(solution)/shard_map/wgrad_two/pallas_call | solution.py:367
  91.5 0.0 collective-permute-done
  91.5 0.0 collective-permute-done.1
  91.5 0.0 collective-permute-done.2
  91.5 0.0 copy-done
  91.5 0.0 copy-done.1
  91.5 1.7 %add_convert_fusion = bf16[64,1024]{1,0:T(8,128)(2,1)} fusion(f32[64,1024]{1,0:T(8,128)S(1)} %copy-done, f32[64,1024]{1,0:T(8,128)} %collective-permute-done.2, f32[64,1024]{1,0:T(8,128)S(1)} %collective-permute-done, f32[64,1024]{1,0:T(8,128)S(1)} %collective-permute-done.1, bf16[64,1024]{1,0:T(8,128)(2,1)S(1)} %copy-done.1), kind=kLoop, calls=%fused_computation | loop fusion | flops 393216 | bytes 1310720 | tf_op jit(solution)/shard_map/convert_element_type | solution.py:402
  (4 shorter events, 0.0 us)
Async XLA Ops:
  62.9 28.7 %collective-permute-start = (f32[64,1024]{1,0:T(8,128)}, f32[64,1024]{1,0:T(8,128)S(1)}, u32[]{:S(2)}, u32[]{:S(2)}) collective-permute-start(f32[64,1024]{1,0:T(8,128)} %get-tuple-element.30), channel_id=1, source_target_pairs={{0,2},{1,3},{2,0},{3,1},{4,6},{5,7},{6,4},{7,5}} | collective-permute-start | bytes 786440 | tf_op jit(solution)/shard_map/ppermute | solution.py:399
  63.4 28.1 %collective-permute-start.1 = (f32[64,1024]{1,0:T(8,128)}, f32[64,1024]{1,0:T(8,128)S(1)}, u32[]{:S(2)}, u32[]{:S(2)}) collective-permute-start(f32[64,1024]{1,0:T(8,128)} %get-tuple-element.31), channel_id=1, source_target_pairs={{0,4},{1,5},{2,6},{3,7},{4,0},{5,1},{6,2},{7,3}} | collective-permute-start | bytes 786440 | tf_op jit(solution)/shard_map/ppermute | solution.py:399
  64.0 27.5 %collective-permute-start.2 = (f32[64,1024]{1,0:T(8,128)}, f32[64,1024]{1,0:T(8,128)}, u32[]{:S(2)}, u32[]{:S(2)}) collective-permute-start(f32[64,1024]{1,0:T(8,128)} %get-tuple-element.32), channel_id=1, source_target_pairs={{0,6},{1,7},{2,4},{3,5},{4,2},{5,3},{6,0},{7,1}} | collective-permute-start | bytes 786440 | tf_op jit(solution)/shard_map/ppermute | solution.py:399
  78.9 12.6 %copy-start = (f32[64,1024]{1,0:T(8,128)S(1)}, f32[64,1024]{1,0:T(8,128)}, u32[]{:S(2)}) copy-start(f32[64,1024]{1,0:T(8,128)} %get-tuple-element.29) | copy-start | bytes 786436
  78.9 12.6 %copy-start.1 = (bf16[64,1024]{1,0:T(8,128)(2,1)S(1)}, bf16[64,1024]{1,0:T(8,128)(2,1)}, u32[]{:S(2)}) copy-start(bf16[64,1024]{1,0:T(8,128)(2,1)} %get-tuple-element.28) | copy-start | bytes 393220

commit v3 on v2

--- a/solution.py
+++ b/solution.py
@@ -23,11 +23,15 @@
 PROWS = E * PAIR
 CH = 4
 CW = D // CH
-VMEM_LIMIT = 66_000_000
+MAIN_VMEM = 48_000_000
+WGRAD_VMEM = 40_000_000
 
 S_ROUTE, S_Y, S_DY, S_X, S_D1 = 0, 1, 2, 3, 4
 N_STREAMS = S_D1 + CH
 
+SETS = 2
+HALVES = 2
+
 
 def nt_dot(a, b):
     return lax.dot_general(a, b, (((1,), (1,)), ((), ())), preferred_element_type=F32)
@@ -43,12 +47,15 @@
 
 def main_kernel(
     route_ref, x_ref, y_ref, dy_ref, w1b_hbm, w3b_hbm, w2b_hbm, w1a_hbm, w3a_hbm, w2a_hbm,
-    own_hbm, d1_hbm, far0_hbm, far1_hbm, far2_hbm, xrb_hbm, zrb_hbm, hb_hbm, dab_hbm, dbb_hbm, xra_hbm, zra_hbm, ha_hbm, daa_hbm, dba_hbm,
+    own_hbm, d1_hbm, far0_hbm, far1_hbm, far2_hbm,
+    xr_two, zr_two, hid_two, da_two, db_two, xr_one, zr_one, hid_one, da_one, db_one,
     w_vm, route_g, y_g, dy_g, x_g, d1_g, d1_own,
-    xr, zr, act_s, act_f, hid, da, db, dxp, perm, perm_t, gate,
+    act_s, act_f, dxp, perm, perm_t, gate,
     part, mate_recv, far_recv,
     w_sem, ag_send, ag_recv, rs_send, rs_recv, out_sem,
 ):
+    xr, zr, hid = (xr_two, xr_one), (zr_two, zr_one), (hid_two, hid_one)
+    da, db = (da_two, da_one), (db_two, db_one)
     me = lax.axis_index("expert")
     core = lax.rem(me, 2)
     xpos = lax.rem(me // 2, 2)
@@ -138,27 +145,27 @@
                 got = got * gate[p]
             got = got.astype(BF16)
             for e in range(E):
-                dst[layer, e, p * PAIR : (p + 1) * PAIR, cols] = got[e * PAIR : (e + 1) * PAIR]
+                dst[layer][e, p * PAIR : (p + 1) * PAIR, cols] = got[e * PAIR : (e + 1) * PAIR]
 
     def forward_expert(layer, e):
         w1, w3 = w_vm[3 * layer], w_vm[3 * layer + 1]
-        rows = xr[layer, e]
+        rows = xr[layer][e]
         a = nn_dot(rows, w1[e]).astype(BF16).astype(F32)
         b = nn_dot(rows, w3[e]).astype(BF16).astype(F32)
         sig = jax.nn.sigmoid(a)
         s = a * sig
         act_s[e] = s
         act_f[e] = b * (sig * (1.0 + a * (1.0 - sig)))
-        hid[layer, e] = (s * b).astype(BF16)
+        hid[layer][e] = (s * b).astype(BF16)
 
     def hidden_grads(layer):
         w2 = w_vm[3 * layer + 2]
 
         @pl.loop(0, E)
         def _(e):
-            dh = nt_dot(zr[layer, e], w2[e])
-            da[layer, e] = (dh * act_f[e]).astype(BF16)
-            db[layer, e] = (dh * act_s[e]).astype(BF16)
+            dh = nt_dot(zr[layer][e], w2[e])
+            da[layer][e] = (dh * act_f[e]).astype(BF16)
+            db[layer][e] = (dh * act_s[e]).astype(BF16)
 
     def row_chunk(layer, k):
         w1, w3 = w_vm[3 * layer], w_vm[3 * layer + 1]
@@ -166,7 +173,7 @@
 
         @pl.loop(0, E)
         def _(e):
-            g = nt_dot(da[layer, e], w1[e, cols, :]) + nt_dot(db[layer, e], w3[e, cols, :])
+            g = nt_dot(da[layer][e], w1[e, cols, :]) + nt_dot(db[layer][e], w3[e, cols, :])
             g = g.astype(BF16)
             for p in range(CHIPS):
                 dxp[k % 2, p, e] = g[p * PAIR : (p + 1) * PAIR]
@@ -218,7 +225,6 @@
         ag_finish(S_Y, y_g)
     with scope("rows_y"):
         gather_rows(lambda p: pair_of(y_g, p), xr, 0, slice(None), False)
-        out_start(xr.at[0], xrb_hbm)
         w_copy(0).wait()
         w_copy(1).wait()
 
@@ -227,18 +233,14 @@
         def _(e):
             forward_expert(0, e)
 
-        out_start(hid.at[0], hb_hbm)
     with scope("wait_dy"):
         ag_pass_on(S_DY, dy_g)
         ag_finish(S_DY, dy_g)
     with scope("rows_dy"):
         gather_rows(lambda p: pair_of(dy_g, p), zr, 0, slice(None), True)
-        out_start(zr.at[0], zrb_hbm)
         w_copy(2).wait()
     with scope("hidden_two"):
         hidden_grads(0)
-        out_start(da.at[0], dab_hbm)
-        out_start(db.at[0], dbb_hbm)
     for k in range(CH):
         with scope(f"chunk_two_{k}"):
             row_chunk(0, k)
@@ -254,7 +256,6 @@
         ag_finish(S_X, x_g)
     with scope("rows_x"):
         gather_rows(lambda p: pair_of(x_g, p), xr, 1, slice(None), False)
-        out_start(xr.at[1], xra_hbm)
         for i in range(3, 6):
             w_copy(i).wait()
 
@@ -271,7 +272,6 @@
             forward_expert(1, k)
         with scope(f"mid_{k}"):
             mid_grad(k)
-    out_start(hid.at[1], ha_hbm)
     for k in range(CH):
         with scope(f"pass_on_{k}"):
             ag_pass_on(S_D1 + k, d1_g.at[k])
@@ -280,11 +280,8 @@
             ag_finish(S_D1 + k, d1_g.at[k])
         with scope(f"rows_d1_{k}"):
             gather_rows(lambda p: d1_g[k, 2 * p : 2 * p + 2].reshape(2 * TOK, CW), zr, 1, slice(k * CW, (k + 1) * CW), True)
-    out_start(zr.at[1], zra_hbm)
     with scope("hidden_one"):
         hidden_grads(1)
-        out_start(da.at[1], daa_hbm)
-        out_start(db.at[1], dba_hbm)
     for k in range(CH):
         with scope(f"chunk_one_{k}"):
             row_chunk(1, k)
@@ -303,8 +300,8 @@
 def main_call(route, x, y, dy, weights_two, weights_one):
     vm = pl.BlockSpec(memory_space=pltpu.VMEM)
     hbm = pl.BlockSpec(memory_space=pl.ANY)
-    rows_d = jax.ShapeDtypeStruct((E, ROWS, D), BF16)
-    rows_f = jax.ShapeDtypeStruct((E, ROWS, F), BF16)
+    rows_d = pltpu.VMEM((E, ROWS, D), BF16)
+    rows_f = pltpu.VMEM((E, ROWS, F), BF16)
     sums = jax.ShapeDtypeStruct((TOK, D), F32)
     saved = (rows_d, rows_d, rows_f, rows_f, rows_f)
     w_up = pltpu.VMEM((E, D, F), BF16)
@@ -314,7 +311,7 @@
         main_kernel,
         out_shape=(sums, jax.ShapeDtypeStruct((TOK, D), BF16), sums, sums, sums) + saved + saved,
         in_specs=[vm] * 4 + [hbm] * 6,
-        out_specs=(hbm,) * 15,
+        out_specs=(hbm,) * 5 + (vm,) * 10,
         scratch_shapes=[
             (w_up, w_up, w_dn, w_up, w_up, w_dn),
             pltpu.VMEM((DEVS, 2, 16, 2 * TOK), F32),
@@ -323,13 +320,8 @@
             pltpu.VMEM((DEVS, TOK, D), BF16),
             pltpu.VMEM((CH, DEVS, TOK, CW), BF16),
             pltpu.VMEM((CH, TOK, CW), BF16),
-            pltpu.VMEM((2, E, ROWS, D), BF16),
-            pltpu.VMEM((2, E, ROWS, D), BF16),
             pltpu.VMEM((E, ROWS, F), F32),
             pltpu.VMEM((E, ROWS, F), F32),
-            pltpu.VMEM((2, E, ROWS, F), BF16),
-            pltpu.VMEM((2, E, ROWS, F), BF16),
-            pltpu.VMEM((2, E, ROWS, F), BF16),
             pltpu.VMEM((2, CHIPS, E, PAIR, CW), BF16),
             pltpu.VMEM((CHIPS, PROWS, 2 * TOK), BF16),
             pltpu.VMEM((CHIPS, 2 * TOK, PROWS), BF16),
@@ -342,38 +334,65 @@
             dma((N_STREAMS, 7)),
             dma((2, CH, 4)),
             dma((2, CH, 4)),
-            dma((10 + 5 * CH,)),
+            dma((5 * CH,)),
         ],
-        compiler_params=pltpu.CompilerParams(collective_id=0, has_side_effects=True, vmem_limit_bytes=VMEM_LIMIT),
+        compiler_params=pltpu.CompilerParams(collective_id=0, has_side_effects=True, vmem_limit_bytes=MAIN_VMEM),
         name="moe_backward",
     )(route, x, y, dy, *weights_two, *weights_one)
 
 
-def wgrad_kernel(x_ref, z_ref, h_ref, da_ref, db_ref, dw1_ref, dw3_ref, dw2_ref):
-    x = x_ref[0]
-    dw1_ref[0] = tn_dot(x, da_ref[0])
-    dw3_ref[0] = tn_dot(x, db_ref[0])
-    dw2_ref[0] = tn_dot(h_ref[0], z_ref[0])
-
-
-def wgrad_call(xr, zr, hid, da, db, name):
-    split = 2
-    whole_d = pl.BlockSpec((1, ROWS, D), lambda e, j: (e, 0, 0))
-    whole_f = pl.BlockSpec((1, ROWS, F), lambda e, j: (e, 0, 0))
-    part_d = pl.BlockSpec((1, ROWS, D // split), lambda e, j: (e, 0, j))
-    part_f = pl.BlockSpec((1, ROWS, F // split), lambda e, j: (e, 0, j))
-    up = pl.BlockSpec((1, D // split, F), lambda e, j: (e, j, 0))
-    dn = pl.BlockSpec((1, F // split, D), lambda e, j: (e, j, 0))
+def wgrad_kernel(*refs):
+    saved, outs, bufs, out_sem = (refs[0:5], refs[5:10]), (refs[10:13], refs[13:16]), refs[16:19], refs[19]
+
+    def out_copy(layer, m, e, slot, h):
+        n = bufs[m].shape[1] // HALVES
+        rows = pl.ds(h * n, n)
+        return pltpu.make_async_copy(bufs[m].at[slot, rows], outs[layer][m].at[e, rows], out_sem.at[slot, m, h])
+
+    for layer in range(2):
+        xr, zr, hid, da, db = saved[layer]
+
+        @pl.loop(0, E)
+        def _(e):
+            i = layer * E + e
+            slot = lax.rem(i, SETS)
+            for m, lhs, rhs in ((2, hid, zr), (0, xr, da), (1, xr, db)):
+                n = bufs[m].shape[1] // HALVES
+                for h in range(HALVES):
+                    rows = slice(h * n, (h + 1) * n)
+
+                    @pl.when(i >= SETS)
+                    def _():
+                        out_copy(layer, m, e, slot, h).wait()
+
+                    bufs[m][slot, rows] = tn_dot(lhs[e, :, rows], rhs[e])
+                    out_copy(layer, m, e, slot, h).start()
+
+    for i in range(2 * E - SETS, 2 * E):
+        for m in (2, 0, 1):
+            for h in range(HALVES):
+                out_copy(i // E, m, i % E, i % SETS, h).wait()
+
+
+def wgrad_call(*saved):
+    up = jax.ShapeDtypeStruct((E, D, F), F32)
+    dn = jax.ShapeDtypeStruct((E, F, D), F32)
+    hbm = pl.BlockSpec(memory_space=pl.ANY)
     return pl.pallas_call(
         wgrad_kernel,
-        grid=(E, split),
-        out_shape=(jax.ShapeDtypeStruct((E, D, F), F32), jax.ShapeDtypeStruct((E, D, F), F32), jax.ShapeDtypeStruct((E, F, D), F32)),
-        in_specs=[part_d, whole_d, part_f, whole_f, whole_f],
-        out_specs=(up, up, dn),
-        compiler_params=pltpu.CompilerParams(vmem_limit_bytes=VMEM_LIMIT),
-        cost_estimate=pl.CostEstimate(flops=6 * E * ROWS * D * F, bytes_accessed=12 * E * D * F, transcendentals=0),
-        name=name,
-    )(xr, zr, hid, da, db)
+        out_shape=(up, up, dn) * 2,
+        in_specs=[pl.BlockSpec(memory_space=pltpu.VMEM)] * 10,
+        out_specs=(hbm,) * 6,
+        scratch_shapes=[
+            pltpu.VMEM((SETS, D, F), F32),
+            pltpu.VMEM((SETS, D, F), F32),
+            pltpu.VMEM((SETS, F, D), F32),
+            pltpu.SemaphoreType.DMA((SETS, 3, HALVES)),
+        ],
+        compiler_params=pltpu.CompilerParams(vmem_limit_bytes=WGRAD_VMEM),
+        cost_estimate=pl.CostEstimate(flops=12 * E * ROWS * D * F, bytes_accessed=24 * E * D * F, transcendentals=0),
+        name="weight_grads",
+    )(*saved)
 
 
 def route_of(experts, gates, slots, core):
@@ -397,9 +416,8 @@
         got = main_call(route, x_tokens, y_mid, dy_out, (w_gate_two, w_up_two, w_down_two), (w_gate_one, w_up_one, w_down_one))
         own, d1 = got[0:2]
         far = [lax.ppermute(got[2 + i], "expert", [(d, d ^ flip) for d in range(DEVS)]) for i, flip in enumerate((2, 4, 6))]
-        grads_two = wgrad_call(*got[5:10], "wgrad_two")
-        grads_one = wgrad_call(*got[10:15], "wgrad_one")
+        grads = wgrad_call(*got[5:15])
         dx = (d1.astype(F32) + (own + (far[0] + far[1] + far[2]))).astype(BF16)
-        return (dx,) + tuple(grads_one) + tuple(grads_two)
+        return (dx,) + tuple(grads[3:6]) + tuple(grads[0:3])
 
     return jax.shard_map(local_step, mesh=mesh, in_specs=(tok_spec,) * 9 + (weight_spec,) * 6, out_specs=(tok_spec,) + (grad_spec,) * 6, check_vma=False)

time: 93.9 us -> 84.3 us (0.90)
  Pallas kernels: 85.1 us -> 76.9 us
  other arithmetic: 3.9 us -> 2.95 us
    pallas_call x2 -> x1, Pallas kernels: 25.1 us -> 17 us  [wgrad_call(): pl.pallas_call(wgrad_kernel, out_shape=(up, up, dn) * 2, in_specs=[pl.Blo...]
    convert_element_type x1, other arithmetic: 1.69 us -> 0.73 us  [local_step(): dx = (d1.astype(F32) + (own + (far[0] + far[1] + far[2]))).astype(BF16)]
  transfers between devices with their start and end apart: 3 -> 3, of which waited for: 0 -> 0; matrix products, arithmetic and copies ran while one was open for 0% -> 0% of each run, Pallas kernels for 27% -> 20%
where the time goes in v3:
time: 84.3 us; the launch traced here: 84.1 us
  Pallas kernels  76.9 us (91%)
  starting transfers between devices  3.51 us (4%)
  other arithmetic  2.95 us (3%)
    pallas_call x1, Pallas kernels, main_call(): pl.pallas_call(main_kernel, out_shape=(sums, jax.ShapeDtypeStruct((TOK, D...  59.9 us
    pallas_call x1, Pallas kernels, wgrad_call(): pl.pallas_call(wgrad_kernel, out_shape=(up, up, dn) * 2, in_specs=[pl.Blo...  17 us
    ppermute x3, starting transfers between devices, local_step(): lax.ppermute(got[2 + i], 'expert', [(d, d ^ flip) for d in range(DEVS)])  3.51 us
  transfers between devices with their start and end apart: 3, of which 0 were waited for; matrix products, arithmetic and copies ran while one was open for 0% of the time, Pallas kernels for 20%

profile of v3, /device:TPU:0, one launch (start us, length us, event | category | flops | bytes accessed | tf_op | source)
XLA Modules:
  0.0 84.1 jit_solution(18309706755501448004)
XLA Ops:
  0.7 0.7 convert_bitcast_fusion
  1.4 0.8 maximum_select_fusion
  2.3 0.6 pad_maximum_fusion.route_ref
  2.9 59.9 %moe_backward.1 = (f32[64,1024]{1,0:T(8,128)}, bf16[64,1024]{1,0:T(8,128)(2,1)}, f32[64,1024]{1,0:T(8,128)}, f32[64,1024]{1,0:T(8,128)}, f32[64,1024]{1,0:T(8,12...) custom-call(f32[2,16,128]{2,1,0:T(8,128)} %pad_maximum_fusion.route_, ...), custom_call_target="tpu_custom_call" | custom-call | tf_op jit(solution)/shard_map/moe_backward/pallas_call | solution.py:310
  62.8 0.6 collective-permute-start
  63.4 0.5 collective-permute-start.1
  63.9 2.4 %collective-permute-start.2 = (f32[64,1024]{1,0:T(8,128)}, f32[64,1024]{1,0:T(8,128)S(1)}, u32[]{:S(2)}, u32[]{:S(2)}) collective-permute-start(f32[64,1024]{1,0:T(8,128)} %get-tuple-element.32), channel_id=1, source_target_pairs={{0,6},{1,7},{2,4},{3,5},{4,2},{5,3},{6,0},{7,1}} | collective-permute-start | bytes 786440 | tf_op jit(solution)/shard_map/ppermute | solution.py:418
  66.3 0.0 copy-start
  66.3 0.0 copy-start.1
  66.3 17.0 %weight_grads.1 = (f32[4,1024,512]{2,1,0:T(8,128)}, f32[4,1024,512]{2,1,0:T(8,128)}, f32[4,512,1024]{2,1,0:T(8,128)}, f32[4,1024,512]{2,1,0:T(8,128)}, f32[4,1024,512]{2,1,0:T(8,128)}, /*index=5*/f32[4,512,1024]{2,1,0:T(8,128)}) custom-call(bf16[4,192,1024]{2,1,0:T(8,128)(2,1)S(1)} %get-tuple-element.33.refs_0_, ...), custom_call_target="tpu_custom_call" | custom-call | flops 4831838208 | bytes 50331648 | tf_op jit(solution)/shard_map/weight_grads/pallas_call | solution.py:381
  83.3 0.0 collective-permute-done
  83.3 0.0 collective-permute-done.1
  83.3 0.0 collective-permute-done.2
  83.3 0.0 copy-done
  83.3 0.0 copy-done.1
  83.4 0.7 add_convert_fusion
  (4 shorter events, 0.0 us)
Async XLA Ops:
  62.8 20.5 %collective-permute-start = (f32[64,1024]{1,0:T(8,128)}, f32[64,1024]{1,0:T(8,128)S(1)}, u32[]{:S(2)}, u32[]{:S(2)}) collective-permute-start(f32[64,1024]{1,0:T(8,128)} %get-tuple-element.30), channel_id=1, source_target_pairs={{0,2},{1,3},{2,0},{3,1},{4,6},{5,7},{6,4},{7,5}} | collective-permute-start | bytes 786440 | tf_op jit(solution)/shard_map/ppermute | solution.py:418
  63.4 19.9 %collective-permute-start.1 = (f32[64,1024]{1,0:T(8,128)}, f32[64,1024]{1,0:T(8,128)S(1)}, u32[]{:S(2)}, u32[]{:S(2)}) collective-permute-start(f32[64,1024]{1,0:T(8,128)} %get-tuple-element.31), channel_id=1, source_target_pairs={{0,4},{1,5},{2,6},{3,7},{4,0},{5,1},{6,2},{7,3}} | collective-permute-start | bytes 786440 | tf_op jit(solution)/shard_map/ppermute | solution.py:418
  63.9 19.4 %collective-permute-start.2 = (f32[64,1024]{1,0:T(8,128)}, f32[64,1024]{1,0:T(8,128)S(1)}, u32[]{:S(2)}, u32[]{:S(2)}) collective-permute-start(f32[64,1024]{1,0:T(8,128)} %get-tuple-element.32), channel_id=1, source_target_pairs={{0,6},{1,7},{2,4},{3,5},{4,2},{5,3},{6,0},{7,1}} | collective-permute-start | bytes 786440 | tf_op jit(solution)/shard_map/ppermute | solution.py:418
  66.3 17.0 %copy-start = (f32[64,1024]{1,0:T(8,128)S(1)}, f32[64,1024]{1,0:T(8,128)}, u32[]{:S(2)}) copy-start(f32[64,1024]{1,0:T(8,128)} %get-tuple-element.29) | copy-start | bytes 786436
  66.3 17.0 %copy-start.1 = (bf16[64,1024]{1,0:T(8,128)(2,1)S(1)}, bf16[64,1024]{1,0:T(8,128)(2,1)}, u32[]{:S(2)}) copy-start(bf16[64,1024]{1,0:T(8,128)(2,1)} %get-tuple-element.28) | copy-start | bytes 393220

commit v4 on v3

v4 whole, which is shorter than its diff:
```python
import functools
import jax
import jax.numpy as jnp
from jax import lax
from jax.experimental import pallas as pl
from jax.experimental.pallas import tpu as pltpu
from jax.sharding import PartitionSpec as P

MESH = pl.DeviceIdType.MESH
scope = jax.named_scope
F32 = jnp.float32
BF16 = jnp.bfloat16

TOK = 64
CHIPS = 4
DEVS = 8
D = 1024
F = 512
E = 4
CAP = 24
PAIR = 2 * CAP
ROWS = CHIPS * PAIR
PROWS = E * PAIR
CH = 4
CW = D // CH
MAIN_VMEM = 48_000_000
WGRAD_VMEM = 40_000_000

S_ROUTE, S_Y, S_DY, S_X, S_D1 = 0, 1, 2, 3, 4
N_STREAMS = S_D1 + CH

SETS = 2
HALVES = 2


def nt_dot(a, b):
    return lax.dot_general(a, b, (((1,), (1,)), ((), ())), preferred_element_type=F32)


def tn_dot(a, b):
    return lax.dot_general(a, b, (((0,), (0,)), ((), ())), preferred_element_type=F32)


def nn_dot(a, b):
    return jnp.dot(a, b, preferred_element_type=F32)


def main_kernel(
    experts_b, gates_b, slots_b, experts_a, gates_a, slots_a,
    x_hbm, y_hbm, dy_hbm, w1b_hbm, w3b_hbm, w2b_hbm, w1a_hbm, w3a_hbm, w2a_hbm,
    own_hbm, d1_hbm, far0_hbm, far1_hbm, far2_hbm,
    xr_two, zr_two, hid_two, da_two, db_two, xr_one, zr_one, hid_one, da_one, db_one,
    w_vm, choice_i, choice_f, route_own, route_g, y_g, dy_g, x_g, d1_g, d1_own,
    act_s, act_f, dh_sum, dxp, perm, perm_t, gate,
    part, mate_recv, near_recv, last_recv,
    in_sem, w_sem, ag_send, ag_recv, rs_send, rs_recv, out_sem,
):
    xr, zr, hid = (xr_two, xr_one), (zr_two, zr_one), (hid_two, hid_one)
    da, db = (da_two, da_one), (db_two, db_one)
    me = lax.axis_index("expert")
    core = lax.rem(me, 2)
    xpos = lax.rem(me // 2, 2)
    ypos = me // 4
    mate = me + 1 - 2 * core
    nx = me + 2 - 4 * xpos
    ny = me + 4 - 8 * ypos
    nd = ny + 2 - 4 * xpos
    na = nx + core * (ny - nx)
    nb = ny + core * (nx - ny)

    def remote(src, dst, send, recv, dev):
        return pltpu.make_async_remote_copy(src_ref=src, dst_ref=dst, send_sem=send, recv_sem=recv, device_id={"expert": dev}, device_id_type=MESH)

    barrier = pltpu.get_barrier_semaphore()
    for dev in (mate, nx, ny, nd):
        pl.semaphore_signal(barrier, inc=1, device_id={"expert": dev}, device_id_type=MESH)

    choices = [
        pltpu.make_async_copy(src, dst, in_sem.at[i])
        for i, (src, dst) in enumerate((
            (experts_b, choice_i.at[0]), (slots_b, choice_i.at[1]), (gates_b, choice_f.at[0]),
            (experts_a, choice_i.at[2]), (slots_a, choice_i.at[3]), (gates_a, choice_f.at[1]),
        ))
    ]
    tiles = [
        pltpu.make_async_copy(src, dst.at[me], in_sem.at[6 + i])
        for i, (src, dst) in enumerate(((y_hbm, y_g), (dy_hbm, dy_g), (x_hbm, x_g)))
    ]
    w_hbm = (w1b_hbm, w3b_hbm, w2b_hbm, w1a_hbm, w3a_hbm, w2a_hbm)

    def w_copy(i):
        return pltpu.make_async_copy(w_hbm[i], w_vm[i], w_sem.at[i])

    for c in choices + tiles:
        c.start()

    for c in choices:
        c.wait()
    for layer in range(2):
        lanes = slice(layer * TOK, (layer + 1) * TOK)
        slot = choice_i[2 * layer + 1]
        code = jnp.where(slot >= 0, choice_i[2 * layer] * PAIR + core * CAP + slot, -1).astype(F32)
        route_own[0:8, lanes] = code
        route_own[8:16, lanes] = choice_f[layer]
    route_g[me] = route_own[...]
    for c in tiles:
        c.wait()
    pl.semaphore_wait(barrier, 4)

    sends = []

    def send(c):
        c.start()
        sends.append(c)

    far = ((0, na), (1, nb), (3, nd))

    def ag_copy(stream, k, src, dst, dev):
        return remote(src, dst, ag_send.at[stream, k], ag_recv.at[stream, k], dev)

    def ag_start(stream, src, buf):
        for k, dev in far + ((2, mate),):
            send(ag_copy(stream, k, src, buf.at[me], dev))

    def ag_got(stream, k, buf, dev):
        ag_copy(stream, k, buf.at[dev], buf.at[dev], mate).wait_recv()

    def ag_pass_on(stream, buf):
        for i, (k, dev) in enumerate(far):
            ag_got(stream, k, buf, dev)
            send(ag_copy(stream, 4 + i, buf.at[dev], buf.at[dev], mate))

    def ag_finish(stream, buf):
        flip = 1 - 2 * core
        for k, dev in ((2, mate), (4, nb + flip), (5, na + flip), (6, nd + flip)):
            ag_got(stream, k, buf, dev)

    outs = []

    def out_start(src, dst):
        c = pltpu.make_async_copy(src, dst, out_sem.at[len(outs)])
        c.start()
        outs.append(c)

    def build_routes(layer):
        base = (me * PROWS).astype(F32)
        row_id = lax.broadcasted_iota(jnp.int32, (PROWS, 2 * TOK), 0).astype(F32)
        lane = lax.broadcasted_iota(jnp.int32, (16, 2 * TOK), 1)
        for p in range(CHIPS):
            halves = [route_g[2 * p], route_g[2 * p + 1]]
            halves[1 - layer] = pltpu.roll(halves[1 - layer], TOK, 1)
            both = jnp.where(lane < TOK, halves[0], halves[1])
            target = both[0:8] - base
            gates = both[8:16]
            hit = jnp.zeros((PROWS, 2 * TOK), F32)
            gsum = jnp.zeros((PROWS, 2 * TOK), F32)
            for j in range(8):
                m = row_id == target[j : j + 1, :]
                hit = jnp.where(m, 1.0, hit)
                gsum = jnp.where(m, gates[j : j + 1, :], gsum)
            perm[p] = hit.astype(BF16)
            perm_t[p] = hit.T.astype(BF16)
            gate[p] = jnp.sum(gsum, axis=1, keepdims=True)

    def gather_rows(tokens, dst, layer, cols, gated):
        for p in range(CHIPS):
            got = nn_dot(perm[p], tokens(p))
            if gated:
                got = got * gate[p]
            got = got.astype(BF16)
            for e in range(E):
                dst[layer][e, p * PAIR : (p + 1) * PAIR, cols] = got[e * PAIR : (e + 1) * PAIR]

    def forward_expert(layer, e):
        w1, w3 = w_vm[3 * layer], w_vm[3 * layer + 1]
        rows = xr[layer][e]
        a = nn_dot(rows, w1[e]).astype(BF16).astype(F32)
        b = nn_dot(rows, w3[e]).astype(BF16).astype(F32)
        sig = jax.nn.sigmoid(a)
        s = a * sig
        act_s[e] = s
        act_f[e] = b * (sig * (1.0 + a * (1.0 - sig)))
        hid[layer][e] = (s * b).astype(BF16)

    def hidden_expert(layer, e, dh):
        da[layer][e] = (dh * act_f[e]).astype(BF16)
        db[layer][e] = (dh * act_s[e]).astype(BF16)

    def row_chunk(layer, k):
        w1, w3 = w_vm[3 * layer], w_vm[3 * layer + 1]
        cols = slice(k * CW, (k + 1) * CW)
        for e in range(E):
            g = nt_dot(da[layer][e], w1[e, cols, :]) + nt_dot(db[layer][e], w3[e, cols, :])
            g = g.astype(BF16)
            for p in range(CHIPS):
                dxp[k % 2, p, e] = g[p * PAIR : (p + 1) * PAIR]
        for p in range(CHIPS):
            r = nn_dot(perm_t[p], dxp[k % 2, p].reshape(PROWS, CW))
            part[layer, k, 0, p] = r[:TOK]
            part[layer, k, 1, p] = r[TOK:]
        send(mate_copy(layer, k))

    def rs_copy(layer, k, i, src, dst, dev):
        return remote(src, dst, rs_send.at[layer, k, i], rs_recv.at[layer, k, i], dev)

    def mate_copy(layer, k):
        return rs_copy(layer, k, 0, part.at[layer, k, 1 - core], mate_recv.at[layer, k], mate)

    def near_copy(k, i):
        return rs_copy(0, k, 1 + i, part.at[0, k, core, (nd, na)[i] // 2], near_recv.at[k, i], na)

    def last_copy(k):
        return rs_copy(0, k, 3, part.at[0, k, core, nb // 2], last_recv.at[k], nb)

    def mate_sum(layer, k):
        mate_copy(layer, k).wait_recv()
        for p in range(CHIPS):
            part[layer, k, core, p] = part[layer, k, core, p] + mate_recv[layer, k, p]

    def near_start(k):
        mate_sum(0, k)
        send(near_copy(k, 0))
        send(near_copy(k, 1))

    def last_start(k):
        near_copy(k, 0).wait_recv()
        part[0, k, core, nb // 2] = part[0, k, core, nb // 2] + near_recv[k, 0]
        send(last_copy(k))

    def sums_out(k):
        mate_sum(1, k)
        cols = pl.ds(k * CW, CW)
        for dev, out in ((me, own_hbm), (nx, far0_hbm), (ny, far1_hbm), (nd, far2_hbm)):
            out_start(part.at[1, k, core, dev // 2], out.at[:, cols])

    def pair_of(buf, p):
        return buf[2 * p : 2 * p + 2].reshape(2 * TOK, buf.shape[-1])

    with scope("start"):
        ag_start(S_ROUTE, route_own, route_g)
        ag_start(S_Y, y_g.at[me], y_g)
        ag_start(S_DY, dy_g.at[me], dy_g)
        for i in range(6):
            w_copy(i).start()

    with scope("route"):
        ag_pass_on(S_ROUTE, route_g)
        ag_finish(S_ROUTE, route_g)
    with scope("build_two"):
        build_routes(0)
    with scope("wait_y"):
        ag_pass_on(S_Y, y_g)
        ag_finish(S_Y, y_g)
    with scope("rows_y"):
        gather_rows(lambda p: pair_of(y_g, p), xr, 0, slice(None), False)
    with scope("forward_two"):
        w_copy(0).wait()
        w_copy(1).wait()
        for e in range(E):
            forward_expert(0, e)
    with scope("wait_dy"):
        ag_start(S_X, x_g.at[me], x_g)
        ag_pass_on(S_DY, dy_g)
        ag_finish(S_DY, dy_g)
    with scope("rows_dy"):
        gather_rows(lambda p: pair_of(dy_g, p), zr, 0, slice(None), True)
    with scope("hidden_two"):
        w_copy(2).wait()
        for e in range(E):
            hidden_expert(0, e, nt_dot(zr[0][e], w_vm[2][e]))
    for k in range(CH):
        with scope(f"chunk_two_{k}"):
            row_chunk(0, k)
        if k >= 1:
            with scope(f"near_{k - 1}"):
                near_start(k - 1)
    with scope(f"near_{CH - 1}"):
        near_start(CH - 1)
    with scope("last_0"):
        last_start(0)

    with scope("wait_x"):
        ag_pass_on(S_X, x_g)
    with scope("build_one"):
        build_routes(1)
    with scope("last_1"):
        last_start(1)
    with scope("rows_x"):
        ag_finish(S_X, x_g)
        gather_rows(lambda p: pair_of(x_g, p), xr, 1, slice(None), False)
    with scope("last_2"):
        last_start(2)
    with scope("forward_one_0"):
        for i in range(3, 6):
            w_copy(i).wait()
        forward_expert(1, 0)
    with scope("last_3"):
        last_start(3)

    def mid_grad(k):
        cols = slice(k * CW, (k + 1) * CW)
        near_copy(k, 1).wait_recv()
        last_copy(k).wait_recv()
        total = part[0, k, core, me // 2] + near_recv[k, 1] + last_recv[k]
        mine = (dy_g[me, :, cols].astype(F32) + total).astype(BF16)
        d1_own[k] = mine
        d1_g[k, me] = mine
        out_start(d1_own.at[k], d1_hbm.at[:, pl.ds(k * CW, CW)])
        ag_start(S_D1 + k, d1_own.at[k], d1_g.at[k])

    def mid_rows(k):
        cols = slice(k * CW, (k + 1) * CW)
        gather_rows(lambda p: pair_of(d1_g.at[k], p), zr, 1, cols, True)

    def hidden_part(k):
        cols = slice(k * CW, (k + 1) * CW)
        for e in range(E):
            dh = nt_dot(zr[1][e, :, cols], w_vm[5][e, :, cols])
            if k > 0:
                dh = dh_sum[e] + dh
            if k < CH - 1:
                dh_sum[e] = dh
            else:
                hidden_expert(1, e, dh)

    for k in range(CH):
        with scope(f"mid_{k}"):
            mid_grad(k)
    for k in range(1, E):
        with scope(f"forward_one_{k}"):
            forward_expert(1, k)
    with scope("pass_on_0"):
        ag_pass_on(S_D1, d1_g.at[0])
    for k in range(CH):
        if k + 1 < CH:
            with scope(f"pass_on_{k + 1}"):
                ag_pass_on(S_D1 + k + 1, d1_g.at[k + 1])
        with scope(f"finish_{k}"):
            ag_finish(S_D1 + k, d1_g.at[k])
        with scope(f"rows_d1_{k}"):
            mid_rows(k)
            hidden_part(k)
    for k in range(CH):
        with scope(f"chunk_one_{k}"):
            row_chunk(1, k)
        if k >= 1:
            with scope(f"mate_one_{k - 1}"):
                sums_out(k - 1)
    with scope("mate_one_last"):
        sums_out(CH - 1)
    with scope("drain"):
        for c in sends:
            c.wait_send()
        for c in outs:
            c.wait()


def main_call(routing, x, y, dy, weights_two, weights_one):
    vm = pl.BlockSpec(memory_space=pltpu.VMEM)
    hbm = pl.BlockSpec(memory_space=pl.ANY)
    rows_d = pltpu.VMEM((E, ROWS, D), BF16)
    rows_f = pltpu.VMEM((E, ROWS, F), BF16)
    sums = jax.ShapeDtypeStruct((TOK, D), F32)
    saved = (rows_d, rows_d, rows_f, rows_f, rows_f)
    w_up = pltpu.VMEM((E, D, F), BF16)
    w_dn = pltpu.VMEM((E, F, D), BF16)
    dma = pltpu.SemaphoreType.DMA
    return pl.pallas_call(
        main_kernel,
        out_shape=(sums, jax.ShapeDtypeStruct((TOK, D), BF16), sums, sums, sums) + saved + saved,
        in_specs=[hbm] * 15,
        out_specs=(hbm,) * 5 + (vm,) * 10,
        scratch_shapes=[
            (w_up, w_up, w_dn, w_up, w_up, w_dn),
            pltpu.VMEM((4, 8, TOK), jnp.int32),
            pltpu.VMEM((2, 8, TOK), F32),
            pltpu.VMEM((16, 2 * TOK), F32),
            pltpu.VMEM((DEVS, 16, 2 * TOK), F32),
            pltpu.VMEM((DEVS, TOK, D), BF16),
            pltpu.VMEM((DEVS, TOK, D), BF16),
            pltpu.VMEM((DEVS, TOK, D), BF16),
            pltpu.VMEM((CH, DEVS, TOK, CW), BF16),
            pltpu.VMEM((CH, TOK, CW), BF16),
            pltpu.VMEM((E, ROWS, F), F32),
            pltpu.VMEM((E, ROWS, F), F32),
            pltpu.VMEM((E, ROWS, F), F32),
            pltpu.VMEM((2, CHIPS, E, PAIR, CW), BF16),
            pltpu.VMEM((CHIPS, PROWS, 2 * TOK), BF16),
            pltpu.VMEM((CHIPS, 2 * TOK, PROWS), BF16),
            pltpu.VMEM((CHIPS, PROWS, 1), F32),
            pltpu.VMEM((2, CH, 2, CHIPS, TOK, CW), F32),
            pltpu.VMEM((2, CH, CHIPS, TOK, CW), F32),
            pltpu.VMEM((CH, 2, TOK, CW), F32),
            pltpu.VMEM((CH, TOK, CW), F32),
            dma((9,)),
            dma((6,)),
            dma((N_STREAMS, 7)),
            dma((N_STREAMS, 7)),
            dma((2, CH, 4)),
            dma((2, CH, 4)),
            dma((5 * CH,)),
        ],
        compiler_params=pltpu.CompilerParams(collective_id=0, has_side_effects=True, vmem_limit_bytes=MAIN_VMEM),
        name="moe_backward",
    )(*routing, x, y, dy, *weights_two, *weights_one)


def wgrad_kernel(*refs):
    saved, outs, bufs, out_sem = (refs[0:5], refs[5:10]), (refs[10:13], refs[13:16]), refs[16:19], refs[19]

    def out_copy(layer, m, e, slot, h):
        n = bufs[m].shape[1] // HALVES
        rows = pl.ds(h * n, n)
        return pltpu.make_async_copy(bufs[m].at[slot, rows], outs[layer][m].at[e, rows], out_sem.at[slot, m, h])

    for layer in range(2):
        xr, zr, hid, da, db = saved[layer]

        @pl.loop(0, E)
        def _(e):
            i = layer * E + e
            slot = lax.rem(i, SETS)
            for m, lhs, rhs in ((2, hid, zr), (0, xr, da), (1, xr, db)):
                n = bufs[m].shape[1] // HALVES
                for h in range(HALVES):
                    rows = slice(h * n, (h + 1) * n)

                    @pl.when(i >= SETS)
                    def _():
                        out_copy(layer, m, e, slot, h).wait()

                    bufs[m][slot, rows] = tn_dot(lhs[e, :, rows], rhs[e])
                    out_copy(layer, m, e, slot, h).start()

    for i in range(2 * E - SETS, 2 * E):
        for m in (2, 0, 1):
            for h in range(HALVES):
                out_copy(i // E, m, i % E, i % SETS, h).wait()


def wgrad_call(*saved):
    up = jax.ShapeDtypeStruct((E, D, F), F32)
    dn = jax.ShapeDtypeStruct((E, F, D), F32)
    hbm = pl.BlockSpec(memory_space=pl.ANY)
    return pl.pallas_call(
        wgrad_kernel,
        out_shape=(up, up, dn) * 2,
        in_specs=[pl.BlockSpec(memory_space=pltpu.VMEM)] * 10,
        out_specs=(hbm,) * 6,
        scratch_shapes=[
            pltpu.VMEM((SETS, D, F), F32),
            pltpu.VMEM((SETS, D, F), F32),
            pltpu.VMEM((SETS, F, D), F32),
            pltpu.SemaphoreType.DMA((SETS, 3, HALVES)),
        ],
        compiler_params=pltpu.CompilerParams(vmem_limit_bytes=WGRAD_VMEM),
        cost_estimate=pl.CostEstimate(flops=12 * E * ROWS * D * F, bytes_accessed=24 * E * D * F, transcendentals=0),
        name="weight_grads",
    )(*saved)


def solution(mesh):
    tok_spec = P(("data", "expert"), None)
    weight_spec = P("expert", None, None)
    grad_spec = P(("data", "expert"), None, None)

    def local_step(x_tokens, y_mid, dy_out, experts_one, gates_one, slots_one, experts_two, gates_two, slots_two, w_gate_one, w_up_one, w_down_one, w_gate_two, w_up_two, w_down_two):
        routing = [a.T for a in (experts_two, gates_two, slots_two, experts_one, gates_one, slots_one)]
        got = main_call(routing, x_tokens, y_mid, dy_out, (w_gate_two, w_up_two, w_down_two), (w_gate_one, w_up_one, w_down_one))
        own, d1 = got[0:2]
        far = [lax.ppermute(got[2 + i], "expert", [(d, d ^ flip) for d in range(DEVS)]) for i, flip in enumerate((2, 4, 6))]
        grads = wgrad_call(*got[5:15])
        dx = (d1.astype(F32) + (own + (far[0] + far[1] + far[2]))).astype(BF16)
        return (dx,) + tuple(grads[3:6]) + tuple(grads[0:3])

    return jax.shard_map(local_step, mesh=mesh, in_specs=(tok_spec,) * 9 + (weight_spec,) * 6, out_specs=(tok_spec,) + (grad_spec,) * 6, check_vma=False)
```

time: 84.3 us -> 73.4 us (0.87)
  Pallas kernels: 76.9 us -> 68.4 us
  other arithmetic: 2.95 us -> 0.73 us
    pallas_call x1, Pallas kernels: 59.9 us -> 51.4 us  [main_call(): pl.pallas_call(main_kernel, out_shape=(sums, jax.ShapeDtypeStruct((TOK, D...]
  transfers between devices with their start and end apart: 3 -> 3, of which waited for: 0 -> 0; matrix products, arithmetic and copies ran while one was open for 0% -> 0% of each run, Pallas kernels for 20% -> 23%
where the time goes in v4:
time: 73.4 us; the launch traced here: 73.3 us
  Pallas kernels  68.4 us (93%)
  starting transfers between devices  3.51 us (5%)
    pallas_call x1, Pallas kernels, main_call(): pl.pallas_call(main_kernel, out_shape=(sums, jax.ShapeDtypeStruct((TOK, D...  51.4 us
    pallas_call x1, Pallas kernels, wgrad_call(): pl.pallas_call(wgrad_kernel, out_shape=(up, up, dn) * 2, in_specs=[pl.Blo...  17 us
    ppermute x3, starting transfers between devices, local_step(): lax.ppermute(got[2 + i], 'expert', [(d, d ^ flip) for d in range(DEVS)])  3.51 us
  transfers between devices with their start and end apart: 3, of which 0 were waited for; matrix products, arithmetic and copies ran while one was open for 0% of the time, Pallas kernels for 23%

profile of v4, /device:TPU:0, one launch (start us, length us, event | category | flops | bytes accessed | tf_op | source)
XLA Modules:
  0.0 73.3 jit_solution(3777045484863765323)
XLA Ops:
  0.6 51.4 %moe_backward.1 = (f32[64,1024]{1,0:T(8,128)}, bf16[64,1024]{1,0:T(8,128)(2,1)}, f32[64,1024]{1,0:T(8,128)}, f32[64,1024]{1,0:T(8,128)}, f32[64,1024]{1,0:T(8,12...) custom-call(s32[8,64]{1,0:T(8,128)} %bitcast.6, ...), custom_call_target="tpu_custom_call" | custom-call | tf_op jit(solution)/shard_map/moe_backward/pallas_call | solution.py:368
  52.0 1.0 %collective-permute-start = (f32[64,1024]{1,0:T(8,128)}, f32[64,1024]{1,0:T(8,128)S(1)}, u32[]{:S(2)}, u32[]{:S(2)}) collective-permute-start(f32[64,1024]{1,0:T(8,128)} %get-tuple-element.30), channel_id=1, source_target_pairs={{0,2},{1,3},{2,0},{3,1},{4,6},{5,7},{6,4},{7,5}} | collective-permute-start | bytes 786440 | tf_op jit(solution)/shard_map/ppermute | solution.py:471
  53.0 1.0 %collective-permute-start.1 = (f32[64,1024]{1,0:T(8,128)}, f32[64,1024]{1,0:T(8,128)S(1)}, u32[]{:S(2)}, u32[]{:S(2)}) collective-permute-start(f32[64,1024]{1,0:T(8,128)} %get-tuple-element.31), channel_id=1, source_target_pairs={{0,4},{1,5},{2,6},{3,7},{4,0},{5,1},{6,2},{7,3}} | collective-permute-start | bytes 786440 | tf_op jit(solution)/shard_map/ppermute | solution.py:471
  54.0 1.5 %collective-permute-start.2 = (f32[64,1024]{1,0:T(8,128)}, f32[64,1024]{1,0:T(8,128)S(1)}, u32[]{:S(2)}, u32[]{:S(2)}) collective-permute-start(f32[64,1024]{1,0:T(8,128)} %get-tuple-element.32), channel_id=1, source_target_pairs={{0,6},{1,7},{2,4},{3,5},{4,2},{5,3},{6,0},{7,1}} | collective-permute-start | bytes 786440 | tf_op jit(solution)/shard_map/ppermute | solution.py:471
  55.5 0.0 copy-start
  55.5 0.0 copy-start.1
  55.5 17.0 %weight_grads.1 = (f32[4,1024,512]{2,1,0:T(8,128)}, f32[4,1024,512]{2,1,0:T(8,128)}, f32[4,512,1024]{2,1,0:T(8,128)}, f32[4,1024,512]{2,1,0:T(8,128)}, f32[4,1024,512]{2,1,0:T(8,128)}, /*index=5*/f32[4,512,1024]{2,1,0:T(8,128)}) custom-call(bf16[4,192,1024]{2,1,0:T(8,128)(2,1)S(1)} %get-tuple-element.33.refs_0_, ...), custom_call_target="tpu_custom_call" | custom-call | flops 4831838208 | bytes 50331648 | tf_op jit(solution)/shard_map/weight_grads/pallas_call | solution.py:445
  72.5 0.0 collective-permute-done
  72.5 0.0 collective-permute-done.1
  72.6 0.0 collective-permute-done.2
  72.6 0.0 copy-done
  72.6 0.0 copy-done.1
  72.6 0.7 add_convert_fusion
Async XLA Ops:
  52.0 20.5 %collective-permute-start = (f32[64,1024]{1,0:T(8,128)}, f32[64,1024]{1,0:T(8,128)S(1)}, u32[]{:S(2)}, u32[]{:S(2)}) collective-permute-start(f32[64,1024]{1,0:T(8,128)} %get-tuple-element.30), channel_id=1, source_target_pairs={{0,2},{1,3},{2,0},{3,1},{4,6},{5,7},{6,4},{7,5}} | collective-permute-start | bytes 786440 | tf_op jit(solution)/shard_map/ppermute | solution.py:471
  53.0 19.5 %collective-permute-start.1 = (f32[64,1024]{1,0:T(8,128)}, f32[64,1024]{1,0:T(8,128)S(1)}, u32[]{:S(2)}, u32[]{:S(2)}) collective-permute-start(f32[64,1024]{1,0:T(8,128)} %get-tuple-element.31), channel_id=1, source_target_pairs={{0,4},{1,5},{2,6},{3,7},{4,0},{5,1},{6,2},{7,3}} | collective-permute-start | bytes 786440 | tf_op jit(solution)/shard_map/ppermute | solution.py:471
  54.0 18.6 %collective-permute-start.2 = (f32[64,1024]{1,0:T(8,128)}, f32[64,1024]{1,0:T(8,128)S(1)}, u32[]{:S(2)}, u32[]{:S(2)}) collective-permute-start(f32[64,1024]{1,0:T(8,128)} %get-tuple-element.32), channel_id=1, source_target_pairs={{0,6},{1,7},{2,4},{3,5},{4,2},{5,3},{6,0},{7,1}} | collective-permute-start | bytes 786440 | tf_op jit(solution)/shard_map/ppermute | solution.py:471
  55.5 17.0 %copy-start = (f32[64,1024]{1,0:T(8,128)S(1)}, f32[64,1024]{1,0:T(8,128)}, u32[]{:S(2)}) copy-start(f32[64,1024]{1,0:T(8,128)} %get-tuple-element.29) | copy-start | bytes 786436
  55.5 17.0 %copy-start.1 = (bf16[64,1024]{1,0:T(8,128)(2,1)S(1)}, bf16[64,1024]{1,0:T(8,128)(2,1)}, u32[]{:S(2)}) copy-start(bf16[64,1024]{1,0:T(8,128)(2,1)} %get-tuple-element.28) | copy-start | bytes 393220

commit v5 on v4

--- a/solution.py
+++ b/solution.py
@@ -30,7 +30,7 @@
 N_STREAMS = S_D1 + CH
 
 SETS = 2
-HALVES = 2
+HALVES = 1
 
 
 def nt_dot(a, b):
@@ -48,12 +48,12 @@
 def main_kernel(
     experts_b, gates_b, slots_b, experts_a, gates_a, slots_a,
     x_hbm, y_hbm, dy_hbm, w1b_hbm, w3b_hbm, w2b_hbm, w1a_hbm, w3a_hbm, w2a_hbm,
-    own_hbm, d1_hbm, far0_hbm, far1_hbm, far2_hbm,
+    own_ref, d1_ref, far0_ref, far1_ref, far2_ref,
     xr_two, zr_two, hid_two, da_two, db_two, xr_one, zr_one, hid_one, da_one, db_one,
-    w_vm, choice_i, choice_f, route_own, route_g, y_g, dy_g, x_g, d1_g, d1_own,
+    w_vm, choice_i, choice_f, route_own, route_g, y_g, dy_g, x_g, d1_g,
     act_s, act_f, dh_sum, dxp, perm, perm_t, gate,
     part, mate_recv, near_recv, last_recv,
-    in_sem, w_sem, ag_send, ag_recv, rs_send, rs_recv, out_sem,
+    choice_sem, tile_sem, w_sem, send_sem, ag_recv, mate_sem, near_sem, last_sem,
 ):
     xr, zr, hid = (xr_two, xr_one), (zr_two, zr_one), (hid_two, hid_one)
     da, db = (da_two, da_one), (db_two, db_one)
@@ -76,14 +76,14 @@
         pl.semaphore_signal(barrier, inc=1, device_id={"expert": dev}, device_id_type=MESH)
 
     choices = [
-        pltpu.make_async_copy(src, dst, in_sem.at[i])
-        for i, (src, dst) in enumerate((
-            (experts_b, choice_i.at[0]), (slots_b, choice_i.at[1]), (gates_b, choice_f.at[0]),
-            (experts_a, choice_i.at[2]), (slots_a, choice_i.at[3]), (gates_a, choice_f.at[1]),
-        ))
+        pltpu.make_async_copy(src, dst, choice_sem.at[i])
+        for i, src, dst in (
+            (0, experts_b, choice_i.at[0]), (0, slots_b, choice_i.at[1]), (1, gates_b, choice_f.at[0]),
+            (0, experts_a, choice_i.at[2]), (0, slots_a, choice_i.at[3]), (1, gates_a, choice_f.at[1]),
+        )
     ]
     tiles = [
-        pltpu.make_async_copy(src, dst.at[me], in_sem.at[6 + i])
+        pltpu.make_async_copy(src, dst.at[me], tile_sem.at[i])
         for i, (src, dst) in enumerate(((y_hbm, y_g), (dy_hbm, dy_g), (x_hbm, x_g)))
     ]
     w_hbm = (w1b_hbm, w3b_hbm, w2b_hbm, w1a_hbm, w3a_hbm, w2a_hbm)
@@ -94,8 +94,8 @@
     for c in choices + tiles:
         c.start()
 
-    for c in choices:
-        c.wait()
+    for i, whole in enumerate((choice_i, choice_f)):
+        pltpu.make_async_copy(whole, whole, choice_sem.at[i]).wait()
     for layer in range(2):
         lanes = slice(layer * TOK, (layer + 1) * TOK)
         slot = choice_i[2 * layer + 1]
@@ -107,40 +107,25 @@
         c.wait()
     pl.semaphore_wait(barrier, 4)
 
-    sends = []
-
-    def send(c):
-        c.start()
-        sends.append(c)
-
     far = ((0, na), (1, nb), (3, nd))
 
-    def ag_copy(stream, k, src, dst, dev):
-        return remote(src, dst, ag_send.at[stream, k], ag_recv.at[stream, k], dev)
+    def ag_send(stream, k, src, dst, dev):
+        remote(src, dst, send_sem.at[min(stream, S_D1)], ag_recv.at[stream, k], dev).start()
 
     def ag_start(stream, src, buf):
         for k, dev in far + ((2, mate),):
-            send(ag_copy(stream, k, src, buf.at[me], dev))
-
-    def ag_got(stream, k, buf, dev):
-        ag_copy(stream, k, buf.at[dev], buf.at[dev], mate).wait_recv()
+            ag_send(stream, k, src, buf.at[me], dev)
+
+    def ag_got(stream, k, buf):
+        remote(buf, buf, send_sem.at[min(stream, S_D1)], ag_recv.at[stream, k], mate).wait_recv()
 
     def ag_pass_on(stream, buf):
-        for i, (k, dev) in enumerate(far):
-            ag_got(stream, k, buf, dev)
-            send(ag_copy(stream, 4 + i, buf.at[dev], buf.at[dev], mate))
+        for k, dev in far:
+            ag_got(stream, k, buf.at[dev])
+            ag_send(stream, 2, buf.at[dev], buf.at[dev], mate)
 
     def ag_finish(stream, buf):
-        flip = 1 - 2 * core
-        for k, dev in ((2, mate), (4, nb + flip), (5, na + flip), (6, nd + flip)):
-            ag_got(stream, k, buf, dev)
-
-    outs = []
-
-    def out_start(src, dst):
-        c = pltpu.make_async_copy(src, dst, out_sem.at[len(outs)])
-        c.start()
-        outs.append(c)
+        ag_got(stream, 2, buf.at[pl.ds(0, CHIPS)])
 
     def build_routes(layer):
         base = (me * PROWS).astype(F32)
@@ -198,40 +183,34 @@
             r = nn_dot(perm_t[p], dxp[k % 2, p].reshape(PROWS, CW))
             part[layer, k, 0, p] = r[:TOK]
             part[layer, k, 1, p] = r[TOK:]
-        send(mate_copy(layer, k))
-
-    def rs_copy(layer, k, i, src, dst, dev):
-        return remote(src, dst, rs_send.at[layer, k, i], rs_recv.at[layer, k, i], dev)
+        mate_copy(layer, k).start()
 
     def mate_copy(layer, k):
-        return rs_copy(layer, k, 0, part.at[layer, k, 1 - core], mate_recv.at[layer, k], mate)
+        return remote(part.at[layer, k, 1 - core], mate_recv.at[layer, k], send_sem.at[S_D1 + 1], mate_sem.at[layer, k], mate)
 
     def near_copy(k, i):
-        return rs_copy(0, k, 1 + i, part.at[0, k, core, (nd, na)[i] // 2], near_recv.at[k, i], na)
+        return remote(part.at[0, k, core, (nd, na)[i] // 2], near_recv.at[k, i], send_sem.at[S_D1 + 2], near_sem.at[k, i], na)
 
     def last_copy(k):
-        return rs_copy(0, k, 3, part.at[0, k, core, nb // 2], last_recv.at[k], nb)
-
-    def mate_sum(layer, k):
-        mate_copy(layer, k).wait_recv()
+        return remote(part.at[0, k, core, nb // 2], last_recv.at[k], send_sem.at[S_D1 + 3], last_sem.at[k], nb)
+
+    def near_start(k):
+        mate_copy(0, k).wait_recv()
         for p in range(CHIPS):
-            part[layer, k, core, p] = part[layer, k, core, p] + mate_recv[layer, k, p]
-
-    def near_start(k):
-        mate_sum(0, k)
-        send(near_copy(k, 0))
-        send(near_copy(k, 1))
+            part[0, k, core, p] = part[0, k, core, p] + mate_recv[0, k, p]
+        near_copy(k, 0).start()
+        near_copy(k, 1).start()
 
     def last_start(k):
         near_copy(k, 0).wait_recv()
         part[0, k, core, nb // 2] = part[0, k, core, nb // 2] + near_recv[k, 0]
-        send(last_copy(k))
+        last_copy(k).start()
 
     def sums_out(k):
-        mate_sum(1, k)
-        cols = pl.ds(k * CW, CW)
-        for dev, out in ((me, own_hbm), (nx, far0_hbm), (ny, far1_hbm), (nd, far2_hbm)):
-            out_start(part.at[1, k, core, dev // 2], out.at[:, cols])
+        mate_copy(1, k).wait_recv()
+        cols = slice(k * CW, (k + 1) * CW)
+        for dev, out in ((me, own_ref), (nx, far0_ref), (ny, far1_ref), (nd, far2_ref)):
+            out[:, cols] = part[1, k, core, dev // 2] + mate_recv[1, k, dev // 2]
 
     def pair_of(buf, p):
         return buf[2 * p : 2 * p + 2].reshape(2 * TOK, buf.shape[-1])
@@ -303,10 +282,9 @@
         last_copy(k).wait_recv()
         total = part[0, k, core, me // 2] + near_recv[k, 1] + last_recv[k]
         mine = (dy_g[me, :, cols].astype(F32) + total).astype(BF16)
-        d1_own[k] = mine
+        d1_ref[:, cols] = mine
         d1_g[k, me] = mine
-        out_start(d1_own.at[k], d1_hbm.at[:, pl.ds(k * CW, CW)])
-        ag_start(S_D1 + k, d1_own.at[k], d1_g.at[k])
+        ag_start(S_D1 + k, d1_g.at[k, me], d1_g.at[k])
 
     def mid_rows(k):
         cols = slice(k * CW, (k + 1) * CW)
@@ -343,16 +321,21 @@
     for k in range(CH):
         with scope(f"chunk_one_{k}"):
             row_chunk(1, k)
-        if k >= 1:
-            with scope(f"mate_one_{k - 1}"):
-                sums_out(k - 1)
+        if k >= 2:
+            with scope(f"mate_one_{k - 2}"):
+                sums_out(k - 2)
+    with scope("mate_one_late"):
+        sums_out(CH - 2)
     with scope("mate_one_last"):
         sums_out(CH - 1)
     with scope("drain"):
-        for c in sends:
-            c.wait_send()
-        for c in outs:
-            c.wait()
+        seven = pl.ds(0, DEVS - 1)
+        sent = (
+            (S_ROUTE, route_g.at[seven]), (S_Y, y_g.at[seven]), (S_DY, dy_g.at[seven]), (S_X, x_g.at[seven]), (S_D1, d1_g.at[:, seven]),
+            (S_D1 + 1, mate_recv), (S_D1 + 2, near_recv), (S_D1 + 3, last_recv),
+        )
+        for i, whole in sent:
+            remote(whole, whole, send_sem.at[i], ag_recv.at[0, 0], mate).wait_send()
 
 
 def main_call(routing, x, y, dy, weights_two, weights_one):
@@ -360,16 +343,16 @@
     hbm = pl.BlockSpec(memory_space=pl.ANY)
     rows_d = pltpu.VMEM((E, ROWS, D), BF16)
     rows_f = pltpu.VMEM((E, ROWS, F), BF16)
-    sums = jax.ShapeDtypeStruct((TOK, D), F32)
+    sums = pltpu.VMEM((TOK, D), F32)
     saved = (rows_d, rows_d, rows_f, rows_f, rows_f)
     w_up = pltpu.VMEM((E, D, F), BF16)
     w_dn = pltpu.VMEM((E, F, D), BF16)
     dma = pltpu.SemaphoreType.DMA
     return pl.pallas_call(
         main_kernel,
-        out_shape=(sums, jax.ShapeDtypeStruct((TOK, D), BF16), sums, sums, sums) + saved + saved,
+        out_shape=(sums, pltpu.VMEM((TOK, D), BF16), sums, sums, sums) + saved + saved,
         in_specs=[hbm] * 15,
-        out_specs=(hbm,) * 5 + (vm,) * 10,
+        out_specs=(vm,) * 15,
         scratch_shapes=[
             (w_up, w_up, w_dn, w_up, w_up, w_dn),
             pltpu.VMEM((4, 8, TOK), jnp.int32),
@@ -380,7 +363,6 @@
             pltpu.VMEM((DEVS, TOK, D), BF16),
             pltpu.VMEM((DEVS, TOK, D), BF16),
             pltpu.VMEM((CH, DEVS, TOK, CW), BF16),
-            pltpu.VMEM((CH, TOK, CW), BF16),
             pltpu.VMEM((E, ROWS, F), F32),
             pltpu.VMEM((E, ROWS, F), F32),
             pltpu.VMEM((E, ROWS, F), F32),
@@ -392,13 +374,14 @@
             pltpu.VMEM((2, CH, CHIPS, TOK, CW), F32),
             pltpu.VMEM((CH, 2, TOK, CW), F32),
             pltpu.VMEM((CH, TOK, CW), F32),
-            dma((9,)),
+            dma((2,)),
+            dma((3,)),
             dma((6,)),
-            dma((N_STREAMS, 7)),
-            dma((N_STREAMS, 7)),
-            dma((2, CH, 4)),
-            dma((2, CH, 4)),
-            dma((5 * CH,)),
+            dma((S_D1 + 4,)),
+            dma((N_STREAMS, 4)),
+            dma((2, CH)),
+            dma((CH, 2)),
+            dma((CH,)),
         ],
         compiler_params=pltpu.CompilerParams(collective_id=0, has_side_effects=True, vmem_limit_bytes=MAIN_VMEM),
         name="moe_backward",

time: 73.4 us -> 70.5 us (0.960)
  Pallas kernels: 68.4 us -> 65.5 us
    pallas_call x1, Pallas kernels: 51.4 us -> 49 us  [main_call(): pl.pallas_call(main_kernel, out_shape=(sums, pltpu.VMEM((TOK, D), BF16),...]
where the time goes in v5:
time: 70.5 us; the launch traced here: 70.4 us
  Pallas kernels  65.5 us (93%)
  starting transfers between devices  3.51 us (5%)
  other arithmetic  0.76 us (1%)
    pallas_call x1, Pallas kernels, main_call(): pl.pallas_call(main_kernel, out_shape=(sums, pltpu.VMEM((TOK, D), BF16),...  49 us
    pallas_call x1, Pallas kernels, wgrad_call(): pl.pallas_call(wgrad_kernel, out_shape=(up, up, dn) * 2, in_specs=[pl.Blo...  16.5 us
    ppermute x3, starting transfers between devices, local_step(): lax.ppermute(got[2 + i], 'expert', [(d, d ^ flip) for d in range(DEVS)])  3.51 us
  transfers between devices with their start and end apart: 3, of which 0 were waited for; matrix products, arithmetic and copies ran while one was open for 0% of the time, Pallas kernels for 23%

profile of v5, /device:TPU:0, one launch (start us, length us, event | category | flops | bytes accessed | tf_op | source)
XLA Modules:
  0.0 70.4 jit_solution(17446696408326262497)
XLA Ops:
  0.6 49.0 %moe_backward.1 = (f32[64,1024]{1,0:T(8,128)S(1)}, bf16[64,1024]{1,0:T(8,128)(2,1)S(1)}, f32[64,1024]{1,0:T(8,128)S(1)}, f32[64,1024]{1,0:T(8,128)S(1)}, f32[64,...) custom-call(s32[8,64]{1,0:T(8,128)} %bitcast.6, ...), custom_call_target="tpu_custom_call" | custom-call | tf_op jit(solution)/shard_map/moe_backward/pallas_call | solution.py:351
  49.6 1.0 %collective-permute-start = (f32[64,1024]{1,0:T(8,128)S(1)}, f32[64,1024]{1,0:T(8,128)S(1)}, u32[]{:S(2)}, u32[]{:S(2)}) collective-permute-start(f32[64,1024]{1,0:T(8,128)S(1)} %get-tuple-element.30), channel_id=1, source_target_pairs={{0,2},{1,3},{2,0},{3,1},{4,6},{5,7},{6,4},{7,5}} | collective-permute-start | bytes 786440 | tf_op jit(solution)/shard_map/ppermute | solution.py:454
  50.6 1.0 %collective-permute-start.1 = (f32[64,1024]{1,0:T(8,128)S(1)}, f32[64,1024]{1,0:T(8,128)S(1)}, u32[]{:S(2)}, u32[]{:S(2)}) collective-permute-start(f32[64,1024]{1,0:T(8,128)S(1)} %get-tuple-element.31), channel_id=1, source_target_pairs={{0,4},{1,5},{2,6},{3,7},{4,0},{5,1},{6,2},{7,3}} | collective-permute-start | bytes 786440 | tf_op jit(solution)/shard_map/ppermute | solution.py:454
  51.6 1.6 %collective-permute-start.2 = (f32[64,1024]{1,0:T(8,128)S(1)}, f32[64,1024]{1,0:T(8,128)S(1)}, u32[]{:S(2)}, u32[]{:S(2)}) collective-permute-start(f32[64,1024]{1,0:T(8,128)S(1)} %get-tuple-element.32), channel_id=1, source_target_pairs={{0,6},{1,7},{2,4},{3,5},{4,2},{5,3},{6,0},{7,1}} | collective-permute-start | bytes 786440 | tf_op jit(solution)/shard_map/ppermute | solution.py:454
  53.1 16.5 %weight_grads.1 = (f32[4,1024,512]{2,1,0:T(8,128)}, f32[4,1024,512]{2,1,0:T(8,128)}, f32[4,512,1024]{2,1,0:T(8,128)}, f32[4,1024,512]{2,1,0:T(8,128)}, f32[4,1024,512]{2,1,0:T(8,128)}, /*index=5*/f32[4,512,1024]{2,1,0:T(8,128)}) custom-call(bf16[4,192,1024]{2,1,0:T(8,128)(2,1)S(1)} %get-tuple-element.33.refs_0_, ...), custom_call_target="tpu_custom_call" | custom-call | flops 4831838208 | bytes 50331648 | tf_op jit(solution)/shard_map/weight_grads/pallas_call | solution.py:428
  69.6 0.0 collective-permute-done
  69.6 0.0 collective-permute-done.1
  69.6 0.0 collective-permute-done.2
  69.7 0.8 %add_convert_fusion = bf16[64,1024]{1,0:T(8,128)(2,1)} fusion(f32[64,1024]{1,0:T(8,128)S(1)} %get-tuple-element.29, f32[64,1024]{1,0:T(8,128)S(1)} %collective-permute-done.2, f32[64,1024]{1,0:T(8,128)S(1)} %collective-permute-done, f32[64,1024]{1,0:T(8,128)S(1)} %collective-permute-done.1, bf16[64,1024]{1,0:T(8,128)(2,1)S(1)} %get-tuple-element.28), kind=kLoop, calls=%fused_computation | loop fusion | flops 393216 | bytes 1310720 | tf_op jit(solution)/shard_map/convert_element_type | solution.py:456
Async XLA Ops:
  49.6 20.0 %collective-permute-start = (f32[64,1024]{1,0:T(8,128)S(1)}, f32[64,1024]{1,0:T(8,128)S(1)}, u32[]{:S(2)}, u32[]{:S(2)}) collective-permute-start(f32[64,1024]{1,0:T(8,128)S(1)} %get-tuple-element.30), channel_id=1, source_target_pairs={{0,2},{1,3},{2,0},{3,1},{4,6},{5,7},{6,4},{7,5}} | collective-permute-start | bytes 786440 | tf_op jit(solution)/shard_map/ppermute | solution.py:454
  50.6 19.0 %collective-permute-start.1 = (f32[64,1024]{1,0:T(8,128)S(1)}, f32[64,1024]{1,0:T(8,128)S(1)}, u32[]{:S(2)}, u32[]{:S(2)}) collective-permute-start(f32[64,1024]{1,0:T(8,128)S(1)} %get-tuple-element.31), channel_id=1, source_target_pairs={{0,4},{1,5},{2,6},{3,7},{4,0},{5,1},{6,2},{7,3}} | collective-permute-start | bytes 786440 | tf_op jit(solution)/shard_map/ppermute | solution.py:454
  51.6 18.1 %collective-permute-start.2 = (f32[64,1024]{1,0:T(8,128)S(1)}, f32[64,1024]{1,0:T(8,128)S(1)}, u32[]{:S(2)}, u32[]{:S(2)}) collective-permute-start(f32[64,1024]{1,0:T(8,128)S(1)} %get-tuple-element.32), channel_id=1, source_target_pairs={{0,6},{1,7},{2,4},{3,5},{4,2},{5,3},{6,0},{7,1}} | collective-permute-start | bytes 786440 | tf_op jit(solution)/shard_map/ppermute | solution.py:454

commit v6 on v5

--- a/solution.py
+++ b/solution.py
@@ -127,6 +127,21 @@
     def ag_finish(stream, buf):
         ag_got(stream, 2, buf.at[pl.ds(0, CHIPS)])
 
+    def ring_start(stream, buf):
+        for k, dev in ((0, na), (1, nb), (2, mate)):
+            ag_send(stream, k, buf.at[me], buf.at[me], dev)
+
+    def ring_step(stream, buf):
+        ag_got(stream, 0, buf.at[na])
+        ag_send(stream, 3, buf.at[na], buf.at[na], nb)
+        ag_send(stream, 2, buf.at[na], buf.at[na], mate)
+        ag_got(stream, 1, buf.at[nb])
+        ag_send(stream, 2, buf.at[nb], buf.at[nb], mate)
+
+    def ring_last(stream, buf):
+        ag_got(stream, 3, buf.at[nd])
+        ag_send(stream, 2, buf.at[nd], buf.at[nd], mate)
+
     def build_routes(layer):
         base = (me * PROWS).astype(F32)
         row_id = lax.broadcasted_iota(jnp.int32, (PROWS, 2 * TOK), 0).astype(F32)
@@ -217,29 +232,37 @@
 
     with scope("start"):
         ag_start(S_ROUTE, route_own, route_g)
-        ag_start(S_Y, y_g.at[me], y_g)
-        ag_start(S_DY, dy_g.at[me], dy_g)
+        ring_start(S_Y, y_g)
+        ring_start(S_DY, dy_g)
         for i in range(6):
             w_copy(i).start()
 
     with scope("route"):
         ag_pass_on(S_ROUTE, route_g)
         ag_finish(S_ROUTE, route_g)
+    with scope("step_y"):
+        ring_step(S_Y, y_g)
     with scope("build_two"):
         build_routes(0)
+    with scope("step_dy"):
+        ring_step(S_DY, dy_g)
     with scope("wait_y"):
-        ag_pass_on(S_Y, y_g)
+        ring_last(S_Y, y_g)
         ag_finish(S_Y, y_g)
     with scope("rows_y"):
         gather_rows(lambda p: pair_of(y_g, p), xr, 0, slice(None), False)
-    with scope("forward_two"):
         w_copy(0).wait()
         w_copy(1).wait()
-        for e in range(E):
+    with scope("forward_two"):
+        for e in range(2):
+            forward_expert(0, e)
+    with scope("last_dy"):
+        ring_last(S_DY, dy_g)
+        ag_start(S_X, x_g.at[me], x_g)
+    with scope("forward_two_b"):
+        for e in range(2, E):
             forward_expert(0, e)
     with scope("wait_dy"):
-        ag_start(S_X, x_g.at[me], x_g)
-        ag_pass_on(S_DY, dy_g)
         ag_finish(S_DY, dy_g)
     with scope("rows_dy"):
         gather_rows(lambda p: pair_of(dy_g, p), zr, 0, slice(None), True)
@@ -301,23 +324,40 @@
             else:
                 hidden_expert(1, e, dh)
 
-    for k in range(CH):
+    def mid_step(k):
         with scope(f"mid_{k}"):
             mid_grad(k)
-    for k in range(1, E):
-        with scope(f"forward_one_{k}"):
-            forward_expert(1, k)
-    with scope("pass_on_0"):
-        ag_pass_on(S_D1, d1_g.at[0])
-    for k in range(CH):
-        if k + 1 < CH:
-            with scope(f"pass_on_{k + 1}"):
-                ag_pass_on(S_D1 + k + 1, d1_g.at[k + 1])
+
+    def pass_step(k):
+        with scope(f"pass_on_{k}"):
+            ag_pass_on(S_D1 + k, d1_g.at[k])
+
+    def rows_step(k):
         with scope(f"finish_{k}"):
             ag_finish(S_D1 + k, d1_g.at[k])
         with scope(f"rows_d1_{k}"):
             mid_rows(k)
             hidden_part(k)
+
+    def forward_step(k):
+        with scope(f"forward_one_{k}"):
+            forward_expert(1, k)
+
+    mid_step(0)
+    mid_step(1)
+    mid_step(2)
+    forward_step(1)
+    forward_step(2)
+    forward_step(3)
+    mid_step(3)
+    pass_step(0)
+    pass_step(1)
+    pass_step(2)
+    rows_step(0)
+    pass_step(3)
+    rows_step(1)
+    rows_step(2)
+    rows_step(3)
     for k in range(CH):
         with scope(f"chunk_one_{k}"):
             row_chunk(1, k)

time: 70.5 us -> 69 us (0.979)
  Pallas kernels: 65.5 us -> 64 us
    pallas_call x1, Pallas kernels: 49 us -> 47.5 us  [main_call(): pl.pallas_call(main_kernel, out_shape=(sums, pltpu.VMEM((TOK, D), BF16),...]
  transfers between devices with their start and end apart: 3 -> 3, of which waited for: 0 -> 0; matrix products, arithmetic and copies ran while one was open for 0% -> 0% of each run, Pallas kernels for 23% -> 24%
where the time goes in v6:
time: 69 us; the launch traced here: 68.9 us
  Pallas kernels  64 us (93%)
  starting transfers between devices  3.51 us (5%)
  other arithmetic  0.76 us (1%)
    pallas_call x1, Pallas kernels, main_call(): pl.pallas_call(main_kernel, out_shape=(sums, pltpu.VMEM((TOK, D), BF16),...  47.5 us
    pallas_call x1, Pallas kernels, wgrad_call(): pl.pallas_call(wgrad_kernel, out_shape=(up, up, dn) * 2, in_specs=[pl.Blo...  16.5 us
    ppermute x3, starting transfers between devices, local_step(): lax.ppermute(got[2 + i], 'expert', [(d, d ^ flip) for d in range(DEVS)])  3.51 us
  transfers between devices with their start and end apart: 3, of which 0 were waited for; matrix products, arithmetic and copies ran while one was open for 0% of the time, Pallas kernels for 24%

profile of v6, /device:TPU:0, one launch (start us, length us, event | category | flops | bytes accessed | tf_op | source)
XLA Modules:
  0.0 68.9 jit_solution(10110440790081109867)
XLA Ops:
  0.6 47.5 %moe_backward.1 = (f32[64,1024]{1,0:T(8,128)S(1)}, bf16[64,1024]{1,0:T(8,128)(2,1)S(1)}, f32[64,1024]{1,0:T(8,128)S(1)}, f32[64,1024]{1,0:T(8,128)S(1)}, f32[64,...) custom-call(s32[8,64]{1,0:T(8,128)} %bitcast.6, ...), custom_call_target="tpu_custom_call" | custom-call | tf_op jit(solution)/shard_map/moe_backward/pallas_call | solution.py:391
  48.1 1.0 %collective-permute-start = (f32[64,1024]{1,0:T(8,128)S(1)}, f32[64,1024]{1,0:T(8,128)S(1)}, u32[]{:S(2)}, u32[]{:S(2)}) collective-permute-start(f32[64,1024]{1,0:T(8,128)S(1)} %get-tuple-element.30), channel_id=1, source_target_pairs={{0,2},{1,3},{2,0},{3,1},{4,6},{5,7},{6,4},{7,5}} | collective-permute-start | bytes 786440 | tf_op jit(solution)/shard_map/ppermute | solution.py:494
  49.1 1.3 %collective-permute-start.1 = (f32[64,1024]{1,0:T(8,128)S(1)}, f32[64,1024]{1,0:T(8,128)S(1)}, u32[]{:S(2)}, u32[]{:S(2)}) collective-permute-start(f32[64,1024]{1,0:T(8,128)S(1)} %get-tuple-element.31), channel_id=1, source_target_pairs={{0,4},{1,5},{2,6},{3,7},{4,0},{5,1},{6,2},{7,3}} | collective-permute-start | bytes 786440 | tf_op jit(solution)/shard_map/ppermute | solution.py:494
  50.4 1.3 %collective-permute-start.2 = (f32[64,1024]{1,0:T(8,128)S(1)}, f32[64,1024]{1,0:T(8,128)S(1)}, u32[]{:S(2)}, u32[]{:S(2)}) collective-permute-start(f32[64,1024]{1,0:T(8,128)S(1)} %get-tuple-element.32), channel_id=1, source_target_pairs={{0,6},{1,7},{2,4},{3,5},{4,2},{5,3},{6,0},{7,1}} | collective-permute-start | bytes 786440 | tf_op jit(solution)/shard_map/ppermute | solution.py:494
  51.6 16.5 %weight_grads.1 = (f32[4,1024,512]{2,1,0:T(8,128)}, f32[4,1024,512]{2,1,0:T(8,128)}, f32[4,512,1024]{2,1,0:T(8,128)}, f32[4,1024,512]{2,1,0:T(8,128)}, f32[4,1024,512]{2,1,0:T(8,128)}, /*index=5*/f32[4,512,1024]{2,1,0:T(8,128)}) custom-call(bf16[4,192,1024]{2,1,0:T(8,128)(2,1)S(1)} %get-tuple-element.33.refs_0_, ...), custom_call_target="tpu_custom_call" | custom-call | flops 4831838208 | bytes 50331648 | tf_op jit(solution)/shard_map/weight_grads/pallas_call | solution.py:468
  68.1 0.0 collective-permute-done
  68.1 0.0 collective-permute-done.1
  68.1 0.0 collective-permute-done.2
  68.2 0.8 %add_convert_fusion = bf16[64,1024]{1,0:T(8,128)(2,1)} fusion(f32[64,1024]{1,0:T(8,128)S(1)} %get-tuple-element.29, f32[64,1024]{1,0:T(8,128)S(1)} %collective-permute-done.2, f32[64,1024]{1,0:T(8,128)S(1)} %collective-permute-done, f32[64,1024]{1,0:T(8,128)S(1)} %collective-permute-done.1, bf16[64,1024]{1,0:T(8,128)(2,1)S(1)} %get-tuple-element.28), kind=kLoop, calls=%fused_computation | loop fusion | flops 393216 | bytes 1310720 | tf_op jit(solution)/shard_map/convert_element_type | solution.py:496
Async XLA Ops:
  48.1 20.0 %collective-permute-start = (f32[64,1024]{1,0:T(8,128)S(1)}, f32[64,1024]{1,0:T(8,128)S(1)}, u32[]{:S(2)}, u32[]{:S(2)}) collective-permute-start(f32[64,1024]{1,0:T(8,128)S(1)} %get-tuple-element.30), channel_id=1, source_target_pairs={{0,2},{1,3},{2,0},{3,1},{4,6},{5,7},{6,4},{7,5}} | collective-permute-start | bytes 786440 | tf_op jit(solution)/shard_map/ppermute | solution.py:494
  49.1 19.0 %collective-permute-start.1 = (f32[64,1024]{1,0:T(8,128)S(1)}, f32[64,1024]{1,0:T(8,128)S(1)}, u32[]{:S(2)}, u32[]{:S(2)}) collective-permute-start(f32[64,1024]{1,0:T(8,128)S(1)} %get-tuple-element.31), channel_id=1, source_target_pairs={{0,4},{1,5},{2,6},{3,7},{4,0},{5,1},{6,2},{7,3}} | collective-permute-start | bytes 786440 | tf_op jit(solution)/shard_map/ppermute | solution.py:494
  50.4 17.8 %collective-permute-start.2 = (f32[64,1024]{1,0:T(8,128)S(1)}, f32[64,1024]{1,0:T(8,128)S(1)}, u32[]{:S(2)}, u32[]{:S(2)}) collective-permute-start(f32[64,1024]{1,0:T(8,128)S(1)} %get-tuple-element.32), channel_id=1, source_target_pairs={{0,6},{1,7},{2,4},{3,5},{4,2},{5,3},{6,0},{7,1}} | collective-permute-start | bytes 786440 | tf_op jit(solution)/shard_map/ppermute | solution.py:494

commit v7 on v6

--- a/solution.py
+++ b/solution.py
@@ -26,8 +26,9 @@
 MAIN_VMEM = 48_000_000
 WGRAD_VMEM = 40_000_000
 
-S_ROUTE, S_Y, S_DY, S_X, S_D1 = 0, 1, 2, 3, 4
+S_ROUTE, S_Y, S_DY, S_X, S_D1 = 0, 1, 3, 5, 6
 N_STREAMS = S_D1 + CH
+HW = D // 2
 
 SETS = 2
 HALVES = 1
@@ -84,7 +85,10 @@
     ]
     tiles = [
         pltpu.make_async_copy(src, dst.at[me], tile_sem.at[i])
-        for i, (src, dst) in enumerate(((y_hbm, y_g), (dy_hbm, dy_g), (x_hbm, x_g)))
+        for i, (src, dst) in enumerate((
+            (y_hbm.at[:, pl.ds(0, HW)], y_g.at[0]), (y_hbm.at[:, pl.ds(HW, HW)], y_g.at[1]),
+            (dy_hbm.at[:, pl.ds(0, HW)], dy_g.at[0]), (dy_hbm.at[:, pl.ds(HW, HW)], dy_g.at[1]), (x_hbm, x_g),
+        ))
     ]
     w_hbm = (w1b_hbm, w3b_hbm, w2b_hbm, w1a_hbm, w3a_hbm, w2a_hbm)
 
@@ -171,16 +175,28 @@
             for e in range(E):
                 dst[layer][e, p * PAIR : (p + 1) * PAIR, cols] = got[e * PAIR : (e + 1) * PAIR]
 
-    def forward_expert(layer, e):
-        w1, w3 = w_vm[3 * layer], w_vm[3 * layer + 1]
-        rows = xr[layer][e]
-        a = nn_dot(rows, w1[e]).astype(BF16).astype(F32)
-        b = nn_dot(rows, w3[e]).astype(BF16).astype(F32)
+    def activate(layer, e, a, b):
+        a = a.astype(BF16).astype(F32)
+        b = b.astype(BF16).astype(F32)
         sig = jax.nn.sigmoid(a)
         s = a * sig
         act_s[e] = s
         act_f[e] = b * (sig * (1.0 + a * (1.0 - sig)))
         hid[layer][e] = (s * b).astype(BF16)
+
+    def forward_expert(layer, e):
+        rows = xr[layer][e]
+        activate(layer, e, nn_dot(rows, w_vm[3 * layer][e]), nn_dot(rows, w_vm[3 * layer + 1][e]))
+
+    def forward_half(e, h):
+        cols = slice(h * HW, (h + 1) * HW)
+        a = nn_dot(xr[0][e, :, cols], w_vm[0][e, cols, :])
+        b = nn_dot(xr[0][e, :, cols], w_vm[1][e, cols, :])
+        if h == 0:
+            act_s[e] = a
+            act_f[e] = b
+        else:
+            activate(0, e, act_s[e] + a, act_f[e] + b)
 
     def hidden_expert(layer, e, dh):
         da[layer][e] = (dh * act_f[e]).astype(BF16)
@@ -232,44 +248,77 @@
 
     with scope("start"):
         ag_start(S_ROUTE, route_own, route_g)
-        ring_start(S_Y, y_g)
-        ring_start(S_DY, dy_g)
+        for h in range(2):
+            ring_start(S_Y + h, y_g.at[h])
+        for h in range(2):
+            ring_start(S_DY + h, dy_g.at[h])
         for i in range(6):
             w_copy(i).start()
+
+    def y_step(h):
+        with scope(f"y_step_{h}"):
+            ring_step(S_Y + h, y_g.at[h])
+
+    def y_last(h):
+        with scope(f"y_last_{h}"):
+            ring_last(S_Y + h, y_g.at[h])
+
+    def dy_step(h):
+        with scope(f"dy_step_{h}"):
+            ring_step(S_DY + h, dy_g.at[h])
+
+    def dy_last(h):
+        with scope(f"dy_last_{h}"):
+            ring_last(S_DY + h, dy_g.at[h])
+
+    def half_cols(h):
+        return slice(h * HW, (h + 1) * HW)
+
+    def y_rows(h):
+        with scope(f"y_finish_{h}"):
+            ag_finish(S_Y + h, y_g.at[h])
+        with scope(f"rows_y_{h}"):
+            gather_rows(lambda p: pair_of(y_g.at[h], p), xr, 0, half_cols(h), False)
+
+    def dy_rows(h):
+        with scope(f"dy_finish_{h}"):
+            ag_finish(S_DY + h, dy_g.at[h])
+        with scope(f"rows_dy_{h}"):
+            gather_rows(lambda p: pair_of(dy_g.at[h], p), zr, 0, half_cols(h), True)
+
+    def forward_part(h, experts):
+        with scope(f"forward_two_{h}"):
+            for e in experts:
+                forward_half(e, h)
 
     with scope("route"):
         ag_pass_on(S_ROUTE, route_g)
         ag_finish(S_ROUTE, route_g)
-    with scope("step_y"):
-        ring_step(S_Y, y_g)
+    y_step(0)
+    y_step(1)
     with scope("build_two"):
         build_routes(0)
-    with scope("step_dy"):
-        ring_step(S_DY, dy_g)
-    with scope("wait_y"):
-        ring_last(S_Y, y_g)
-        ag_finish(S_Y, y_g)
-    with scope("rows_y"):
-        gather_rows(lambda p: pair_of(y_g, p), xr, 0, slice(None), False)
-        w_copy(0).wait()
-        w_copy(1).wait()
-    with scope("forward_two"):
-        for e in range(2):
-            forward_expert(0, e)
-    with scope("last_dy"):
-        ring_last(S_DY, dy_g)
+    dy_step(0)
+    y_last(0)
+    dy_step(1)
+    y_last(1)
+    for i in range(3):
+        w_copy(i).wait()
+    y_rows(0)
+    forward_part(0, range(E))
+    dy_last(0)
+    y_rows(1)
+    forward_part(1, range(2))
+    dy_last(1)
+    with scope("x_start"):
         ag_start(S_X, x_g.at[me], x_g)
-    with scope("forward_two_b"):
-        for e in range(2, E):
-            forward_expert(0, e)
-    with scope("wait_dy"):
-        ag_finish(S_DY, dy_g)
-    with scope("rows_dy"):
-        gather_rows(lambda p: pair_of(dy_g, p), zr, 0, slice(None), True)
+    forward_part(1, range(2, E))
+    dy_rows(0)
+    dy_rows(1)
     with scope("hidden_two"):
-        w_copy(2).wait()
         for e in range(E):
             hidden_expert(0, e, nt_dot(zr[0][e], w_vm[2][e]))
+
     for k in range(CH):
         with scope(f"chunk_two_{k}"):
             row_chunk(0, k)
@@ -278,36 +327,45 @@
                 near_start(k - 1)
     with scope(f"near_{CH - 1}"):
         near_start(CH - 1)
-    with scope("last_0"):
-        last_start(0)
-
-    with scope("wait_x"):
-        ag_pass_on(S_X, x_g)
-    with scope("build_one"):
-        build_routes(1)
-    with scope("last_1"):
-        last_start(1)
-    with scope("rows_x"):
-        ag_finish(S_X, x_g)
-        gather_rows(lambda p: pair_of(x_g, p), xr, 1, slice(None), False)
-    with scope("last_2"):
-        last_start(2)
-    with scope("forward_one_0"):
-        for i in range(3, 6):
-            w_copy(i).wait()
-        forward_expert(1, 0)
-    with scope("last_3"):
-        last_start(3)
+    def last_step(k):
+        with scope(f"last_{k}"):
+            last_start(k)
+
+    def x_wait():
+        with scope("wait_x"):
+            ag_pass_on(S_X, x_g)
+
+    def x_build():
+        with scope("build_one"):
+            build_routes(1)
+
+    def x_rows():
+        with scope("rows_x"):
+            ag_finish(S_X, x_g)
+            gather_rows(lambda p: pair_of(x_g, p), xr, 1, slice(None), False)
+            for i in range(3, 6):
+                w_copy(i).wait()
+
+    def ring_one(k):
+        with scope(f"step_{k}"):
+            ring_step(S_D1 + k, d1_g.at[k])
+
+    def ring_two(k):
+        with scope(f"last_d1_{k}"):
+            ring_last(S_D1 + k, d1_g.at[k])
 
     def mid_grad(k):
         cols = slice(k * CW, (k + 1) * CW)
         near_copy(k, 1).wait_recv()
         last_copy(k).wait_recv()
         total = part[0, k, core, me // 2] + near_recv[k, 1] + last_recv[k]
-        mine = (dy_g[me, :, cols].astype(F32) + total).astype(BF16)
+        mine = (dy_g[k // 2, me, :, (k % 2) * CW : (k % 2 + 1) * CW].astype(F32) + total).astype(BF16)
         d1_ref[:, cols] = mine
         d1_g[k, me] = mine
-        ag_start(S_D1 + k, d1_g.at[k, me], d1_g.at[k])
+        if k < 2:
+            ring_start(S_D1 + k, d1_g.at[k])
+        else:
+            ag_start(S_D1 + k, d1_g.at[k, me], d1_g.at[k])
 
     def mid_rows(k):
         cols = slice(k * CW, (k + 1) * CW)
@@ -343,17 +401,27 @@
         with scope(f"forward_one_{k}"):
             forward_expert(1, k)
 
+    last_step(0)
+    x_wait()
+    x_build()
+    last_step(1)
+    x_rows()
+    last_step(2)
     mid_step(0)
+    forward_step(0)
+    last_step(3)
     mid_step(1)
     mid_step(2)
     forward_step(1)
+    ring_one(0)
     forward_step(2)
     forward_step(3)
     mid_step(3)
-    pass_step(0)
-    pass_step(1)
+    ring_one(1)
+    ring_two(0)
     pass_step(2)
     rows_step(0)
+    ring_two(1)
     pass_step(3)
     rows_step(1)
     rows_step(2)
@@ -371,7 +439,7 @@
     with scope("drain"):
         seven = pl.ds(0, DEVS - 1)
         sent = (
-            (S_ROUTE, route_g.at[seven]), (S_Y, y_g.at[seven]), (S_DY, dy_g.at[seven]), (S_X, x_g.at[seven]), (S_D1, d1_g.at[:, seven]),
+            (S_ROUTE, route_g.at[seven]), (S_Y, y_g.at[0, seven]), (S_Y + 1, y_g.at[1, seven]), (S_DY, dy_g.at[0, seven]), (S_DY + 1, dy_g.at[1, seven]), (S_X, x_g.at[seven]), (S_D1, d1_g.at[:, seven]),
             (S_D1 + 1, mate_recv), (S_D1 + 2, near_recv), (S_D1 + 3, last_recv),
         )
         for i, whole in sent:
@@ -399,8 +467,8 @@
             pltpu.VMEM((2, 8, TOK), F32),
             pltpu.VMEM((16, 2 * TOK), F32),
             pltpu.VMEM((DEVS, 16, 2 * TOK), F32),
-            pltpu.VMEM((DEVS, TOK, D), BF16),
-            pltpu.VMEM((DEVS, TOK, D), BF16),
+            pltpu.VMEM((2, DEVS, TOK, HW), BF16),
+            pltpu.VMEM((2, DEVS, TOK, HW), BF16),
             pltpu.VMEM((DEVS, TOK, D), BF16),
             pltpu.VMEM((CH, DEVS, TOK, CW), BF16),
             pltpu.VMEM((E, ROWS, F), F32),
@@ -415,7 +483,7 @@
             pltpu.VMEM((CH, 2, TOK, CW), F32),
             pltpu.VMEM((CH, TOK, CW), F32),
             dma((2,)),
-            dma((3,)),
+            dma((5,)),
             dma((6,)),
             dma((S_D1 + 4,)),
             dma((N_STREAMS, 4)),

time: 69 us -> 67.9 us (0.984)
  Pallas kernels: 64 us -> 62.8 us
    pallas_call x1, Pallas kernels: 47.5 us -> 46.4 us  [main_call(): pl.pallas_call(main_kernel, out_shape=(sums, pltpu.VMEM((TOK, D), BF16),...]
where the time goes in v7:
time: 67.9 us; the launch traced here: 67.8 us
  Pallas kernels  62.8 us (92%)
  starting transfers between devices  3.51 us (5%)
  other arithmetic  0.76 us (1%)
  between operations  0.68 us (1%)
    pallas_call x1, Pallas kernels, main_call(): pl.pallas_call(main_kernel, out_shape=(sums, pltpu.VMEM((TOK, D), BF16),...  46.4 us
    pallas_call x1, Pallas kernels, wgrad_call(): pl.pallas_call(wgrad_kernel, out_shape=(up, up, dn) * 2, in_specs=[pl.Blo...  16.5 us
    ppermute x3, starting transfers between devices, local_step(): lax.ppermute(got[2 + i], 'expert', [(d, d ^ flip) for d in range(DEVS)])  3.51 us
  transfers between devices with their start and end apart: 3, of which 0 were waited for; matrix products, arithmetic and copies ran while one was open for 0% of the time, Pallas kernels for 24%

profile of v7, /device:TPU:0, one launch (start us, length us, event | category | flops | bytes accessed | tf_op | source)
XLA Modules:
  0.0 67.8 jit_solution(8323426467500067111)
XLA Ops:
  0.6 46.4 %moe_backward.1 = (f32[64,1024]{1,0:T(8,128)S(1)}, bf16[64,1024]{1,0:T(8,128)(2,1)S(1)}, f32[64,1024]{1,0:T(8,128)S(1)}, f32[64,1024]{1,0:T(8,128)S(1)}, f32[64,...) custom-call(s32[8,64]{1,0:T(8,128)} %bitcast.6, ...), custom_call_target="tpu_custom_call" | custom-call | tf_op jit(solution)/shard_map/moe_backward/pallas_call | solution.py:459
  47.0 0.8 %collective-permute-start = (f32[64,1024]{1,0:T(8,128)S(1)}, f32[64,1024]{1,0:T(8,128)S(1)}, u32[]{:S(2)}, u32[]{:S(2)}) collective-permute-start(f32[64,1024]{1,0:T(8,128)S(1)} %get-tuple-element.30), channel_id=1, source_target_pairs={{0,2},{1,3},{2,0},{3,1},{4,6},{5,7},{6,4},{7,5}} | collective-permute-start | bytes 786440 | tf_op jit(solution)/shard_map/ppermute | solution.py:562
  47.8 1.1 %collective-permute-start.1 = (f32[64,1024]{1,0:T(8,128)S(1)}, f32[64,1024]{1,0:T(8,128)S(1)}, u32[]{:S(2)}, u32[]{:S(2)}) collective-permute-start(f32[64,1024]{1,0:T(8,128)S(1)} %get-tuple-element.31), channel_id=1, source_target_pairs={{0,4},{1,5},{2,6},{3,7},{4,0},{5,1},{6,2},{7,3}} | collective-permute-start | bytes 786440 | tf_op jit(solution)/shard_map/ppermute | solution.py:562
  49.0 1.6 %collective-permute-start.2 = (f32[64,1024]{1,0:T(8,128)S(1)}, f32[64,1024]{1,0:T(8,128)S(1)}, u32[]{:S(2)}, u32[]{:S(2)}) collective-permute-start(f32[64,1024]{1,0:T(8,128)S(1)} %get-tuple-element.32), channel_id=1, source_target_pairs={{0,6},{1,7},{2,4},{3,5},{4,2},{5,3},{6,0},{7,1}} | collective-permute-start | bytes 786440 | tf_op jit(solution)/shard_map/ppermute | solution.py:562
  50.5 16.5 %weight_grads.1 = (f32[4,1024,512]{2,1,0:T(8,128)}, f32[4,1024,512]{2,1,0:T(8,128)}, f32[4,512,1024]{2,1,0:T(8,128)}, f32[4,1024,512]{2,1,0:T(8,128)}, f32[4,1024,512]{2,1,0:T(8,128)}, /*index=5*/f32[4,512,1024]{2,1,0:T(8,128)}) custom-call(bf16[4,192,1024]{2,1,0:T(8,128)(2,1)S(1)} %get-tuple-element.33.refs_0_, ...), custom_call_target="tpu_custom_call" | custom-call | flops 4831838208 | bytes 50331648 | tf_op jit(solution)/shard_map/weight_grads/pallas_call | solution.py:536
  67.0 0.0 collective-permute-done
  67.0 0.0 collective-permute-done.1
  67.0 0.0 collective-permute-done.2
  67.0 0.8 %add_convert_fusion = bf16[64,1024]{1,0:T(8,128)(2,1)} fusion(f32[64,1024]{1,0:T(8,128)S(1)} %get-tuple-element.29, f32[64,1024]{1,0:T(8,128)S(1)} %collective-permute-done.2, f32[64,1024]{1,0:T(8,128)S(1)} %collective-permute-done, f32[64,1024]{1,0:T(8,128)S(1)} %collective-permute-done.1, bf16[64,1024]{1,0:T(8,128)(2,1)S(1)} %get-tuple-element.28), kind=kLoop, calls=%fused_computation | loop fusion | flops 393216 | bytes 1310720 | tf_op jit(solution)/shard_map/convert_element_type | solution.py:564
Async XLA Ops:
  47.0 20.0 %collective-permute-start = (f32[64,1024]{1,0:T(8,128)S(1)}, f32[64,1024]{1,0:T(8,128)S(1)}, u32[]{:S(2)}, u32[]{:S(2)}) collective-permute-start(f32[64,1024]{1,0:T(8,128)S(1)} %get-tuple-element.30), channel_id=1, source_target_pairs={{0,2},{1,3},{2,0},{3,1},{4,6},{5,7},{6,4},{7,5}} | collective-permute-start | bytes 786440 | tf_op jit(solution)/shard_map/ppermute | solution.py:562
  47.8 19.2 %collective-permute-start.1 = (f32[64,1024]{1,0:T(8,128)S(1)}, f32[64,1024]{1,0:T(8,128)S(1)}, u32[]{:S(2)}, u32[]{:S(2)}) collective-permute-start(f32[64,1024]{1,0:T(8,128)S(1)} %get-tuple-element.31), channel_id=1, source_target_pairs={{0,4},{1,5},{2,6},{3,7},{4,0},{5,1},{6,2},{7,3}} | collective-permute-start | bytes 786440 | tf_op jit(solution)/shard_map/ppermute | solution.py:562
  49.0 18.1 %collective-permute-start.2 = (f32[64,1024]{1,0:T(8,128)S(1)}, f32[64,1024]{1,0:T(8,128)S(1)}, u32[]{:S(2)}, u32[]{:S(2)}) collective-permute-start(f32[64,1024]{1,0:T(8,128)S(1)} %get-tuple-element.32), channel_id=1, source_target_pairs={{0,6},{1,7},{2,4},{3,5},{4,2},{5,3},{6,0},{7,1}} | collective-permute-start | bytes 786440 | tf_op jit(solution)/shard_map/ppermute | solution.py:562

commit v8 on v7

--- a/solution.py
+++ b/solution.py
@@ -23,7 +23,7 @@
 PROWS = E * PAIR
 CH = 4
 CW = D // CH
-MAIN_VMEM = 48_000_000
+MAIN_VMEM = 51_000_000
 WGRAD_VMEM = 40_000_000
 
 S_ROUTE, S_Y, S_DY, S_X, S_D1 = 0, 1, 3, 5, 6
@@ -51,7 +51,7 @@
     x_hbm, y_hbm, dy_hbm, w1b_hbm, w3b_hbm, w2b_hbm, w1a_hbm, w3a_hbm, w2a_hbm,
     own_ref, d1_ref, far0_ref, far1_ref, far2_ref,
     xr_two, zr_two, hid_two, da_two, db_two, xr_one, zr_one, hid_one, da_one, db_one,
-    w_vm, choice_i, choice_f, route_own, route_g, y_g, dy_g, x_g, d1_g,
+    w_vm, w3_turned, choice_i, choice_f, route_own, route_g, y_g, dy_g, x_g, d1_g,
     act_s, act_f, dh_sum, dxp, perm, perm_t, gate,
     part, mate_recv, near_recv, last_recv,
     choice_sem, tile_sem, w_sem, send_sem, ag_recv, mate_sem, near_sem, last_sem,
@@ -202,11 +202,26 @@
         da[layer][e] = (dh * act_f[e]).astype(BF16)
         db[layer][e] = (dh * act_s[e]).astype(BF16)
 
+    w2_turned, w1_turned = w_vm[3], w_vm[2]
+
+    def turn_two(experts):
+        with scope("turn_two"):
+            for e in experts:
+                w2_turned[e] = w_vm[2][e].T
+
+    def turn_one(tasks):
+        with scope("turn_one"):
+            for e, src, dst in tasks:
+                dst[e] = src[e].T
+
     def row_chunk(layer, k):
         w1, w3 = w_vm[3 * layer], w_vm[3 * layer + 1]
         cols = slice(k * CW, (k + 1) * CW)
         for e in range(E):
-            g = nt_dot(da[layer][e], w1[e, cols, :]) + nt_dot(db[layer][e], w3[e, cols, :])
+            if layer == 0:
+                g = nt_dot(da[0][e], w1[e, cols, :]) + nt_dot(db[0][e], w3[e, cols, :])
+            else:
+                g = nn_dot(da[1][e], w1_turned[e, :, cols]) + nn_dot(db[1][e], w3_turned[e, :, cols])
             g = g.astype(BF16)
             for p in range(CHIPS):
                 dxp[k % 2, p, e] = g[p * PAIR : (p + 1) * PAIR]
@@ -252,7 +267,7 @@
             ring_start(S_Y + h, y_g.at[h])
         for h in range(2):
             ring_start(S_DY + h, dy_g.at[h])
-        for i in range(6):
+        for i in (2, 0, 1, 4, 5):
             w_copy(i).start()
 
     def y_step(h):
@@ -298,11 +313,15 @@
     y_step(1)
     with scope("build_two"):
         build_routes(0)
+    w_copy(2).wait()
+    turn_two((0,))
     dy_step(0)
+    turn_two((1, 2))
     y_last(0)
+    turn_two((3,))
     dy_step(1)
     y_last(1)
-    for i in range(3):
+    for i in range(2):
         w_copy(i).wait()
     y_rows(0)
     forward_part(0, range(E))
@@ -317,16 +336,23 @@
     dy_rows(1)
     with scope("hidden_two"):
         for e in range(E):
-            hidden_expert(0, e, nt_dot(zr[0][e], w_vm[2][e]))
-
+            hidden_expert(0, e, nn_dot(zr[0][e], w2_turned[e]))
+        w_copy(3).start()
+
+    turns = [(e, w_vm[4], w3_turned) for e in range(E)] + [(e, w_vm[3], w1_turned) for e in range(E)]
     for k in range(CH):
         with scope(f"chunk_two_{k}"):
             row_chunk(0, k)
+        if k == 3:
+            w_copy(4).wait()
+            turn_one(turns[0:1])
         if k >= 1:
             with scope(f"near_{k - 1}"):
                 near_start(k - 1)
+    turn_one(turns[1:3])
     with scope(f"near_{CH - 1}"):
         near_start(CH - 1)
+
     def last_step(k):
         with scope(f"last_{k}"):
             last_start(k)
@@ -343,8 +369,7 @@
         with scope("rows_x"):
             ag_finish(S_X, x_g)
             gather_rows(lambda p: pair_of(x_g, p), xr, 1, slice(None), False)
-            for i in range(3, 6):
-                w_copy(i).wait()
+            w_copy(5).wait()
 
     def ring_one(k):
         with scope(f"step_{k}"):
@@ -362,7 +387,7 @@
         mine = (dy_g[k // 2, me, :, (k % 2) * CW : (k % 2 + 1) * CW].astype(F32) + total).astype(BF16)
         d1_ref[:, cols] = mine
         d1_g[k, me] = mine
-        if k < 2:
+        if k < 1:
             ring_start(S_D1 + k, d1_g.at[k])
         else:
             ag_start(S_D1 + k, d1_g.at[k, me], d1_g.at[k])
@@ -371,13 +396,16 @@
         cols = slice(k * CW, (k + 1) * CW)
         gather_rows(lambda p: pair_of(d1_g.at[k], p), zr, 1, cols, True)
 
+    parts_done = []
+
     def hidden_part(k):
         cols = slice(k * CW, (k + 1) * CW)
+        parts_done.append(k)
         for e in range(E):
             dh = nt_dot(zr[1][e, :, cols], w_vm[5][e, :, cols])
-            if k > 0:
+            if len(parts_done) > 1:
                 dh = dh_sum[e] + dh
-            if k < CH - 1:
+            if len(parts_done) < CH:
                 dh_sum[e] = dh
             else:
                 hidden_expert(1, e, dh)
@@ -404,11 +432,17 @@
     last_step(0)
     x_wait()
     x_build()
+    turn_one(turns[3:4])
+    w_copy(3).wait()
     last_step(1)
+    turn_one(turns[4:5])
     x_rows()
+    turn_one(turns[5:6])
     last_step(2)
+    turn_one(turns[6:7])
     mid_step(0)
     forward_step(0)
+    turn_one(turns[7:8])
     last_step(3)
     mid_step(1)
     mid_step(2)
@@ -417,13 +451,12 @@
     forward_step(2)
     forward_step(3)
     mid_step(3)
-    ring_one(1)
+    pass_step(1)
+    pass_step(2)
     ring_two(0)
-    pass_step(2)
+    rows_step(1)
     rows_step(0)
-    ring_two(1)
     pass_step(3)
-    rows_step(1)
     rows_step(2)
     rows_step(3)
     for k in range(CH):
@@ -463,6 +496,7 @@
         out_specs=(vm,) * 15,
         scratch_shapes=[
             (w_up, w_up, w_dn, w_up, w_up, w_dn),
+            w_dn,
             pltpu.VMEM((4, 8, TOK), jnp.int32),
             pltpu.VMEM((2, 8, TOK), F32),
             pltpu.VMEM((16, 2 * TOK), F32),

time: 67.9 us -> 65.8 us (0.969)
  Pallas kernels: 62.8 us -> 60.7 us
    pallas_call x1, Pallas kernels: 46.4 us -> 44.3 us  [main_call(): pl.pallas_call(main_kernel, out_shape=(sums, pltpu.VMEM((TOK, D), BF16),...]
  transfers between devices with their start and end apart: 3 -> 3, of which waited for: 0 -> 0; matrix products, arithmetic and copies ran while one was open for 0% -> 0% of each run, Pallas kernels for 24% -> 25%
where the time goes in v8:
time: 65.8 us; the launch traced here: 65.7 us
  Pallas kernels  60.7 us (92%)
  starting transfers between devices  3.51 us (5%)
  other arithmetic  0.74 us (1%)
  between operations  0.68 us (1%)
    pallas_call x1, Pallas kernels, main_call(): pl.pallas_call(main_kernel, out_shape=(sums, pltpu.VMEM((TOK, D), BF16),...  44.3 us
    pallas_call x1, Pallas kernels, wgrad_call(): pl.pallas_call(wgrad_kernel, out_shape=(up, up, dn) * 2, in_specs=[pl.Blo...  16.5 us
    ppermute x3, starting transfers between devices, local_step(): lax.ppermute(got[2 + i], 'expert', [(d, d ^ flip) for d in range(DEVS)])  3.51 us
  transfers between devices with their start and end apart: 3, of which 0 were waited for; matrix products, arithmetic and copies ran while one was open for 0% of the time, Pallas kernels for 25%

profile of v8, /device:TPU:0, one launch (start us, length us, event | category | flops | bytes accessed | tf_op | source)
XLA Modules:
  0.0 65.7 jit_solution(11182099010936118734)
XLA Ops:
  0.6 44.3 %moe_backward.1 = (f32[64,1024]{1,0:T(8,128)S(1)}, bf16[64,1024]{1,0:T(8,128)(2,1)S(1)}, f32[64,1024]{1,0:T(8,128)S(1)}, f32[64,1024]{1,0:T(8,128)S(1)}, f32[64,...) custom-call(s32[8,64]{1,0:T(8,128)} %bitcast.6, ...), custom_call_target="tpu_custom_call" | custom-call | tf_op jit(solution)/shard_map/moe_backward/pallas_call | solution.py:492
  44.9 1.2 %collective-permute-start = (f32[64,1024]{1,0:T(8,128)S(1)}, f32[64,1024]{1,0:T(8,128)S(1)}, u32[]{:S(2)}, u32[]{:S(2)}) collective-permute-start(f32[64,1024]{1,0:T(8,128)S(1)} %get-tuple-element.30), channel_id=1, source_target_pairs={{0,2},{1,3},{2,0},{3,1},{4,6},{5,7},{6,4},{7,5}} | collective-permute-start | bytes 786440 | tf_op jit(solution)/shard_map/ppermute | solution.py:596
  46.1 0.8 %collective-permute-start.1 = (f32[64,1024]{1,0:T(8,128)S(1)}, f32[64,1024]{1,0:T(8,128)S(1)}, u32[]{:S(2)}, u32[]{:S(2)}) collective-permute-start(f32[64,1024]{1,0:T(8,128)S(1)} %get-tuple-element.31), channel_id=1, source_target_pairs={{0,4},{1,5},{2,6},{3,7},{4,0},{5,1},{6,2},{7,3}} | collective-permute-start | bytes 786440 | tf_op jit(solution)/shard_map/ppermute | solution.py:596
  46.9 1.5 %collective-permute-start.2 = (f32[64,1024]{1,0:T(8,128)S(1)}, f32[64,1024]{1,0:T(8,128)S(1)}, u32[]{:S(2)}, u32[]{:S(2)}) collective-permute-start(f32[64,1024]{1,0:T(8,128)S(1)} %get-tuple-element.32), channel_id=1, source_target_pairs={{0,6},{1,7},{2,4},{3,5},{4,2},{5,3},{6,0},{7,1}} | collective-permute-start | bytes 786440 | tf_op jit(solution)/shard_map/ppermute | solution.py:596
  48.4 16.5 %weight_grads.1 = (f32[4,1024,512]{2,1,0:T(8,128)}, f32[4,1024,512]{2,1,0:T(8,128)}, f32[4,512,1024]{2,1,0:T(8,128)}, f32[4,1024,512]{2,1,0:T(8,128)}, f32[4,1024,512]{2,1,0:T(8,128)}, /*index=5*/f32[4,512,1024]{2,1,0:T(8,128)}) custom-call(bf16[4,192,1024]{2,1,0:T(8,128)(2,1)S(1)} %get-tuple-element.33.refs_0_, ...), custom_call_target="tpu_custom_call" | custom-call | flops 4831838208 | bytes 50331648 | tf_op jit(solution)/shard_map/weight_grads/pallas_call | solution.py:570
  64.9 0.0 collective-permute-done
  64.9 0.0 collective-permute-done.1
  64.9 0.0 collective-permute-done.2
  64.9 0.7 %add_convert_fusion = bf16[64,1024]{1,0:T(8,128)(2,1)} fusion(f32[64,1024]{1,0:T(8,128)S(1)} %get-tuple-element.29, f32[64,1024]{1,0:T(8,128)S(1)} %collective-permute-done.2, f32[64,1024]{1,0:T(8,128)S(1)} %collective-permute-done, f32[64,1024]{1,0:T(8,128)S(1)} %collective-permute-done.1, bf16[64,1024]{1,0:T(8,128)(2,1)S(1)} %get-tuple-element.28), kind=kLoop, calls=%fused_computation | loop fusion | flops 393216 | bytes 1310720 | tf_op jit(solution)/shard_map/convert_element_type | solution.py:598
Async XLA Ops:
  44.9 20.0 %collective-permute-start = (f32[64,1024]{1,0:T(8,128)S(1)}, f32[64,1024]{1,0:T(8,128)S(1)}, u32[]{:S(2)}, u32[]{:S(2)}) collective-permute-start(f32[64,1024]{1,0:T(8,128)S(1)} %get-tuple-element.30), channel_id=1, source_target_pairs={{0,2},{1,3},{2,0},{3,1},{4,6},{5,7},{6,4},{7,5}} | collective-permute-start | bytes 786440 | tf_op jit(solution)/shard_map/ppermute | solution.py:596
  46.1 18.8 %collective-permute-start.1 = (f32[64,1024]{1,0:T(8,128)S(1)}, f32[64,1024]{1,0:T(8,128)S(1)}, u32[]{:S(2)}, u32[]{:S(2)}) collective-permute-start(f32[64,1024]{1,0:T(8,128)S(1)} %get-tuple-element.31), channel_id=1, source_target_pairs={{0,4},{1,5},{2,6},{3,7},{4,0},{5,1},{6,2},{7,3}} | collective-permute-start | bytes 786440 | tf_op jit(solution)/shard_map/ppermute | solution.py:596
  46.9 18.0 %collective-permute-start.2 = (f32[64,1024]{1,0:T(8,128)S(1)}, f32[64,1024]{1,0:T(8,128)S(1)}, u32[]{:S(2)}, u32[]{:S(2)}) collective-permute-start(f32[64,1024]{1,0:T(8,128)S(1)} %get-tuple-element.32), channel_id=1, source_target_pairs={{0,6},{1,7},{2,4},{3,5},{4,2},{5,3},{6,0},{7,1}} | collective-permute-start | bytes 786440 | tf_op jit(solution)/shard_map/ppermute | solution.py:596

commit v9 on v8

--- a/solution.py
+++ b/solution.py
@@ -326,11 +326,11 @@
     y_rows(0)
     forward_part(0, range(E))
     dy_last(0)
+    with scope("x_start"):
+        ag_start(S_X, x_g.at[me], x_g)
     y_rows(1)
     forward_part(1, range(2))
     dy_last(1)
-    with scope("x_start"):
-        ag_start(S_X, x_g.at[me], x_g)
     forward_part(1, range(2, E))
     dy_rows(0)
     dy_rows(1)
@@ -449,15 +449,15 @@
     forward_step(1)
     ring_one(0)
     forward_step(2)
+    mid_step(3)
     forward_step(3)
-    mid_step(3)
     pass_step(1)
     pass_step(2)
     ring_two(0)
     rows_step(1)
-    rows_step(0)
     pass_step(3)
     rows_step(2)
+    rows_step(0)
     rows_step(3)
     for k in range(CH):
         with scope(f"chunk_one_{k}"):

time: 65.8 us -> 65.3 us (level)
  no operation moved by 1% of the time
where the time goes in v9:
time: 65.3 us; the launch traced here: 65.2 us
  Pallas kernels  60.2 us (92%)
  starting transfers between devices  3.51 us (5%)
  other arithmetic  0.74 us (1%)
  between operations  0.68 us (1%)
    pallas_call x1, Pallas kernels, main_call(): pl.pallas_call(main_kernel, out_shape=(sums, pltpu.VMEM((TOK, D), BF16),...  43.8 us
    pallas_call x1, Pallas kernels, wgrad_call(): pl.pallas_call(wgrad_kernel, out_shape=(up, up, dn) * 2, in_specs=[pl.Blo...  16.5 us
    ppermute x3, starting transfers between devices, local_step(): lax.ppermute(got[2 + i], 'expert', [(d, d ^ flip) for d in range(DEVS)])  3.51 us
  transfers between devices with their start and end apart: 3, of which 0 were waited for; matrix products, arithmetic and copies ran while one was open for 0% of the time, Pallas kernels for 25%

profile of v9, /device:TPU:0, one launch (start us, length us, event | category | flops | bytes accessed | tf_op | source)
XLA Modules:
  0.0 65.2 jit_solution(2289052524851669964)
XLA Ops:
  0.6 43.8 %moe_backward.1 = (f32[64,1024]{1,0:T(8,128)S(1)}, bf16[64,1024]{1,0:T(8,128)(2,1)S(1)}, f32[64,1024]{1,0:T(8,128)S(1)}, f32[64,1024]{1,0:T(8,128)S(1)}, f32[64,...) custom-call(s32[8,64]{1,0:T(8,128)} %bitcast.6, ...), custom_call_target="tpu_custom_call" | custom-call | tf_op jit(solution)/shard_map/moe_backward/pallas_call | solution.py:492
  44.4 0.8 %collective-permute-start = (f32[64,1024]{1,0:T(8,128)S(1)}, f32[64,1024]{1,0:T(8,128)S(1)}, u32[]{:S(2)}, u32[]{:S(2)}) collective-permute-start(f32[64,1024]{1,0:T(8,128)S(1)} %get-tuple-element.30), channel_id=1, source_target_pairs={{0,2},{1,3},{2,0},{3,1},{4,6},{5,7},{6,4},{7,5}} | collective-permute-start | bytes 786440 | tf_op jit(solution)/shard_map/ppermute | solution.py:596
  45.2 1.2 %collective-permute-start.1 = (f32[64,1024]{1,0:T(8,128)S(1)}, f32[64,1024]{1,0:T(8,128)S(1)}, u32[]{:S(2)}, u32[]{:S(2)}) collective-permute-start(f32[64,1024]{1,0:T(8,128)S(1)} %get-tuple-element.31), channel_id=1, source_target_pairs={{0,4},{1,5},{2,6},{3,7},{4,0},{5,1},{6,2},{7,3}} | collective-permute-start | bytes 786440 | tf_op jit(solution)/shard_map/ppermute | solution.py:596
  46.3 1.6 %collective-permute-start.2 = (f32[64,1024]{1,0:T(8,128)S(1)}, f32[64,1024]{1,0:T(8,128)S(1)}, u32[]{:S(2)}, u32[]{:S(2)}) collective-permute-start(f32[64,1024]{1,0:T(8,128)S(1)} %get-tuple-element.32), channel_id=1, source_target_pairs={{0,6},{1,7},{2,4},{3,5},{4,2},{5,3},{6,0},{7,1}} | collective-permute-start | bytes 786440 | tf_op jit(solution)/shard_map/ppermute | solution.py:596
  47.9 16.5 %weight_grads.1 = (f32[4,1024,512]{2,1,0:T(8,128)}, f32[4,1024,512]{2,1,0:T(8,128)}, f32[4,512,1024]{2,1,0:T(8,128)}, f32[4,1024,512]{2,1,0:T(8,128)}, f32[4,1024,512]{2,1,0:T(8,128)}, /*index=5*/f32[4,512,1024]{2,1,0:T(8,128)}) custom-call(bf16[4,192,1024]{2,1,0:T(8,128)(2,1)S(1)} %get-tuple-element.33.refs_0_, ...), custom_call_target="tpu_custom_call" | custom-call | flops 4831838208 | bytes 50331648 | tf_op jit(solution)/shard_map/weight_grads/pallas_call | solution.py:570
  64.4 0.0 collective-permute-done
  64.4 0.0 collective-permute-done.1
  64.4 0.0 collective-permute-done.2
  64.4 0.7 %add_convert_fusion = bf16[64,1024]{1,0:T(8,128)(2,1)} fusion(f32[64,1024]{1,0:T(8,128)S(1)} %get-tuple-element.29, f32[64,1024]{1,0:T(8,128)S(1)} %collective-permute-done.2, f32[64,1024]{1,0:T(8,128)S(1)} %collective-permute-done, f32[64,1024]{1,0:T(8,128)S(1)} %collective-permute-done.1, bf16[64,1024]{1,0:T(8,128)(2,1)S(1)} %get-tuple-element.28), kind=kLoop, calls=%fused_computation | loop fusion | flops 393216 | bytes 1310720 | tf_op jit(solution)/shard_map/convert_element_type | solution.py:598
Async XLA Ops:
  44.4 20.0 %collective-permute-start = (f32[64,1024]{1,0:T(8,128)S(1)}, f32[64,1024]{1,0:T(8,128)S(1)}, u32[]{:S(2)}, u32[]{:S(2)}) collective-permute-start(f32[64,1024]{1,0:T(8,128)S(1)} %get-tuple-element.30), channel_id=1, source_target_pairs={{0,2},{1,3},{2,0},{3,1},{4,6},{5,7},{6,4},{7,5}} | collective-permute-start | bytes 786440 | tf_op jit(solution)/shard_map/ppermute | solution.py:596
  45.2 19.2 %collective-permute-start.1 = (f32[64,1024]{1,0:T(8,128)S(1)}, f32[64,1024]{1,0:T(8,128)S(1)}, u32[]{:S(2)}, u32[]{:S(2)}) collective-permute-start(f32[64,1024]{1,0:T(8,128)S(1)} %get-tuple-element.31), channel_id=1, source_target_pairs={{0,4},{1,5},{2,6},{3,7},{4,0},{5,1},{6,2},{7,3}} | collective-permute-start | bytes 786440 | tf_op jit(solution)/shard_map/ppermute | solution.py:596
  46.3 18.1 %collective-permute-start.2 = (f32[64,1024]{1,0:T(8,128)S(1)}, f32[64,1024]{1,0:T(8,128)S(1)}, u32[]{:S(2)}, u32[]{:S(2)}) collective-permute-start(f32[64,1024]{1,0:T(8,128)S(1)} %get-tuple-element.32), channel_id=1, source_target_pairs={{0,6},{1,7},{2,4},{3,5},{4,2},{5,3},{6,0},{7,1}} | collective-permute-start | bytes 786440 | tf_op jit(solution)/shard_map/ppermute | solution.py:596

commit v10 on v9

--- a/solution.py
+++ b/solution.py
@@ -538,6 +538,12 @@
         rows = pl.ds(h * n, n)
         return pltpu.make_async_copy(bufs[m].at[slot, rows], outs[layer][m].at[e, rows], out_sem.at[slot, m, h])
 
+    quarter = F // 4
+    for q in range(4):
+        rows = slice(q * quarter, (q + 1) * quarter)
+        bufs[2][0, rows] = tn_dot(saved[0][2][0, :, rows], saved[0][1][0])
+        pltpu.make_async_copy(bufs[2].at[0, pl.ds(q * quarter, quarter)], outs[0][2].at[0, pl.ds(q * quarter, quarter)], out_sem.at[0, 2, 0]).start()
+
     for layer in range(2):
         xr, zr, hid, da, db = saved[layer]
 
@@ -554,8 +560,14 @@
                     def _():
                         out_copy(layer, m, e, slot, h).wait()
 
-                    bufs[m][slot, rows] = tn_dot(lhs[e, :, rows], rhs[e])
-                    out_copy(layer, m, e, slot, h).start()
+                    def make():
+                        bufs[m][slot, rows] = tn_dot(lhs[e, :, rows], rhs[e])
+                        out_copy(layer, m, e, slot, h).start()
+
+                    if (layer, m) == (0, 2):
+                        pl.when(e > 0)(make)
+                    else:
+                        make()
 
     for i in range(2 * E - SETS, 2 * E):
         for m in (2, 0, 1):

time: 65.3 us -> 65.1 us (level)
  no operation moved by 1% of the time
where the time goes in v10:
time: 65.1 us; the launch traced here: 64.9 us
  Pallas kernels  60 us (92%)
  starting transfers between devices  3.51 us (5%)
  other arithmetic  0.74 us (1%)
  between operations  0.68 us (1%)
    pallas_call x1, Pallas kernels, main_call(): pl.pallas_call(main_kernel, out_shape=(sums, pltpu.VMEM((TOK, D), BF16),...  43.8 us
    pallas_call x1, Pallas kernels, wgrad_call(): pl.pallas_call(wgrad_kernel, out_shape=(up, up, dn) * 2, in_specs=[pl.Blo...  16.3 us
    ppermute x3, starting transfers between devices, local_step(): lax.ppermute(got[2 + i], 'expert', [(d, d ^ flip) for d in range(DEVS)])  3.51 us
  transfers between devices with their start and end apart: 3, of which 0 were waited for; matrix products, arithmetic and copies ran while one was open for 0% of the time, Pallas kernels for 25%

profile of v10, /device:TPU:0, one launch (start us, length us, event | category | flops | bytes accessed | tf_op | source)
XLA Modules:
  0.0 64.9 jit_solution(3616116919392962533)
XLA Ops:
  0.6 43.8 %moe_backward.1 = (f32[64,1024]{1,0:T(8,128)S(1)}, bf16[64,1024]{1,0:T(8,128)(2,1)S(1)}, f32[64,1024]{1,0:T(8,128)S(1)}, f32[64,1024]{1,0:T(8,128)S(1)}, f32[64,...) custom-call(s32[8,64]{1,0:T(8,128)} %bitcast.6, ...), custom_call_target="tpu_custom_call" | custom-call | tf_op jit(solution)/shard_map/moe_backward/pallas_call | solution.py:492
  44.4 0.8 %collective-permute-start = (f32[64,1024]{1,0:T(8,128)S(1)}, f32[64,1024]{1,0:T(8,128)S(1)}, u32[]{:S(2)}, u32[]{:S(2)}) collective-permute-start(f32[64,1024]{1,0:T(8,128)S(1)} %get-tuple-element.30), channel_id=1, source_target_pairs={{0,2},{1,3},{2,0},{3,1},{4,6},{5,7},{6,4},{7,5}} | collective-permute-start | bytes 786440 | tf_op jit(solution)/shard_map/ppermute | solution.py:608
  45.2 1.2 %collective-permute-start.1 = (f32[64,1024]{1,0:T(8,128)S(1)}, f32[64,1024]{1,0:T(8,128)S(1)}, u32[]{:S(2)}, u32[]{:S(2)}) collective-permute-start(f32[64,1024]{1,0:T(8,128)S(1)} %get-tuple-element.31), channel_id=1, source_target_pairs={{0,4},{1,5},{2,6},{3,7},{4,0},{5,1},{6,2},{7,3}} | collective-permute-start | bytes 786440 | tf_op jit(solution)/shard_map/ppermute | solution.py:608
  46.3 1.6 %collective-permute-start.2 = (f32[64,1024]{1,0:T(8,128)S(1)}, f32[64,1024]{1,0:T(8,128)S(1)}, u32[]{:S(2)}, u32[]{:S(2)}) collective-permute-start(f32[64,1024]{1,0:T(8,128)S(1)} %get-tuple-element.32), channel_id=1, source_target_pairs={{0,6},{1,7},{2,4},{3,5},{4,2},{5,3},{6,0},{7,1}} | collective-permute-start | bytes 786440 | tf_op jit(solution)/shard_map/ppermute | solution.py:608
  47.9 16.3 %weight_grads.1 = (f32[4,1024,512]{2,1,0:T(8,128)}, f32[4,1024,512]{2,1,0:T(8,128)}, f32[4,512,1024]{2,1,0:T(8,128)}, f32[4,1024,512]{2,1,0:T(8,128)}, f32[4,1024,512]{2,1,0:T(8,128)}, /*index=5*/f32[4,512,1024]{2,1,0:T(8,128)}) custom-call(bf16[4,192,1024]{2,1,0:T(8,128)(2,1)S(1)} %get-tuple-element.33.refs_0_, ...), custom_call_target="tpu_custom_call" | custom-call | flops 4831838208 | bytes 50331648 | tf_op jit(solution)/shard_map/weight_grads/pallas_call | solution.py:582
  64.2 0.0 collective-permute-done
  64.2 0.0 collective-permute-done.1
  64.2 0.0 collective-permute-done.2
  64.2 0.7 %add_convert_fusion = bf16[64,1024]{1,0:T(8,128)(2,1)} fusion(f32[64,1024]{1,0:T(8,128)S(1)} %get-tuple-element.29, f32[64,1024]{1,0:T(8,128)S(1)} %collective-permute-done.2, f32[64,1024]{1,0:T(8,128)S(1)} %collective-permute-done, f32[64,1024]{1,0:T(8,128)S(1)} %collective-permute-done.1, bf16[64,1024]{1,0:T(8,128)(2,1)S(1)} %get-tuple-element.28), kind=kLoop, calls=%fused_computation | loop fusion | flops 393216 | bytes 1310720 | tf_op jit(solution)/shard_map/convert_element_type | solution.py:610
Async XLA Ops:
  44.4 19.8 %collective-permute-start = (f32[64,1024]{1,0:T(8,128)S(1)}, f32[64,1024]{1,0:T(8,128)S(1)}, u32[]{:S(2)}, u32[]{:S(2)}) collective-permute-start(f32[64,1024]{1,0:T(8,128)S(1)} %get-tuple-element.30), channel_id=1, source_target_pairs={{0,2},{1,3},{2,0},{3,1},{4,6},{5,7},{6,4},{7,5}} | collective-permute-start | bytes 786440 | tf_op jit(solution)/shard_map/ppermute | solution.py:608
  45.2 19.0 %collective-permute-start.1 = (f32[64,1024]{1,0:T(8,128)S(1)}, f32[64,1024]{1,0:T(8,128)S(1)}, u32[]{:S(2)}, u32[]{:S(2)}) collective-permute-start(f32[64,1024]{1,0:T(8,128)S(1)} %get-tuple-element.31), channel_id=1, source_target_pairs={{0,4},{1,5},{2,6},{3,7},{4,0},{5,1},{6,2},{7,3}} | collective-permute-start | bytes 786440 | tf_op jit(solution)/shard_map/ppermute | solution.py:608
  46.3 17.8 %collective-permute-start.2 = (f32[64,1024]{1,0:T(8,128)S(1)}, f32[64,1024]{1,0:T(8,128)S(1)}, u32[]{:S(2)}, u32[]{:S(2)}) collective-permute-start(f32[64,1024]{1,0:T(8,128)S(1)} %get-tuple-element.32), channel_id=1, source_target_pairs={{0,6},{1,7},{2,4},{3,5},{4,2},{5,3},{6,0},{7,1}} | collective-permute-start | bytes 786440 | tf_op jit(solution)/shard_map/ppermute | solution.py:608
